TPU v7x, 32 devices: a whole 2x2x4 slice. The times are simulated.
32 devices in a mesh: row: 4 (over y, x), col: 8 (over z, core).
Axes of the slice: x: 2, y: 2, z: 4, core: 2. Of those that a mesh axis runs over, the one named last changes fastest.
Arguments:
- activations: float32 [2048, 4096], P('row', 'col')
- plan: int32 [3, 8], P(None, 'col'), may hold values 0 or 1
Outputs:
- rotated: float32 [2048, 4096], P('row', 'col')
- vectors: float32 [4096, 4096], P('row', 'col')
- spread: float32 [4096], P('col')
All inputs are finite; a program needn't handle non-finite values. No bound on the sum of `plan` on one device may be relied on, other than what follows from the above.
Results may differ from a plain program's by a relative error of at most 0.0001.
Values sent between devices are 32-bit elements; how exact they have to be, the bound alone decides.
No kernel may reach another device: no remote copies, remote signals or barrier semaphores. Data moves between devices by JAX's collectives and lax.ppermute only.
A program may use at most 64 MiB of HBM per device.

v0:
```python
import jax
import jax.numpy as jnp
from jax import lax
from jax.sharding import PartitionSpec as P

ROUNDS = 3
POLAR_STEPS = 3


HIGH = lax.Precision.HIGHEST


def from_behind(block, axis, distance):
    devices = range(lax.axis_size(axis))
    route = [((i - distance) % len(devices), i) for i in devices]
    return lax.ppermute(block, axis, route)


def local_gram(left_block, right_block):
    return lax.dot_general(left_block, right_block, (((0,), (0,)), ((), ())), precision=HIGH)


def rotation(pair_gram):
    half_width = pair_gram.shape[0] // 2
    diagonal = jnp.diagonal(pair_gram) + 1e-06
    root_diag = jnp.sqrt(diagonal)
    coupling = pair_gram[:half_width, half_width:] / (
        root_diag[:half_width, None] * root_diag[None, half_width:]
    )
    strength = jnp.sqrt(jnp.sum(coupling * coupling))
    scaled = coupling / (1.0 + strength)
    zeros_block = jnp.zeros((half_width, half_width), jnp.float32)
    generator = jnp.concatenate(
        [
            jnp.concatenate([zeros_block, scaled], axis=1),
            jnp.concatenate([-scaled.T, zeros_block], axis=1),
        ],
        axis=0,
    )
    iterate = jnp.eye(2 * half_width, dtype=jnp.float32) + generator
    for polar_index in range(POLAR_STEPS):
        product = jnp.dot(iterate, iterate.T, precision=HIGH)
        iterate = 1.5 * iterate - 0.5 * jnp.dot(product, iterate, precision=HIGH)
    return iterate


def split_panels(turned, chosen, half_width):
    first_panel = turned[:, :half_width]
    second_panel = turned[:, half_width:]
    moving = jnp.where(chosen, second_panel, first_panel)
    staying = jnp.where(chosen, first_panel, second_panel)
    return (moving, staying)


def per_device(activations, plan):
    matrix = activations
    width = matrix.shape[1]
    half_width = width // 2
    vector_rows = width * lax.axis_size("col") // lax.axis_size("row")
    row_ids = lax.axis_index("row") * vector_rows + jnp.arange(vector_rows, dtype=jnp.int32)
    col_ids = lax.axis_index("col") * width + jnp.arange(width, dtype=jnp.int32)
    vectors = (row_ids[:, None] == col_ids[None, :]).astype(jnp.float32)
    pair_gram = lax.psum(local_gram(matrix, matrix), "row")
    for round_index in range(ROUNDS):
        chosen = plan[round_index, 0] == 1
        turn = rotation(pair_gram)
        turned = jnp.dot(matrix, turn, precision=HIGH)
        turned_vec = jnp.dot(vectors, turn, precision=HIGH)
        new_gram = jnp.dot(turn.T, jnp.dot(pair_gram, turn, precision=HIGH), precision=HIGH)
        gram_first = new_gram[:half_width, :half_width]
        gram_second = new_gram[half_width:, half_width:]
        gram_moving = jnp.where(chosen, gram_second, gram_first)
        gram_staying = jnp.where(chosen, gram_first, gram_second)
        moving, staying = split_panels(turned, chosen, half_width)
        moving_vec, staying_vec = split_panels(turned_vec, chosen, half_width)
        arrived, arrived_vec, gram_arrived = from_behind(
            (moving, moving_vec, gram_moving), "col", 1
        )
        matrix = jnp.concatenate([staying, arrived], axis=1)
        vectors = jnp.concatenate([staying_vec, arrived_vec], axis=1)
        if round_index + 1 < ROUNDS:
            cross = lax.psum(local_gram(staying, arrived), "row")
            upper = jnp.concatenate([gram_staying, cross], axis=1)
            lower = jnp.concatenate([cross.T, gram_arrived], axis=1)
            pair_gram = jnp.concatenate([upper, lower], axis=0)
    squares = jnp.sum(matrix * matrix, axis=0)
    totals = lax.psum(squares, "row")
    spread = jnp.sqrt(totals / (matrix.shape[0] * lax.axis_size("row")))
    return (matrix, vectors, spread)


def solution(mesh):
    in_specs = (P("row", "col"), P(None, "col"))
    out_specs = (P("row", "col"), P("row", "col"), P("col"))
    return jax.shard_map(
        per_device, mesh=mesh, in_specs=in_specs, out_specs=out_specs, check_vma=False
    )
```

profile of v0, /device:TPU:0, one launch (start us, length us, event | category | flops | bytes accessed | tf_op | source)
XLA Modules:
  0.0 301.0 jit_solution(12144527679041064644)
XLA Ops:
  7.2 1.2 copy-done
  8.4 2.8 fusion.83
  11.3 0.6 fusion.82
  13.9 53.0 %all-reduce.10.cloned.1.call-done = f32[512,512]{1,0:T(8,128)} async-done(((f32[512,512]{1,0:T(8,128)}), f32[512,512]{1,0:T(8,128)}) %all-reduce.10.cloned.1.call-update) | async-done | bytes 1048592 | tf_op jit(solution)/shard_map/psum | solution.py:63
  66.9 9.5 %gather_fusion = f32[512]{0:T(512)S(1)} fusion(f32[512,512]{1,0:T(8,128)} %all-reduce.10.cloned.1.call-done, s32[512]{0:T(512)S(1)} %bitcast.61), kind=kCustom, calls=%fused_computation | custom fusion | bytes 8192 | tf_op jit(solution)/shard_map/jit(diagonal)/cond/branch_0_fun/gather | solution.py:25
  76.4 0.7 fusion.52
  78.1 1.9 fusion.29
  80.0 1.9 fusion.18
  81.9 1.9 fusion.84
  83.8 1.9 fusion.17
  85.7 1.9 fusion.85
  87.6 1.9 fusion.16
  89.6 2.0 convolution_bitcast_fusion
  91.6 1.9 fusion.87
  93.5 1.9 fusion.88
  95.6 0.8 slice_select_fusion.15
  96.4 1.5 collective-permute-start.1
  97.9 2.0 fusion.8
  99.9 6.0 %collective-permute-done = f32[512,256]{0,1:T(8,128)S(1)} collective-permute-done((f32[512,256]{0,1:T(8,128)S(1)}, f32[512,256]{0,1:T(8,128)S(1)}, u32[]{:S(2)}, u32[]{:S(2)}) %collective-permute-start) | collective-permute-done | bytes 524320 | tf_op jit(solution)/shard_map/ppermute | solution.py:16
  106.0 0.8 copy-done.12
  106.8 1.3 fusion.86
  108.1 1.5 slice_select_fusion.5
  109.6 39.8 %all-reduce.12.cloned.1.call-done = f32[256,256]{1,0:T(8,128)} async-done(((f32[256,256]{1,0:T(8,128)}), f32[256,256]{1,0:T(8,128)}) %all-reduce.12.cloned.1.call-update) | async-done | bytes 262160 | tf_op jit(solution)/shard_map/psum | solution.py:82
  149.5 1.1 copy.25
  150.6 1.2 maximum_maximum_fusion
  151.8 4.8 %gather_fusion.1 = f32[512]{0:T(512)S(1)} fusion(f32[512,512]{0,1:T(8,128)S(1)} %maximum_maximum_fusion, s32[512]{0:T(512)S(1)} %bitcast.62), kind=kCustom, calls=%fused_computation.1 | custom fusion | bytes 8192 | tf_op jit(solution)/shard_map/jit(diagonal)/cond/branch_0_fun/gather | solution.py:25
  156.6 0.7 fusion.51
  158.3 1.9 fusion.30
  160.2 1.9 fusion.15
  162.1 1.9 fusion.89
  164.0 1.9 fusion.14
  165.9 1.9 fusion.90
  167.8 1.9 fusion.13
  169.8 2.3 fusion.19
  172.3 4.6 %fusion.75 = f32[512,512]{1,0:T(8,128)S(1)} fusion(f32[512,512]{0,1:T(8,128)S(1)} %fusion.13, f32[256,256]{0,1:T(8,128)} %collective-permute-done.1, f32[256,256]{0,1:T(8,128)S(1)} %bitcast.65, f32[256,256]{0,1:T(8,128)S(1)} %copy.25, f32[256,256]{0,1:T(8,128)S(1)} %get-tuple-element.29), kind=kOutput, calls=%fused_computation.134 | convolution fusion | flops 1611399168 | bytes 3145728 | tf_op jit(solution)/shard_map/dot_general | solution.py:69
  176.9 1.9 fusion.92
  178.8 0.7 slice_select_fusion.13
  179.5 1.5 collective-permute-start.3
  181.0 4.8 %fusion = f32[1024,512]{0,1:T(8,128)S(1)} fusion(f32[512,512]{0,1:T(8,128)S(1)} %fusion.13, f32[1024,256]{0,1:T(8,128)} %collective-permute-done.5, f32[1024,256]{0,1:T(8,128)S(1)} %copy-done.7), kind=kOutput, calls=%fused_computation.3 | convolution fusion | flops 3221749760 | bytes 5242880 | tf_op jit(solution)/shard_map/dot_general | solution.py:68
  185.8 0.8 copy-done.10
  186.6 1.3 fusion.91
  187.9 1.5 slice_select_fusion.3
  189.6 40.6 %all-reduce.14.cloned.1.call-done = f32[256,256]{1,0:T(8,128)} async-done(((f32[256,256]{1,0:T(8,128)}), f32[256,256]{1,0:T(8,128)}) %all-reduce.14.cloned.1.call-update) | async-done | bytes 262160 | tf_op jit(solution)/shard_map/psum | solution.py:82
  230.2 1.8 copy.30
  232.0 1.3 maximum_maximum_fusion.1
  233.3 4.7 %gather_fusion.2 = f32[512]{0:T(512)S(1)} fusion(f32[512,512]{0,1:T(8,128)S(1)} %maximum_maximum_fusion.1, s32[512]{0:T(512)S(1)} %bitcast.63), kind=kCustom, calls=%fused_computation.2 | custom fusion | bytes 8192 | tf_op jit(solution)/shard_map/jit(diagonal)/cond/branch_0_fun/gather | solution.py:25
  238.1 0.7 fusion.50
  239.8 1.9 fusion.31
  241.7 1.9 fusion.12
  243.6 1.9 fusion.93
  245.5 1.9 fusion.11
  247.4 1.9 fusion.94
  249.4 1.9 fusion.10
  251.3 2.1 fusion.23
  253.4 3.5 %fusion.4 = f32[1024,512]{0,1:T(8,128)S(1)} fusion(f32[512,512]{0,1:T(8,128)S(1)} %fusion.10, f32[1024,256]{0,1:T(8,128)S(1)} %collective-permute-done.6, f32[1024,256]{0,1:T(8,128)S(1)} %copy-done.8), kind=kOutput, calls=%fused_computation.7 | convolution fusion | flops 3221749760 | bytes 5242880 | tf_op jit(solution)/shard_map/dot_general | solution.py:68
  256.9 1.2 slice_select_fusion.1
  258.2 1.6 collective-permute-start.4
  259.9 19.9 %collective-permute-done.4 = f32[512,256]{0,1:T(8,128)S(1)} collective-permute-done((f32[512,256]{0,1:T(8,128)S(1)}, f32[512,256]{0,1:T(8,128)S(1)}, u32[]{:S(2)}, u32[]{:S(2)}) %collective-permute-start.4) | collective-permute-done | bytes 524320 | tf_op jit(solution)/shard_map/ppermute | solution.py:16
  279.8 0.2 multiply_reduce_fusion
  280.0 1.3 copy.35
  281.3 8.9 %psum.31 = f32[512]{0:T(512)S(1)} all-reduce(f32[512]{0:T(512)S(1)} %get-tuple-element.21), channel_id=1, replica_groups=mesh['row'=4,'col'=8] {'row'}, use_global_device_ids=true, to_apply=%region_7.8 | all-reduce | flops 512 | bytes 4096 | tf_op jit(solution)/shard_map/psum | solution.py:87
  290.2 0.6 multiply_sqrt_fusion
  290.8 1.7 pad_maximum_fusion
  292.4 1.8 copy.36
  (62 shorter events, 1.6 us)
Async XLA Ops:
  7.2 1.2 copy-start
  7.2 4.1 %copy-start.14 = (s32[3,1]{0,1:T(1,128)S(1)}, s32[3,1]{0,1:T(1,128)}, u32[]{:S(2)}) copy-start(s32[3,1]{0,1:T(1,128)} %param.3) | copy-start | bytes 40
  7.2 59.7 %all-reduce.10.cloned.1.call-start = ((), (), s32[]{:S(2)}) async-start(), calls=%async_computation | async-start | bytes 2097152 | tf_op jit(solution)/shard_map/psum | solution.py:63
  11.2 138.2 %all-reduce.12.cloned.1.call-start = ((), (), s32[]{:S(2)}) async-start(), calls=%async_computation.1 | async-start | bytes 524288 | tf_op jit(solution)/shard_map/psum | solution.py:82
  66.9 9.5 %copy-start.1 = (f32[512,512]{1,0:T(8,128)S(1)}, f32[512,512]{1,0:T(8,128)}, u32[]{:S(2)}) copy-start(f32[512,512]{1,0:T(8,128)} %all-reduce.10.cloned.1.call-done) | copy-start | bytes 3145732
  95.5 10.5 %copy-start.5 = (f32[512,256]{0,1:T(8,128)}, f32[512,256]{0,1:T(8,128)S(1)}, u32[]{:S(2)}) copy-start(f32[512,256]{0,1:T(8,128)S(1)} %get-tuple-element.32) | copy-start | bytes 1572868
  95.5 10.5 %collective-permute-start = (f32[512,256]{0,1:T(8,128)S(1)}, f32[512,256]{0,1:T(8,128)S(1)}, u32[]{:S(2)}, u32[]{:S(2)}) collective-permute-start(f32[512,256]{0,1:T(8,128)S(1)} %get-tuple-element.31), channel_id=1, source_target_pairs={{7,0},{0,1},{1,2},{2,3},{3,4},{4,5},{5,6},{6,7},{15,8},{8,9},{9,10... | collective-permute-start | bytes 1572872 | tf_op jit(solution)/shard_map/ppermute | solution.py:16
  96.4 54.2 %collective-permute-start.1 = (f32[256,256]{0,1:T(8,128)}, f32[256,256]{0,1:T(8,128)}, u32[]{:S(2)}, u32[]{:S(2)}) collective-permute-start(f32[256,256]{0,1:T(8,128)} %get-tuple-element.30), channel_id=1, source_target_pairs={{7,0},{0,1},{1,2},{2,3},{3,4},{4,5},{5,6},{6,7},{15,8},{8,9},{9,10... | collective-permute-start | bytes 786440 | tf_op jit(solution)/shard_map/ppermute | solution.py:16
  106.0 0.8 copy-start.12
  108.1 122.1 %all-reduce.14.cloned.1.call-start = ((), (), s32[]{:S(2)}) async-start(), calls=%async_computation.2 | async-start | bytes 524288 | tf_op jit(solution)/shard_map/psum | solution.py:82
  109.6 71.4 %collective-permute-start.5 = (f32[1024,256]{0,1:T(8,128)}, f32[1024,256]{0,1:T(8,128)}, u32[]{:S(2)}, u32[]{:S(2)}) collective-permute-start(f32[1024,256]{0,1:T(8,128)} %get-tuple-element.20), channel_id=1, source_target_pairs={{7,0},{0,1},{1,2},{2,3},{3,4},{4,5},{5,6},{6,7},{15,8},{8,9},{9,10... | collective-permute-start | bytes 3145736 | tf_op jit(solution)/shard_map/ppermute | solution.py:16
  150.6 6.0 %copy-start.2 = (f32[256,256]{1,0:T(8,128)S(1)}, f32[256,256]{1,0:T(8,128)}, u32[]{:S(2)}) copy-start(f32[256,256]{1,0:T(8,128)} %all-reduce.12.cloned.1.call-done) | copy-start | bytes 786436
  167.8 1.9 copy-start.6
  167.8 1.9 copy-start.13
  172.2 13.6 %copy-start.3 = (f32[512,256]{0,1:T(8,128)}, f32[512,256]{0,1:T(8,128)S(1)}, u32[]{:S(2)}) copy-start(f32[512,256]{0,1:T(8,128)S(1)} %get-tuple-element.28) | copy-start | bytes 1572868
  172.2 13.6 %collective-permute-start.2 = (f32[512,256]{0,1:T(8,128)S(1)}, f32[512,256]{0,1:T(8,128)S(1)}, u32[]{:S(2)}, u32[]{:S(2)}) collective-permute-start(f32[512,256]{0,1:T(8,128)S(1)} %get-tuple-element.27), channel_id=1, source_target_pairs={{7,0},{0,1},{1,2},{2,3},{3,4},{4,5},{5,6},{6,7},{15,8},{8,9},{9,10... | collective-permute-start | bytes 1572872 | tf_op jit(solution)/shard_map/ppermute | solution.py:16
  176.9 4.1 %copy-start.7 = (f32[1024,256]{0,1:T(8,128)S(1)}, f32[1024,256]{0,1:T(8,128)}, u32[]{:S(2)}) copy-start(f32[1024,256]{0,1:T(8,128)} %get-tuple-element.19) | copy-start | bytes 3145732
  179.5 52.5 %collective-permute-start.3 = (f32[256,256]{0,1:T(8,128)S(1)}, f32[256,256]{0,1:T(8,128)}, u32[]{:S(2)}, u32[]{:S(2)}) collective-permute-start(f32[256,256]{0,1:T(8,128)S(1)} %get-tuple-element.26), channel_id=1, source_target_pairs={{7,0},{0,1},{1,2},{2,3},{3,4},{4,5},{5,6},{6,7},{15,8},{8,9},{9,10... | collective-permute-start | bytes 786440 | tf_op jit(solution)/shard_map/ppermute | solution.py:16
  185.8 0.8 copy-start.10
  189.4 64.0 %collective-permute-start.6 = (f32[1024,256]{0,1:T(8,128)}, f32[1024,256]{0,1:T(8,128)S(1)}, u32[]{:S(2)}, u32[]{:S(2)}) collective-permute-start(f32[1024,256]{0,1:T(8,128)} %get-tuple-element.18), channel_id=1, source_target_pairs={{7,0},{0,1},{1,2},{2,3},{3,4},{4,5},{5,6},{6,7},{15,8},{8,9},{9,10... | collective-permute-start | bytes 3145736 | tf_op jit(solution)/shard_map/ppermute | solution.py:16
  232.0 6.1 %copy-start.9 = (f32[256,256]{1,0:T(8,128)S(1)}, f32[256,256]{1,0:T(8,128)}, u32[]{:S(2)}) copy-start(f32[256,256]{1,0:T(8,128)} %all-reduce.14.cloned.1.call-done) | copy-start | bytes 786436
  249.3 1.9 copy-start.4
  249.4 1.9 copy-start.11
  251.3 2.1 copy-start.8
  258.1 32.6 %collective-permute-start.7 = (f32[1024,256]{0,1:T(8,128)S(1)}, f32[1024,256]{0,1:T(8,128)}, u32[]{:S(2)}, u32[]{:S(2)}) collective-permute-start(f32[1024,256]{0,1:T(8,128)S(1)} %get-tuple-element.16), channel_id=1, source_target_pairs={{7,0},{0,1},{1,2},{2,3},{3,4},{4,5},{5,6},{6,7},{15,8},{8,9},{9,10... | collective-permute-start | bytes 3145736 | tf_op jit(solution)/shard_map/ppermute | solution.py:16
  258.2 21.5 %collective-permute-start.4 = (f32[512,256]{0,1:T(8,128)S(1)}, f32[512,256]{0,1:T(8,128)S(1)}, u32[]{:S(2)}, u32[]{:S(2)}) collective-permute-start(f32[512,256]{0,1:T(8,128)S(1)} %get-tuple-element.24), channel_id=1, source_target_pairs={{7,0},{0,1},{1,2},{2,3},{3,4},{4,5},{5,6},{6,7},{15,8},{8,9},{9,10... | collective-permute-start | bytes 1572872 | tf_op jit(solution)/shard_map/ppermute | solution.py:16
Sparse Core Ops, SparseCore 0:
  11.6 55.1 all-reduce.9
  108.2 41.2 all-reduce.11
  188.1 42.0 all-reduce.13
where the time goes:
time: 304 us; the launch traced here: 301 us
  waiting for transfers between devices  159 us (52%)
  matrix products  66.7 us (22%)
  local copies, waits for them, and re-layouts  28.8 us (9%)
  between operations  18.6 us (6%)
  other arithmetic  13.6 us (4%)
  blocking collectives  8.91 us (3%)
  starting transfers between devices  4.99 us (2%)
    psum x2, waiting for transfers between devices, per_device(): cross = lax.psum(local_gram(staying, arrived), 'row')  80.5 us
    psum x1, waiting for transfers between devices, per_device(): pair_gram = lax.psum(local_gram(matrix, matrix), 'row')  53 us
    ppermute x8, waiting for transfers between devices, from_behind(): return lax.ppermute(block, axis, route)  25.9 us
    gather x3, local copies, waits for them, and re-layouts, rotation(): diagonal = jnp.diagonal(pair_gram) + 1e-06  19 us
    dot_general x9, matrix products, rotation(): product = jnp.dot(iterate, iterate.T, precision=HIGH)  17.1 us
    dot_general x9, matrix products, rotation(): iterate = 1.5 * iterate - 0.5 * jnp.dot(product, iterate, precision=HIGH)  17.1 us
    dot_general x3, matrix products, per_device(): turned_vec = jnp.dot(vectors, turn, precision=HIGH)  10.3 us
    psum x1, blocking collectives, per_device(): totals = lax.psum(squares, 'row')  8.91 us
  transfers between devices with their start and end apart: 11, of which 5 were waited for; matrix products, arithmetic and copies ran while one was open for 22% of the time, Pallas kernels for 0%

commit v1 on v0

v1 whole, which is shorter than its diff:
```python
import functools

import jax
import jax.numpy as jnp
import numpy as np
from jax import lax
from jax.experimental import pallas as pl
from jax.experimental.pallas import tpu as pltpu
from jax.sharding import PartitionSpec as P

ROUNDS = 3
POLAR_STEPS = 3
TAIL = 8
VMEM = pl.BlockSpec(memory_space=pltpu.VMEM)
SMEM = pl.BlockSpec(memory_space=pltpu.SMEM)
PARAMS = pltpu.CompilerParams(vmem_limit_bytes=24 << 20)


def from_behind(block, axis, distance):
    count = lax.axis_size(axis)
    return lax.ppermute(block, axis, [((i - distance) % count, i) for i in range(count)])


def exchange(block, axis, bit):
    return lax.ppermute(block, axis, [(i, i ^ bit) for i in range(lax.axis_size(axis))])


def sum_rows(top, bottom):
    count = lax.axis_size("row")
    bits = [1 << k for k in range(count.bit_length() - 1)]
    assert 1 << len(bits) == count
    for k in range(len(bits)):
        top_in = exchange(top, "row", bits[k])
        bottom_in = exchange(bottom, "row", bits[(k + 1) % len(bits)])
        top, bottom = top + top_in, bottom + bottom_in
    return jnp.concatenate([top, bottom], axis=0)


def cut(value):
    high = value.astype(jnp.bfloat16)
    return high, (value - high.astype(jnp.float32)).astype(jnp.bfloat16)


def dot(left, right, dims=(((1,), (0,)), ((), ()))):
    one = lambda a, b: lax.dot_general(a, b, dims, preferred_element_type=jnp.float32)
    return one(left[0], right[0]) + (one(left[0], right[1]) + one(left[1], right[0]))


def polar_series():
    square, factor = [1.0, 1.0], [1.0]
    for _ in range(POLAR_STEPS):
        step = [-0.5 * c for c in square]
        step[0] += 1.5
        factor = np.convolve(factor, step)
        square = np.convolve(square, np.convolve(step, step))
    return [float(c) for c in factor[1:]]


def rotation_halves(pack_ref):
    half = pack_ref.shape[1]
    cut_row = half // 2
    tail = pack_ref[cut_row : cut_row + TAIL]
    cross = jnp.concatenate([pack_ref[:cut_row], pack_ref[cut_row + TAIL :]], axis=0)
    inverse = 1.0 / jnp.sqrt(tail + 1e-06)
    coupling = (cross * inverse.T[:, 0:1]) * inverse[1:2]
    strength = jnp.sqrt(jnp.sum(coupling * coupling))
    scaled = coupling * (1.0 / (1.0 + strength))
    b, bt = cut(scaled), cut(scaled.T)
    rows = lax.broadcasted_iota(jnp.int32, (half, half), 0)
    cols = lax.broadcasted_iota(jnp.int32, (half, half), 1)
    unit = (rows == cols).astype(jnp.float32)
    c = polar_series()
    x = cut(dot(b, bt))
    x2 = cut(dot(x, x))
    xb = dot(x, b)
    powers = [scaled, xb, dot(x2, b), dot(x2, cut(xb))]
    x4 = cut(dot(x2, x2))
    x8 = cut(dot(x4, x4))
    group = lambda k: sum(c[4 * k + j] * powers[j] for j in range(4))
    high = group(2) + c[12] * dot(x4, b)
    u = cut(group(0) + dot(x4, cut(group(1))) + dot(x8, cut(high)))
    first = unit + dot(u, bt)
    second = unit + dot(bt, u)
    over = scaled + dot(x, u)
    under = -over.T
    chosen = tail[2:3] > 0.5
    staying = jnp.where(chosen, first, over), jnp.where(chosen, under, second)
    moving = jnp.where(chosen, over, first), jnp.where(chosen, second, under)
    return staying, moving


def times(parts, matrix_refs):
    half = parts[0].shape[0]
    if len(matrix_refs) == 1:
        whole = cut(jnp.concatenate(parts, axis=0))
        return dot(cut(matrix_refs[0][...]), whole)
    return dot(cut(matrix_refs[0][...]), cut(parts[0])) + dot(
        cut(matrix_refs[1][...]), cut(parts[1])
    )


def store_gram(left, right, flag, top_ref, bottom_ref):
    cut_row = top_ref.shape[0] - TAIL
    cross = dot(cut(left), cut(right), (((0,), (0,)), ((), ())))
    top_ref[:cut_row] = cross[:cut_row]
    bottom_ref[...] = cross[cut_row:]
    top_ref[cut_row:] = jnp.zeros((TAIL, cross.shape[1]), jnp.float32)
    top_ref[cut_row : cut_row + 1] = jnp.sum(left * left, axis=0, keepdims=True)
    top_ref[cut_row + 1 : cut_row + 2] = jnp.sum(right * right, axis=0, keepdims=True)
    top_ref[cut_row + 2 : cut_row + 3] = jnp.full((1, cross.shape[1]), flag, jnp.float32)


def f32(*shape):
    return jax.ShapeDtypeStruct(shape, jnp.float32)


def gram_shapes(half):
    return [f32(half // 2 + TAIL, half), f32(half - half // 2, half)]


def cost(flops):
    return pl.CostEstimate(flops=int(flops), bytes_accessed=1 << 20, transcendentals=0)


def call(kernel, name, outs, specs, operands, flops, **extra):
    return pl.pallas_call(
        kernel,
        name=name,
        out_shape=outs,
        in_specs=specs,
        out_specs=[VMEM] * len(outs),
        compiler_params=PARAMS,
        cost_estimate=cost(flops),
        **extra,
    )(*operands)


def gram_kernel(matrix_ref, plan_ref, top_ref, bottom_ref):
    half = matrix_ref.shape[1] // 2
    flag = plan_ref[0, 0].astype(jnp.float32)
    store_gram(matrix_ref[:, :half], matrix_ref[:, half:], flag, top_ref, bottom_ref)


def own_kernel(count, pack_ref, *refs):
    matrix_refs, (staying_ref, panel_ref) = refs[:count], refs[count:]
    half = pack_ref.shape[1]
    staying, _ = rotation_halves(pack_ref)
    staying_ref[:half], staying_ref[half:] = staying
    panel_ref[...] = times(staying, matrix_refs)


def next_kernel(round_index, count, pack_ref, plan_ref, panel_ref, *refs):
    matrix_refs, outs = refs[:count], refs[count:]
    staying_ref, moving_ref, arrived_ref, top_ref, bottom_ref = outs
    half = pack_ref.shape[1]
    staying, moving = rotation_halves(pack_ref)
    arrived = times(moving, matrix_refs)
    arrived_ref[...] = arrived
    flag = plan_ref[round_index, 0].astype(jnp.float32)
    store_gram(panel_ref[...], arrived, flag, top_ref, bottom_ref)
    staying_ref[:half], staying_ref[half:] = staying
    moving_ref[:half], moving_ref[half:] = moving


def last_kernel(count, pack_ref, panel_ref, *refs):
    matrix_refs, (moving_ref, matrix_ref, sums_ref) = refs[:count], refs[count:]
    half = pack_ref.shape[1]
    _, moving = rotation_halves(pack_ref)
    panel = panel_ref[...]
    arrived = times(moving, matrix_refs)
    sums_ref[:, :half] = jnp.broadcast_to(jnp.sum(panel * panel, axis=0), (8, half))
    sums_ref[:, half:] = jnp.broadcast_to(jnp.sum(arrived * arrived, axis=0), (8, half))
    matrix_ref[:, :half] = panel
    matrix_ref[:, half:] = arrived
    moving_ref[:half], moving_ref[half:] = moving


def turn_kernel(count, staying_ref, *refs):
    matrix_refs, (panel_ref,) = refs[:count], refs[count:]
    half = staying_ref.shape[1]
    panel_ref[...] = times((staying_ref[:half], staying_ref[half:]), matrix_refs)


def holds(pair, rows_each):
    return lax.div(pair, rows_each) == lax.axis_index("row")


def middle_kernel(rows_each, s10, m11, s11, m12, s20, s21, m21, a0, b0, a1, b1, c1, d1, x1):
    half = s20.shape[1]
    pairs = lax.axis_size("col")
    top = lambda ref: cut(ref[:half])
    bottom = lambda ref: cut(ref[half:])
    own, near, side, far = (cut(ref[...]) for ref in (s10, m11, s11, m12))
    c_value = dot(side, top(m21))
    d_value = dot(far, bottom(m21))
    c1[...] = c_value
    d1[...] = d_value
    behind = lax.rem(lax.axis_index("col") + pairs - 1, pairs)
    x1[...] = jnp.where(holds(behind, rows_each), c_value, d_value)
    a0[...] = dot(own, top(s20))
    b0[...] = dot(near, bottom(s20))
    a1[...] = dot(side, top(s21))
    b1[...] = dot(far, bottom(s21))


def vectors_kernel(rows_each, a0, b0, a1, b1, c1, d1, x1, x2, s3, m3, out):
    half = s3.shape[1]
    pairs = lax.axis_size("col")
    pair = lax.axis_index("col")
    block = lax.axis_index("row") * rows_each + pl.program_id(0)
    behind = lax.rem(pair - block + pairs, pairs)
    zeros = jnp.zeros((out.shape[0], half), jnp.float32)
    top = lambda ref: cut(ref[:half])
    bottom = lambda ref: cut(ref[half:])
    whole = lambda ref: cut(ref[...])

    @pl.when(behind == 0)
    def _():
        out[:, :half] = dot(whole(a0), top(s3))
        out[:, half:] = zeros

    @pl.when(behind == 1)
    def _():
        out[:, :half] = dot(whole(b0), top(s3)) + dot(whole(c1), bottom(s3))
        out[:, half:] = dot(whole(a1), top(m3))

    @pl.when(behind == 2)
    def _():
        out[:, :half] = dot(whole(d1), bottom(s3))
        out[:, half:] = dot(whole(b1), top(m3)) + dot(whole(x1), bottom(m3))

    @pl.when(behind == 3)
    def _():
        two = lax.rem(pair + pairs - 2, pairs)
        far = jnp.where(lax.rem(two, rows_each) == 0, x1[...], x2[...])
        out[:, :half] = zeros
        out[:, half:] = dot(cut(far), bottom(m3))

    @pl.when(behind > 3)
    def _():
        out[:, :half] = zeros
        out[:, half:] = zeros


def per_device(activations, plan):
    rows, width = activations.shape
    half = width // 2
    row_count, pairs = lax.axis_size("row"), lax.axis_size("col")
    assert ROUNDS == 3 and pairs > ROUNDS and pairs % row_count == 0
    rows_each = pairs // row_count
    panel, turn = f32(rows, half), f32(width, half)
    cube = 6 * half**3
    turn_flops = 15 * cube + 6 * rows * width * half

    top, bottom = call(
        gram_kernel, "gram", gram_shapes(half), [VMEM, SMEM], (activations, plan), 2 * cube
    )
    own, near = (activations,), (from_behind(activations, "col", 1),)
    kept, sent, kept_near = [], [], []
    for round_index in range(ROUNDS):
        last = round_index + 1 == ROUNDS
        pack = sum_rows(top, bottom)
        pack_near = from_behind(pack, "col", 1)
        if round_index == 1:
            pack, far_turn = lax.optimization_barrier((pack, sent[0]))
            far_turn = from_behind(far_turn, "col", 1)
        if last:
            pack, c1, d1, x1 = lax.optimization_barrier((pack, c1, d1, x1))
            x2 = lax.ppermute(
                d1,
                "col",
                [(i, (i + 1) % pairs) for i in range(pairs) if (i - 1) % pairs % rows_each],
            )
            x1 = from_behind(x1, "col", 1)
        staying, still = call(
            functools.partial(own_kernel, len(own)),
            "own",
            [turn, panel],
            [VMEM] * (1 + len(own)),
            (pack, *own),
            turn_flops,
        )
        kept.append(staying)
        if last:
            moving, matrix, sums = call(
                functools.partial(last_kernel, len(near)),
                "last",
                [turn, f32(rows, width), f32(8, width)],
                [VMEM] * (2 + len(near)),
                (pack_near, still, *near),
                turn_flops,
            )
            sent.append(moving)
            break
        staying_near, moving, arrived, top, bottom = call(
            functools.partial(next_kernel, round_index + 1, len(near)),
            "next",
            [turn, turn, panel] + gram_shapes(half),
            [VMEM, SMEM, VMEM] + [VMEM] * len(near),
            (pack_near, plan, still, *near),
            turn_flops,
        )
        kept_near.append(staying_near)
        sent.append(moving)
        (still_near,) = call(
            functools.partial(turn_kernel, len(near)),
            "turn",
            [panel],
            [VMEM] * (1 + len(near)),
            (staying_near, *near),
            4 * cube,
        )
        own, near = (still, arrived), (still_near, from_behind(arrived, "col", 1))
        if round_index == 1:
            a0, b0, a1, b1, c1, d1, x1 = call(
                functools.partial(middle_kernel, rows_each),
                "middle",
                [turn] * 7,
                [VMEM] * 7,
                (kept[0], sent[0], kept_near[0], far_turn, kept[1], kept_near[1], sent[1]),
                12 * cube,
            )
    bits = [1 << k for k in range(row_count.bit_length() - 1)]
    for bit in bits:
        sums = sums + exchange(sums, "row", bit)
    spread = jnp.sqrt(sums[0] / (rows * row_count))
    vectors = pl.pallas_call(
        functools.partial(vectors_kernel, rows_each),
        name="vectors",
        grid=(rows_each,),
        out_shape=f32(rows_each * width, width),
        in_specs=[VMEM] * 10,
        out_specs=pl.BlockSpec((width, width), lambda i: (i, 0)),
        compiler_params=PARAMS,
        cost_estimate=cost(8 * cube),
    )(a0, b0, a1, b1, c1, d1, x1, x2, kept[2], sent[2])
    return (matrix, vectors, spread)


def solution(mesh):
    in_specs = (P("row", "col"), P(None, "col"))
    out_specs = (P("row", "col"), P("row", "col"), P("col"))
    return jax.shard_map(
        per_device, mesh=mesh, in_specs=in_specs, out_specs=out_specs, check_vma=False
    )
```

time: 304 us -> 91.7 us (0.30)
  waiting for transfers between devices: 159 us -> 34.3 us
  matrix products: 66.7 us -> 0 us
  Pallas kernels: 0 us -> 29.5 us
  local copies, waits for them, and re-layouts: 28.8 us -> 1.96 us
  starting transfers between devices: 4.99 us -> 24 us
  between operations: 18.6 us -> 0.86 us
  other arithmetic: 13.6 us -> 0.9 us
  blocking collectives: 8.91 us -> 0 us
    psum x3 -> x0, waiting for transfers between devices: 133 us -> none  [the longest x2 80.5 us: per_device(): cross = lax.psum(local_gram(staying, arrived), 'row')]
    dot_general x31 -> x0, matrix products: 66.7 us -> none  [the longest x9 17.1 us: rotation(): product = jnp.dot(iterate, iterate.T, precision=HIGH)]
    pallas_call x0 -> x11, Pallas kernels: none -> 29.5 us  [the longest x10 27.8 us: call(): pl.pallas_call(kernel, name=name, out_shape=outs, in_specs=specs, out_spe...]
    ppermute x8 -> x23, starting transfers between devices: 4.87 us -> 24 us  [the longest x14 20.4 us: exchange(): lax.ppermute(block, axis, [(i, i ^ bit) for i in range(lax.axis_size(axis...]
    gather x3 -> x0, local copies, waits for them, and re-layouts: 19 us -> none  [rotation(): diagonal = jnp.diagonal(pair_gram) + 1e-06]
    psum x1 -> x0, blocking collectives: 8.91 us -> none  [per_device(): totals = lax.psum(squares, 'row')]
    ppermute x8 -> x23, waiting for transfers between devices: 25.9 us -> 34.3 us  [the longest x14 25.6 us: exchange(): lax.ppermute(block, axis, [(i, i ^ bit) for i in range(lax.axis_size(axis...]
    select_n x8 -> x0, other arithmetic: 6.04 us -> none  [the longest x4 4.26 us: split_panels(): staying = jnp.where(chosen, first_panel, second_panel)]
  transfers between devices with their start and end apart: 11 -> 23, of which waited for: 5 -> 13; matrix products, arithmetic and copies ran while one was open for 22% -> 2% of each run, Pallas kernels for 0% -> 25%
where the time goes in v1:
time: 91.7 us; the launch traced here: 91.6 us
  waiting for transfers between devices  34.3 us (37%)
  Pallas kernels  29.5 us (32%)
  starting transfers between devices  24 us (26%)
  local copies, waits for them, and re-layouts  1.96 us (2%)
    pallas_call x10, Pallas kernels, call(): pl.pallas_call(kernel, name=name, out_shape=outs, in_specs=specs, out_spe...  27.8 us
    ppermute x14, waiting for transfers between devices, exchange(): lax.ppermute(block, axis, [(i, i ^ bit) for i in range(lax.axis_size(axis...  25.6 us
    ppermute x14, starting transfers between devices, exchange(): lax.ppermute(block, axis, [(i, i ^ bit) for i in range(lax.axis_size(axis...  20.4 us
    ppermute x8, waiting for transfers between devices, from_behind(): lax.ppermute(block, axis, [((i - distance) % count, i) for i in range(cou...  8.67 us
    ppermute x8, starting transfers between devices, from_behind(): lax.ppermute(block, axis, [((i - distance) % count, i) for i in range(cou...  2.11 us
    unnamed x3, local copies, waits for them, and re-layouts  1.96 us
  transfers between devices with their start and end apart: 23, of which 13 were waited for; matrix products, arithmetic and copies ran while one was open for 2% of the time, Pallas kernels for 25%

profile of v1, /device:TPU:0, one launch (start us, length us, event | category | flops | bytes accessed | tf_op | source)
XLA Modules:
  0.0 91.6 jit_solution(9390716829218832413)
XLA Ops:
  0.6 0.5 collective-permute-start.5
  1.2 0.7 copy.5.plan_ref
  1.9 0.0 copy-start
  1.9 1.2 %copy-done = f32[512,512]{1,0:T(8,128)S(1)} copy-done((f32[512,512]{1,0:T(8,128)S(1)}, f32[512,512]{1,0:T(8,128)}, u32[]{:S(2)}) %copy-start) | copy-done | bytes 1048600
  3.1 1.0 %gram.1 = (f32[136,256]{1,0:T(8,128)S(1)}, f32[128,256]{1,0:T(8,128)S(1)}) custom-call(f32[512,512]{1,0:T(8,128)S(1)} %copy-done, s32[3,1]{1,0:T(4,128)S(1)} %copy.5.plan_ref), custom_call_target="tpu_custom_call" | custom-call | flops 201326592 | bytes 1048576 | tf_op jit(solution)/shard_map/gram/pallas_call | solution.py:126
  4.2 2.6 %collective-permute-start = (f32[136,256]{1,0:T(8,128)S(1)}, f32[136,256]{1,0:T(8,128)S(1)}, u32[]{:S(2)}, u32[]{:S(2)}) collective-permute-start(f32[136,256]{1,0:T(8,128)S(1)} %get-tuple-element.37), channel_id=1, source_target_pairs={{0,8},{8,0},{16,24},{24,16},{1,9},{9,1},{17,25},{25,17},{2,10},{10... | collective-permute-start | bytes 417800 | tf_op jit(solution)/shard_map/ppermute | solution.py:25
  6.7 1.5 %collective-permute-start.2 = (f32[128,256]{1,0:T(8,128)S(1)}, f32[128,256]{1,0:T(8,128)S(1)}, u32[]{:S(2)}, u32[]{:S(2)}) collective-permute-start(f32[128,256]{1,0:T(8,128)S(1)} %get-tuple-element.38), channel_id=1, source_target_pairs={{0,16},{8,24},{16,0},{24,8},{1,17},{9,25},{17,1},{25,9},{2,18},{10... | collective-permute-start | bytes 393224 | tf_op jit(solution)/shard_map/ppermute | solution.py:25
  8.3 1.8 %collective-permute-done = f32[136,256]{1,0:T(8,128)S(1)} collective-permute-done((f32[136,256]{1,0:T(8,128)S(1)}, f32[136,256]{1,0:T(8,128)S(1)}, u32[]{:S(2)}, u32[]{:S(2)}) %collective-permute-start) | collective-permute-done | bytes 139296 | tf_op jit(solution)/shard_map/ppermute | solution.py:25
  10.1 2.6 %collective-permute-start.1 = (f32[136,256]{1,0:T(8,128)S(1)}, f32[136,256]{1,0:T(8,128)S(1)}, u32[]{:S(2)}, u32[]{:S(2)}) collective-permute-start(f32[136,256]{1,0:T(8,128)S(1)} %add.42), channel_id=1, source_target_pairs={{0,16},{8,24},{16,0},{24,8},{1,17},{9,25},{17,1},{25,9},{2,18},{10... | collective-permute-start | bytes 417800 | tf_op jit(solution)/shard_map/ppermute | solution.py:25
  12.7 0.0 collective-permute-done.2
  12.7 1.6 %collective-permute-start.3 = (f32[128,256]{1,0:T(8,128)S(1)}, f32[128,256]{1,0:T(8,128)S(1)}, u32[]{:S(2)}, u32[]{:S(2)}) collective-permute-start(f32[128,256]{1,0:T(8,128)S(1)} %add.44), channel_id=1, source_target_pairs={{0,8},{8,0},{16,24},{24,16},{1,9},{9,1},{17,25},{25,17},{2,10},{10... | collective-permute-start | bytes 393224 | tf_op jit(solution)/shard_map/ppermute | solution.py:25
  14.3 4.4 %collective-permute-done.3 = f32[128,256]{1,0:T(8,128)S(1)} collective-permute-done((f32[128,256]{1,0:T(8,128)S(1)}, f32[128,256]{1,0:T(8,128)S(1)}, u32[]{:S(2)}, u32[]{:S(2)}) %collective-permute-start.3) | collective-permute-done | bytes 131104 | tf_op jit(solution)/shard_map/ppermute | solution.py:25
  18.7 0.0 collective-permute-done.1
  18.8 0.1 collective-permute-start.4
  18.9 3.4 %own.3 = (f32[512,256]{1,0:T(8,128)S(1)}, f32[512,256]{1,0:T(8,128)S(1)}) custom-call(f32[264,256]{1,0:T(8,128)S(1)} %pad_maximum_fusion.pack_ref, f32[512,512]{1,0:T(8,128)S(1)} %copy-done), custom_call_target="tpu_custom_call" | custom-call | flops 1912602624 | bytes 1048576 | tf_op jit(solution)/shard_map/own/pallas_call | solution.py:126
  22.3 4.2 %collective-permute-done.4.pack_ref = f32[264,256]{1,0:T(8,128)S(1)} collective-permute-done((f32[264,256]{1,0:T(8,128)S(1)}, f32[264,256]{1,0:T(8,128)S(1)}, u32[]{:S(2)}, u32[]{:S(2)}) %collective-permute-start.4) | collective-permute-done | bytes 270368 | tf_op jit(solution)/shard_map/ppermute | solution.py:21
  26.5 0.0 collective-permute-done.5.refs_0_
  26.6 4.8 %next.2 = (f32[512,256]{1,0:T(8,128)S(1)}, f32[512,256]{1,0:T(8,128)S(1)}, f32[512,256]{1,0:T(8,128)S(1)}, f32[136,256]{1,0:T(8,128)S(1)}, f32[128,256]{1,0:T(8,128)S(1)}) custom-call(f32[264,256]{1,0:T(8,128)S(1)} %collective-permute-done.4.pack_ref, s32[3,1]{1,0:T(4,128)S(1)} %copy.5.plan_ref, f32[512,256]{1,0:T(8,128)S(1)} %get-tuple-element.39.panel_ref.refs_0_, ...), custom_call_target="tpu_custom_call" | custom-call | flops 1912602624 | bytes 1048576 | tf_op jit(solution)/shard_map/next/pallas_call | solution.py:126
  31.3 1.6 %collective-permute-start.6 = (f32[136,256]{1,0:T(8,128)S(1)}, f32[136,256]{1,0:T(8,128)S(1)}, u32[]{:S(2)}, u32[]{:S(2)}) collective-permute-start(f32[136,256]{1,0:T(8,128)S(1)} %get-tuple-element.40), channel_id=1, source_target_pairs={{0,8},{8,0},{16,24},{24,16},{1,9},{9,1},{17,25},{25,17},{2,10},{10... | collective-permute-start | bytes 417800 | tf_op jit(solution)/shard_map/ppermute | solution.py:25
  32.9 0.5 collective-permute-start.8
  33.4 3.0 %collective-permute-done.6 = f32[136,256]{1,0:T(8,128)S(1)} collective-permute-done((f32[136,256]{1,0:T(8,128)S(1)}, f32[136,256]{1,0:T(8,128)S(1)}, u32[]{:S(2)}, u32[]{:S(2)}) %collective-permute-start.6) | collective-permute-done | bytes 139296 | tf_op jit(solution)/shard_map/ppermute | solution.py:25
  36.5 1.6 %collective-permute-start.7 = (f32[136,256]{1,0:T(8,128)S(1)}, f32[136,256]{1,0:T(8,128)S(1)}, u32[]{:S(2)}, u32[]{:S(2)}) collective-permute-start(f32[136,256]{1,0:T(8,128)S(1)} %add.46), channel_id=1, source_target_pairs={{0,16},{8,24},{16,0},{24,8},{1,17},{9,25},{17,1},{25,9},{2,18},{10... | collective-permute-start | bytes 417800 | tf_op jit(solution)/shard_map/ppermute | solution.py:25
  38.0 0.0 collective-permute-start.11
  38.0 0.3 collective-permute-done.8
  38.3 1.5 %collective-permute-start.9 = (f32[128,256]{1,0:T(8,128)S(1)}, f32[128,256]{1,0:T(8,128)S(1)}, u32[]{:S(2)}, u32[]{:S(2)}) collective-permute-start(f32[128,256]{1,0:T(8,128)S(1)} %add.48), channel_id=1, source_target_pairs={{0,8},{8,0},{16,24},{24,16},{1,9},{9,1},{17,25},{25,17},{2,10},{10... | collective-permute-start | bytes 393224 | tf_op jit(solution)/shard_map/ppermute | solution.py:25
  39.9 3.6 %collective-permute-done.9 = f32[128,256]{1,0:T(8,128)S(1)} collective-permute-done((f32[128,256]{1,0:T(8,128)S(1)}, f32[128,256]{1,0:T(8,128)S(1)}, u32[]{:S(2)}, u32[]{:S(2)}) %collective-permute-start.9) | collective-permute-done | bytes 131104 | tf_op jit(solution)/shard_map/ppermute | solution.py:25
  43.4 0.0 collective-permute-done.7
  43.5 0.1 collective-permute-start.10
  43.6 0.6 turn.2.refs_0_
  44.2 1.3 %collective-permute-start.17 = (f32[512,256]{1,0:T(8,128)S(1)}, f32[512,256]{1,0:T(8,128)S(1)}, u32[]{:S(2)}, u32[]{:S(2)}) collective-permute-start(f32[512,256]{1,0:T(8,128)S(1)} %get-tuple-element.50.m11), channel_id=1, source_target_pairs={{7,0},{0,1},{1,2},{2,3},{3,4},{4,5},{5,6},{6,7},{15,8},{8,9},{9,10... | collective-permute-start | bytes 1572872 | tf_op jit(solution)/shard_map/ppermute | solution.py:21
  45.5 3.4 %own.4 = (f32[512,256]{1,0:T(8,128)S(1)}, f32[512,256]{1,0:T(8,128)S(1)}) custom-call(f32[264,256]{1,0:T(8,128)S(1)} %pad_maximum_fusion.1.pack_ref, f32[512,256]{1,0:T(8,128)S(1)} %get-tuple-element.39.panel_ref.refs_0_, f32[512,256]{1,0:T(8,128)S(1)} %get-tuple-element.44.refs_1_), custom_call_target="tpu_custom_call" | custom-call | flops 1912602624 | bytes 1048576 | tf_op jit(solution)/shard_map/own/pallas_call | solution.py:126
  48.9 0.0 collective-permute-done.11.refs_1_
  48.9 2.4 %collective-permute-done.10.pack_ref = f32[264,256]{1,0:T(8,128)S(1)} collective-permute-done((f32[264,256]{1,0:T(8,128)S(1)}, f32[264,256]{1,0:T(8,128)S(1)}, u32[]{:S(2)}, u32[]{:S(2)}) %collective-permute-start.10) | collective-permute-done | bytes 270368 | tf_op jit(solution)/shard_map/ppermute | solution.py:21
  51.3 4.7 %next.3 = (f32[512,256]{1,0:T(8,128)S(1)}, f32[512,256]{1,0:T(8,128)S(1)}, f32[512,256]{1,0:T(8,128)S(1)}, f32[136,256]{1,0:T(8,128)S(1)}, f32[128,256]{1,0:T(8,128)S(1)}) custom-call(f32[264,256]{1,0:T(8,128)S(1)} %collective-permute-done.10.pack_ref, s32[3,1]{1,0:T(4,128)S(1)} %copy.5.plan_ref, f32[512,256]{1,0:T(8,128)S(1)} %get-tuple-element.45.panel_ref.refs_0_, ...), custom_call_target="tpu_custom_call" | custom-call | flops 1912602624 | bytes 1048576 | tf_op jit(solution)/shard_map/next/pallas_call | solution.py:126
  56.0 1.4 %collective-permute-start.12 = (f32[136,256]{1,0:T(8,128)S(1)}, f32[136,256]{1,0:T(8,128)S(1)}, u32[]{:S(2)}, u32[]{:S(2)}) collective-permute-start(f32[136,256]{1,0:T(8,128)S(1)} %get-tuple-element.47), channel_id=1, source_target_pairs={{0,8},{8,0},{16,24},{24,16},{1,9},{9,1},{17,25},{25,17},{2,10},{10... | collective-permute-start | bytes 417800 | tf_op jit(solution)/shard_map/ppermute | solution.py:25
  57.4 0.7 collective-permute-start.14
  58.1 3.3 %collective-permute-done.12 = f32[136,256]{1,0:T(8,128)S(1)} collective-permute-done((f32[136,256]{1,0:T(8,128)S(1)}, f32[136,256]{1,0:T(8,128)S(1)}, u32[]{:S(2)}, u32[]{:S(2)}) %collective-permute-start.12) | collective-permute-done | bytes 139296 | tf_op jit(solution)/shard_map/ppermute | solution.py:25
  61.4 1.1 %collective-permute-start.13 = (f32[136,256]{1,0:T(8,128)S(1)}, f32[136,256]{1,0:T(8,128)S(1)}, u32[]{:S(2)}, u32[]{:S(2)}) collective-permute-start(f32[136,256]{1,0:T(8,128)S(1)} %add.50), channel_id=1, source_target_pairs={{0,16},{8,24},{16,0},{24,8},{1,17},{9,25},{17,1},{25,9},{2,18},{10... | collective-permute-start | bytes 417800 | tf_op jit(solution)/shard_map/ppermute | solution.py:25
  62.5 1.0 %collective-permute-done.14 = f32[128,256]{1,0:T(8,128)S(1)} collective-permute-done((f32[128,256]{1,0:T(8,128)S(1)}, f32[128,256]{1,0:T(8,128)S(1)}, u32[]{:S(2)}, u32[]{:S(2)}) %collective-permute-start.14) | collective-permute-done | bytes 131104 | tf_op jit(solution)/shard_map/ppermute | solution.py:25
  63.6 0.4 collective-permute-start.15
  64.0 0.0 collective-permute-start.18
  64.1 0.6 turn.3.refs_0_
  64.7 4.0 %collective-permute-done.15 = f32[128,256]{1,0:T(8,128)S(1)} collective-permute-done((f32[128,256]{1,0:T(8,128)S(1)}, f32[128,256]{1,0:T(8,128)S(1)}, u32[]{:S(2)}, u32[]{:S(2)}) %collective-permute-start.15) | collective-permute-done | bytes 131104 | tf_op jit(solution)/shard_map/ppermute | solution.py:25
  68.7 0.0 collective-permute-done.13
  68.7 0.1 collective-permute-start.16
  68.8 0.0 collective-permute-done.17.m12
  68.8 1.4 %middle.1 = (f32[512,256]{1,0:T(8,128)S(1)}, f32[512,256]{1,0:T(8,128)S(1)}, f32[512,256]{1,0:T(8,128)S(1)}, f32[512,256]{1,0:T(8,128)S(1)}, f32[512,256]{1,0:T(...) custom-call(f32[512,256]{1,0:T(8,128)S(1)} %get-tuple-element.49.s10, f32[512,256]{1,0:T(8,128)S(1)} %get-tuple-element.50.m11, ...), custom_call_target="tpu_custom_call" | custom-call | flops 1207959552 | bytes 1048576 | tf_op jit(solution)/shard_map/middle/pallas_call | solution.py:126
  70.3 0.1 collective-permute-start.19
  70.3 1.5 %collective-permute-start.20 = (f32[512,256]{1,0:T(8,128)S(1)}, f32[512,256]{1,0:T(8,128)S(1)}, u32[]{:S(2)}, u32[]{:S(2)}) collective-permute-start(f32[512,256]{1,0:T(8,128)S(1)} %get-tuple-element.66.d1), channel_id=1, source_target_pairs={{0,1},{2,3},{4,5},{6,7},{8,9},{10,11},{12,13},{14,15},{16,17},{18,... | collective-permute-start | bytes 1572872 | tf_op jit(solution)/shard_map/ppermute | solution.py:269
  71.9 3.4 %own.5 = (f32[512,256]{1,0:T(8,128)S(1)}, f32[512,256]{1,0:T(8,128)S(1)}) custom-call(f32[264,256]{1,0:T(8,128)S(1)} %pad_maximum_fusion.2.pack_ref, f32[512,256]{1,0:T(8,128)S(1)} %get-tuple-element.45.panel_ref.refs_0_, f32[512,256]{1,0:T(8,128)S(1)} %get-tuple-element.58.refs_1_), custom_call_target="tpu_custom_call" | custom-call | flops 1912602624 | bytes 1048576 | tf_op jit(solution)/shard_map/own/pallas_call | solution.py:126
  75.3 0.0 collective-permute-done.18.refs_1_
  75.3 2.0 %collective-permute-done.16.pack_ref = f32[264,256]{1,0:T(8,128)S(1)} collective-permute-done((f32[264,256]{1,0:T(8,128)S(1)}, f32[264,256]{1,0:T(8,128)S(1)}, u32[]{:S(2)}, u32[]{:S(2)}) %collective-permute-start.16) | collective-permute-done | bytes 270368 | tf_op jit(solution)/shard_map/ppermute | solution.py:21
  77.3 4.4 %last.1 = (f32[512,256]{1,0:T(8,128)S(1)}, f32[512,512]{1,0:T(8,128)}, f32[8,512]{1,0:T(8,128)S(1)}) custom-call(f32[264,256]{1,0:T(8,128)S(1)} %collective-permute-done.16.pack_ref, f32[512,256]{1,0:T(8,128)S(1)} %get-tuple-element.59.panel_ref, f32[512,256]{1,0:T(8,128)S(1)} %turn.3.refs_0_, f32[512,256]{1,0:T(8,128)S(1)} %collective-permute-done.18.refs_1_), custom_call_target="tpu_custom_call" | custom-call | flops 1912602624 | bytes 1048576 | tf_op jit(solution)/shard_map/last/pallas_call | solution.py:126
  81.8 1.7 %collective-permute-start.21 = (f32[8,512]{1,0:T(8,128)S(1)}, f32[8,512]{1,0:T(8,128)S(1)}, u32[]{:S(2)}, u32[]{:S(2)}) collective-permute-start(f32[8,512]{1,0:T(8,128)S(1)} %get-tuple-element.70), channel_id=1, source_target_pairs={{0,8},{8,0},{16,24},{24,16},{1,9},{9,1},{17,25},{25,17},{2,10},{10... | collective-permute-start | bytes 49160 | tf_op jit(solution)/shard_map/ppermute | solution.py:25
  83.4 2.1 %collective-permute-done.21 = f32[8,512]{1,0:T(8,128)S(1)} collective-permute-done((f32[8,512]{1,0:T(8,128)S(1)}, f32[8,512]{1,0:T(8,128)S(1)}, u32[]{:S(2)}, u32[]{:S(2)}) %collective-permute-start.21) | collective-permute-done | bytes 16416 | tf_op jit(solution)/shard_map/ppermute | solution.py:25
  85.5 1.7 %collective-permute-start.22 = (f32[8,512]{1,0:T(8,128)S(1)}, f32[8,512]{1,0:T(8,128)S(1)}, u32[]{:S(2)}, u32[]{:S(2)}) collective-permute-start(f32[8,512]{1,0:T(8,128)S(1)} %add.54), channel_id=1, source_target_pairs={{0,16},{8,24},{16,0},{24,8},{1,17},{9,25},{17,1},{25,9},{2,18},{10... | collective-permute-start | bytes 49160 | tf_op jit(solution)/shard_map/ppermute | solution.py:25
  87.2 2.1 %collective-permute-done.22 = f32[8,512]{1,0:T(8,128)S(1)} collective-permute-done((f32[8,512]{1,0:T(8,128)S(1)}, f32[8,512]{1,0:T(8,128)S(1)}, u32[]{:S(2)}, u32[]{:S(2)}) %collective-permute-start.22) | collective-permute-done | bytes 16416 | tf_op jit(solution)/shard_map/ppermute | solution.py:25
  89.2 0.6 fusion.1
  89.8 0.0 collective-permute-done.19.x1
  89.8 0.0 collective-permute-done.20.x2
  89.8 1.7 %vectors.1 = f32[1024,512]{1,0:T(8,128)} custom-call(f32[512,256]{1,0:T(8,128)S(1)} %get-tuple-element.61.a0, f32[512,256]{1,0:T(8,128)S(1)} %get-tuple-element.62.b0, f32[512,256]{1,0:T(8,128)S(1)} %get-tuple-element.63.a1, f32[512,256]{1,0:T(8,128)S(1)} %get-tuple-element.64.b1, f32[512,256]{1,0:T(8,128)S(1)} %get-tuple-element.65.c1, ...), custom_call_target="tpu_custom_call" | custom-call | flops 805306368 | bytes 1048576 | tf_op jit(solution)/shard_map/vectors/pallas_call | solution.py:327
  (16 shorter events, 0.3 us)
Async XLA Ops:
  0.6 25.9 %collective-permute-start.5 = (f32[512,512]{1,0:T(8,128)}, f32[512,512]{1,0:T(8,128)S(1)}, u32[]{:S(2)}, u32[]{:S(2)}) collective-permute-start(f32[512,512]{1,0:T(8,128)} %refs_0_.1), channel_id=1, source_target_pairs={{7,0},{0,1},{1,2},{2,3},{3,4},{4,5},{5,6},{6,7},{15,8},{8,9},{9,10... | collective-permute-start | bytes 3145736 | tf_op jit(solution)/shard_map/ppermute | solution.py:21
  1.9 1.2 %copy-start = (f32[512,512]{1,0:T(8,128)S(1)}, f32[512,512]{1,0:T(8,128)}, u32[]{:S(2)}) copy-start(f32[512,512]{1,0:T(8,128)} %refs_0_.1) | copy-start | bytes 3145732
  4.2 5.9 %collective-permute-start = (f32[136,256]{1,0:T(8,128)S(1)}, f32[136,256]{1,0:T(8,128)S(1)}, u32[]{:S(2)}, u32[]{:S(2)}) collective-permute-start(f32[136,256]{1,0:T(8,128)S(1)} %get-tuple-element.37), channel_id=1, source_target_pairs={{0,8},{8,0},{16,24},{24,16},{1,9},{9,1},{17,25},{25,17},{2,10},{10... | collective-permute-start | bytes 417800 | tf_op jit(solution)/shard_map/ppermute | solution.py:25
  6.7 5.9 %collective-permute-start.2 = (f32[128,256]{1,0:T(8,128)S(1)}, f32[128,256]{1,0:T(8,128)S(1)}, u32[]{:S(2)}, u32[]{:S(2)}) collective-permute-start(f32[128,256]{1,0:T(8,128)S(1)} %get-tuple-element.38), channel_id=1, source_target_pairs={{0,16},{8,24},{16,0},{24,8},{1,17},{9,25},{17,1},{25,9},{2,18},{10... | collective-permute-start | bytes 393224 | tf_op jit(solution)/shard_map/ppermute | solution.py:25
  10.1 8.6 %collective-permute-start.1 = (f32[136,256]{1,0:T(8,128)S(1)}, f32[136,256]{1,0:T(8,128)S(1)}, u32[]{:S(2)}, u32[]{:S(2)}) collective-permute-start(f32[136,256]{1,0:T(8,128)S(1)} %add.42), channel_id=1, source_target_pairs={{0,16},{8,24},{16,0},{24,8},{1,17},{9,25},{17,1},{25,9},{2,18},{10... | collective-permute-start | bytes 417800 | tf_op jit(solution)/shard_map/ppermute | solution.py:25
  12.7 6.0 %collective-permute-start.3 = (f32[128,256]{1,0:T(8,128)S(1)}, f32[128,256]{1,0:T(8,128)S(1)}, u32[]{:S(2)}, u32[]{:S(2)}) collective-permute-start(f32[128,256]{1,0:T(8,128)S(1)} %add.44), channel_id=1, source_target_pairs={{0,8},{8,0},{16,24},{24,16},{1,9},{9,1},{17,25},{25,17},{2,10},{10... | collective-permute-start | bytes 393224 | tf_op jit(solution)/shard_map/ppermute | solution.py:25
  18.8 7.7 %collective-permute-start.4 = (f32[264,256]{1,0:T(8,128)S(1)}, f32[264,256]{1,0:T(8,128)S(1)}, u32[]{:S(2)}, u32[]{:S(2)}) collective-permute-start(f32[264,256]{1,0:T(8,128)S(1)} %pad_maximum_fusion.pack_ref), channel_id=1, source_target_pairs={{7,0},{0,1},{1,2},{2,3},{3,4},{4,5},{5,6},{6,7},{15,8},{8,9},{9,10... | collective-permute-start | bytes 811016 | tf_op jit(solution)/shard_map/ppermute | solution.py:21
  31.3 5.1 %collective-permute-start.6 = (f32[136,256]{1,0:T(8,128)S(1)}, f32[136,256]{1,0:T(8,128)S(1)}, u32[]{:S(2)}, u32[]{:S(2)}) collective-permute-start(f32[136,256]{1,0:T(8,128)S(1)} %get-tuple-element.40), channel_id=1, source_target_pairs={{0,8},{8,0},{16,24},{24,16},{1,9},{9,1},{17,25},{25,17},{2,10},{10... | collective-permute-start | bytes 417800 | tf_op jit(solution)/shard_map/ppermute | solution.py:25
  32.9 5.4 %collective-permute-start.8 = (f32[128,256]{1,0:T(8,128)S(1)}, f32[128,256]{1,0:T(8,128)S(1)}, u32[]{:S(2)}, u32[]{:S(2)}) collective-permute-start(f32[128,256]{1,0:T(8,128)S(1)} %get-tuple-element.41), channel_id=1, source_target_pairs={{0,16},{8,24},{16,0},{24,8},{1,17},{9,25},{17,1},{25,9},{2,18},{10... | collective-permute-start | bytes 393224 | tf_op jit(solution)/shard_map/ppermute | solution.py:25
  36.5 7.0 %collective-permute-start.7 = (f32[136,256]{1,0:T(8,128)S(1)}, f32[136,256]{1,0:T(8,128)S(1)}, u32[]{:S(2)}, u32[]{:S(2)}) collective-permute-start(f32[136,256]{1,0:T(8,128)S(1)} %add.46), channel_id=1, source_target_pairs={{0,16},{8,24},{16,0},{24,8},{1,17},{9,25},{17,1},{25,9},{2,18},{10... | collective-permute-start | bytes 417800 | tf_op jit(solution)/shard_map/ppermute | solution.py:25
  38.0 10.9 %collective-permute-start.11 = (f32[512,256]{1,0:T(8,128)S(1)}, f32[512,256]{1,0:T(8,128)S(1)}, u32[]{:S(2)}, u32[]{:S(2)}) collective-permute-start(f32[512,256]{1,0:T(8,128)S(1)} %get-tuple-element.44.refs_1_), channel_id=1, source_target_pairs={{7,0},{0,1},{1,2},{2,3},{3,4},{4,5},{5,6},{6,7},{15,8},{8,9},{9,10... | collective-permute-start | bytes 1572872 | tf_op jit(solution)/shard_map/ppermute | solution.py:21
  38.3 5.1 %collective-permute-start.9 = (f32[128,256]{1,0:T(8,128)S(1)}, f32[128,256]{1,0:T(8,128)S(1)}, u32[]{:S(2)}, u32[]{:S(2)}) collective-permute-start(f32[128,256]{1,0:T(8,128)S(1)} %add.48), channel_id=1, source_target_pairs={{0,8},{8,0},{16,24},{24,16},{1,9},{9,1},{17,25},{25,17},{2,10},{10... | collective-permute-start | bytes 393224 | tf_op jit(solution)/shard_map/ppermute | solution.py:25
  43.5 7.8 %collective-permute-start.10 = (f32[264,256]{1,0:T(8,128)S(1)}, f32[264,256]{1,0:T(8,128)S(1)}, u32[]{:S(2)}, u32[]{:S(2)}) collective-permute-start(f32[264,256]{1,0:T(8,128)S(1)} %pad_maximum_fusion.1.pack_ref), channel_id=1, source_target_pairs={{7,0},{0,1},{1,2},{2,3},{3,4},{4,5},{5,6},{6,7},{15,8},{8,9},{9,10... | collective-permute-start | bytes 811016 | tf_op jit(solution)/shard_map/ppermute | solution.py:21
  44.2 24.6 %collective-permute-start.17 = (f32[512,256]{1,0:T(8,128)S(1)}, f32[512,256]{1,0:T(8,128)S(1)}, u32[]{:S(2)}, u32[]{:S(2)}) collective-permute-start(f32[512,256]{1,0:T(8,128)S(1)} %get-tuple-element.50.m11), channel_id=1, source_target_pairs={{7,0},{0,1},{1,2},{2,3},{3,4},{4,5},{5,6},{6,7},{15,8},{8,9},{9,10... | collective-permute-start | bytes 1572872 | tf_op jit(solution)/shard_map/ppermute | solution.py:21
  56.0 5.4 %collective-permute-start.12 = (f32[136,256]{1,0:T(8,128)S(1)}, f32[136,256]{1,0:T(8,128)S(1)}, u32[]{:S(2)}, u32[]{:S(2)}) collective-permute-start(f32[136,256]{1,0:T(8,128)S(1)} %get-tuple-element.47), channel_id=1, source_target_pairs={{0,8},{8,0},{16,24},{24,16},{1,9},{9,1},{17,25},{25,17},{2,10},{10... | collective-permute-start | bytes 417800 | tf_op jit(solution)/shard_map/ppermute | solution.py:25
  57.4 6.2 %collective-permute-start.14 = (f32[128,256]{1,0:T(8,128)S(1)}, f32[128,256]{1,0:T(8,128)S(1)}, u32[]{:S(2)}, u32[]{:S(2)}) collective-permute-start(f32[128,256]{1,0:T(8,128)S(1)} %get-tuple-element.48), channel_id=1, source_target_pairs={{0,16},{8,24},{16,0},{24,8},{1,17},{9,25},{17,1},{25,9},{2,18},{10... | collective-permute-start | bytes 393224 | tf_op jit(solution)/shard_map/ppermute | solution.py:25
  61.4 7.3 %collective-permute-start.13 = (f32[136,256]{1,0:T(8,128)S(1)}, f32[136,256]{1,0:T(8,128)S(1)}, u32[]{:S(2)}, u32[]{:S(2)}) collective-permute-start(f32[136,256]{1,0:T(8,128)S(1)} %add.50), channel_id=1, source_target_pairs={{0,16},{8,24},{16,0},{24,8},{1,17},{9,25},{17,1},{25,9},{2,18},{10... | collective-permute-start | bytes 417800 | tf_op jit(solution)/shard_map/ppermute | solution.py:25
  63.6 5.0 %collective-permute-start.15 = (f32[128,256]{1,0:T(8,128)S(1)}, f32[128,256]{1,0:T(8,128)S(1)}, u32[]{:S(2)}, u32[]{:S(2)}) collective-permute-start(f32[128,256]{1,0:T(8,128)S(1)} %add.52), channel_id=1, source_target_pairs={{0,8},{8,0},{16,24},{24,16},{1,9},{9,1},{17,25},{25,17},{2,10},{10... | collective-permute-start | bytes 393224 | tf_op jit(solution)/shard_map/ppermute | solution.py:25
  64.0 11.3 %collective-permute-start.18 = (f32[512,256]{1,0:T(8,128)S(1)}, f32[512,256]{1,0:T(8,128)S(1)}, u32[]{:S(2)}, u32[]{:S(2)}) collective-permute-start(f32[512,256]{1,0:T(8,128)S(1)} %get-tuple-element.58.refs_1_), channel_id=1, source_target_pairs={{7,0},{0,1},{1,2},{2,3},{3,4},{4,5},{5,6},{6,7},{15,8},{8,9},{9,10... | collective-permute-start | bytes 1572872 | tf_op jit(solution)/shard_map/ppermute | solution.py:21
  68.7 8.6 %collective-permute-start.16 = (f32[264,256]{1,0:T(8,128)S(1)}, f32[264,256]{1,0:T(8,128)S(1)}, u32[]{:S(2)}, u32[]{:S(2)}) collective-permute-start(f32[264,256]{1,0:T(8,128)S(1)} %pad_maximum_fusion.2.pack_ref), channel_id=1, source_target_pairs={{7,0},{0,1},{1,2},{2,3},{3,4},{4,5},{5,6},{6,7},{15,8},{8,9},{9,10... | collective-permute-start | bytes 811016 | tf_op jit(solution)/shard_map/ppermute | solution.py:21
  70.3 19.6 %collective-permute-start.19 = (f32[512,256]{1,0:T(8,128)S(1)}, f32[512,256]{1,0:T(8,128)S(1)}, u32[]{:S(2)}, u32[]{:S(2)}) collective-permute-start(f32[512,256]{1,0:T(8,128)S(1)} %get-tuple-element.67), channel_id=1, source_target_pairs={{7,0},{0,1},{1,2},{2,3},{3,4},{4,5},{5,6},{6,7},{15,8},{8,9},{9,10... | collective-permute-start | bytes 1572872 | tf_op jit(solution)/shard_map/ppermute | solution.py:21
  70.3 19.5 %collective-permute-start.20 = (f32[512,256]{1,0:T(8,128)S(1)}, f32[512,256]{1,0:T(8,128)S(1)}, u32[]{:S(2)}, u32[]{:S(2)}) collective-permute-start(f32[512,256]{1,0:T(8,128)S(1)} %get-tuple-element.66.d1), channel_id=1, source_target_pairs={{0,1},{2,3},{4,5},{6,7},{8,9},{10,11},{12,13},{14,15},{16,17},{18,... | collective-permute-start | bytes 1572872 | tf_op jit(solution)/shard_map/ppermute | solution.py:269
  81.8 3.7 %collective-permute-start.21 = (f32[8,512]{1,0:T(8,128)S(1)}, f32[8,512]{1,0:T(8,128)S(1)}, u32[]{:S(2)}, u32[]{:S(2)}) collective-permute-start(f32[8,512]{1,0:T(8,128)S(1)} %get-tuple-element.70), channel_id=1, source_target_pairs={{0,8},{8,0},{16,24},{24,16},{1,9},{9,1},{17,25},{25,17},{2,10},{10... | collective-permute-start | bytes 49160 | tf_op jit(solution)/shard_map/ppermute | solution.py:25
  85.5 3.7 %collective-permute-start.22 = (f32[8,512]{1,0:T(8,128)S(1)}, f32[8,512]{1,0:T(8,128)S(1)}, u32[]{:S(2)}, u32[]{:S(2)}) collective-permute-start(f32[8,512]{1,0:T(8,128)S(1)} %add.54), channel_id=1, source_target_pairs={{0,16},{8,24},{16,0},{24,8},{1,17},{9,25},{17,1},{25,9},{2,18},{10... | collective-permute-start | bytes 49160 | tf_op jit(solution)/shard_map/ppermute | solution.py:25

commit v2 on v1

--- a/solution.py
+++ b/solution.py
@@ -8,11 +8,11 @@
 from jax.experimental.pallas import tpu as pltpu
 from jax.sharding import PartitionSpec as P
 
+
 ROUNDS = 3
 POLAR_STEPS = 3
 TAIL = 8
 VMEM = pl.BlockSpec(memory_space=pltpu.VMEM)
-SMEM = pl.BlockSpec(memory_space=pltpu.SMEM)
 PARAMS = pltpu.CompilerParams(vmem_limit_bytes=24 << 20)
 
 
@@ -21,11 +21,11 @@
     return lax.ppermute(block, axis, [((i - distance) % count, i) for i in range(count)])
 
 
-def exchange(block, axis, bit):
-    return lax.ppermute(block, axis, [(i, i ^ bit) for i in range(lax.axis_size(axis))])
-
-
-def sum_rows(top, bottom):
+def exchange(block, axis, mask):
+    return lax.ppermute(block, axis, [(i, i ^ mask) for i in range(lax.axis_size(axis))])
+
+
+def sum_rows(top, bottom, flag):
     count = lax.axis_size("row")
     bits = [1 << k for k in range(count.bit_length() - 1)]
     assert 1 << len(bits) == count
@@ -33,6 +33,8 @@
         top_in = exchange(top, "row", bits[k])
         bottom_in = exchange(bottom, "row", bits[(k + 1) % len(bits)])
         top, bottom = top + top_in, bottom + bottom_in
+    row = lax.broadcasted_iota(jnp.int32, top.shape, 0)
+    top = jnp.where(row == top.shape[0] - TAIL + 2, flag.astype(jnp.float32), top)
     return jnp.concatenate([top, bottom], axis=0)
 
 
@@ -90,7 +92,6 @@
 
 
 def times(parts, matrix_refs):
-    half = parts[0].shape[0]
     if len(matrix_refs) == 1:
         whole = cut(jnp.concatenate(parts, axis=0))
         return dot(cut(matrix_refs[0][...]), whole)
@@ -99,7 +100,7 @@
     )
 
 
-def store_gram(left, right, flag, top_ref, bottom_ref):
+def store_gram(left, right, top_ref, bottom_ref):
     cut_row = top_ref.shape[0] - TAIL
     cross = dot(cut(left), cut(right), (((0,), (0,)), ((), ())))
     top_ref[:cut_row] = cross[:cut_row]
@@ -107,7 +108,6 @@
     top_ref[cut_row:] = jnp.zeros((TAIL, cross.shape[1]), jnp.float32)
     top_ref[cut_row : cut_row + 1] = jnp.sum(left * left, axis=0, keepdims=True)
     top_ref[cut_row + 1 : cut_row + 2] = jnp.sum(right * right, axis=0, keepdims=True)
-    top_ref[cut_row + 2 : cut_row + 3] = jnp.full((1, cross.shape[1]), flag, jnp.float32)
 
 
 def f32(*shape):
@@ -122,10 +122,9 @@
     return pl.CostEstimate(flops=int(flops), bytes_accessed=1 << 20, transcendentals=0)
 
 
-def call(kernel, name, outs, specs, operands, flops, **extra):
+def call(kernel, outs, specs, operands, flops, **extra):
     return pl.pallas_call(
         kernel,
-        name=name,
         out_shape=outs,
         in_specs=specs,
         out_specs=[VMEM] * len(outs),
@@ -135,10 +134,9 @@
     )(*operands)
 
 
-def gram_kernel(matrix_ref, plan_ref, top_ref, bottom_ref):
+def gram_kernel(matrix_ref, top_ref, bottom_ref):
     half = matrix_ref.shape[1] // 2
-    flag = plan_ref[0, 0].astype(jnp.float32)
-    store_gram(matrix_ref[:, :half], matrix_ref[:, half:], flag, top_ref, bottom_ref)
+    store_gram(matrix_ref[:, :half], matrix_ref[:, half:], top_ref, bottom_ref)
 
 
 def own_kernel(count, pack_ref, *refs):
@@ -149,29 +147,27 @@
     panel_ref[...] = times(staying, matrix_refs)
 
 
-def next_kernel(round_index, count, pack_ref, plan_ref, panel_ref, *refs):
+def next_kernel(count, pack_ref, panel_ref, *refs):
     matrix_refs, outs = refs[:count], refs[count:]
     staying_ref, moving_ref, arrived_ref, top_ref, bottom_ref = outs
     half = pack_ref.shape[1]
     staying, moving = rotation_halves(pack_ref)
     arrived = times(moving, matrix_refs)
     arrived_ref[...] = arrived
-    flag = plan_ref[round_index, 0].astype(jnp.float32)
-    store_gram(panel_ref[...], arrived, flag, top_ref, bottom_ref)
+    store_gram(panel_ref[...], arrived, top_ref, bottom_ref)
     staying_ref[:half], staying_ref[half:] = staying
     moving_ref[:half], moving_ref[half:] = moving
 
 
 def last_kernel(count, pack_ref, panel_ref, *refs):
-    matrix_refs, (moving_ref, matrix_ref, sums_ref) = refs[:count], refs[count:]
+    matrix_refs, (moving_ref, arrived_ref, sums_ref) = refs[:count], refs[count:]
     half = pack_ref.shape[1]
     _, moving = rotation_halves(pack_ref)
     panel = panel_ref[...]
     arrived = times(moving, matrix_refs)
     sums_ref[:, :half] = jnp.broadcast_to(jnp.sum(panel * panel, axis=0), (8, half))
     sums_ref[:, half:] = jnp.broadcast_to(jnp.sum(arrived * arrived, axis=0), (8, half))
-    matrix_ref[:, :half] = panel
-    matrix_ref[:, half:] = arrived
+    arrived_ref[...] = arrived
     moving_ref[:half], moving_ref[half:] = moving
 
 
@@ -203,13 +199,15 @@
     b1[...] = dot(far, bottom(s21))
 
 
-def vectors_kernel(rows_each, a0, b0, a1, b1, c1, d1, x1, x2, s3, m3, out):
+def finish_kernel(rows_each, a0, b0, a1, b1, c1, d1, x1, x2, s3, m3, still, arrived, matrix, out):
     half = s3.shape[1]
     pairs = lax.axis_size("col")
     pair = lax.axis_index("col")
     block = lax.axis_index("row") * rows_each + pl.program_id(0)
     behind = lax.rem(pair - block + pairs, pairs)
     zeros = jnp.zeros((out.shape[0], half), jnp.float32)
+    matrix[:, :half] = still[...]
+    matrix[:, half:] = arrived[...]
     top = lambda ref: cut(ref[:half])
     bottom = lambda ref: cut(ref[half:])
     whole = lambda ref: cut(ref[...])
@@ -252,88 +250,81 @@
     cube = 6 * half**3
     turn_flops = 15 * cube + 6 * rows * width * half
 
-    top, bottom = call(
-        gram_kernel, "gram", gram_shapes(half), [VMEM, SMEM], (activations, plan), 2 * cube
-    )
-    own, near = (activations,), (from_behind(activations, "col", 1),)
+    top, bottom = call(gram_kernel, gram_shapes(half), [VMEM], (activations,), 2 * cube)
+    near = (from_behind(activations, "col", 1),)
+    own = (activations,)
     kept, sent, kept_near = [], [], []
     for round_index in range(ROUNDS):
-        last = round_index + 1 == ROUNDS
-        pack = sum_rows(top, bottom)
+        pack = sum_rows(top, bottom, plan[round_index, 0])
         pack_near = from_behind(pack, "col", 1)
-        if round_index == 1:
-            pack, far_turn = lax.optimization_barrier((pack, sent[0]))
-            far_turn = from_behind(far_turn, "col", 1)
-        if last:
-            pack, c1, d1, x1 = lax.optimization_barrier((pack, c1, d1, x1))
-            x2 = lax.ppermute(
-                d1,
-                "col",
-                [(i, (i + 1) % pairs) for i in range(pairs) if (i - 1) % pairs % rows_each],
-            )
-            x1 = from_behind(x1, "col", 1)
         staying, still = call(
             functools.partial(own_kernel, len(own)),
-            "own",
             [turn, panel],
             [VMEM] * (1 + len(own)),
             (pack, *own),
             turn_flops,
         )
         kept.append(staying)
-        if last:
-            moving, matrix, sums = call(
-                functools.partial(last_kernel, len(near)),
-                "last",
-                [turn, f32(rows, width), f32(8, width)],
-                [VMEM] * (2 + len(near)),
-                (pack_near, still, *near),
-                turn_flops,
-            )
-            sent.append(moving)
+        if round_index + 1 == ROUNDS:
             break
         staying_near, moving, arrived, top, bottom = call(
-            functools.partial(next_kernel, round_index + 1, len(near)),
-            "next",
+            functools.partial(next_kernel, len(near)),
             [turn, turn, panel] + gram_shapes(half),
-            [VMEM, SMEM, VMEM] + [VMEM] * len(near),
-            (pack_near, plan, still, *near),
+            [VMEM] * (2 + len(near)),
+            (pack_near, still, *near),
             turn_flops,
         )
         kept_near.append(staying_near)
         sent.append(moving)
+        arrived_near = from_behind(arrived, "col", 1)
+        if round_index == 0:
+            far_turn = from_behind(moving, "col", 1)
+        else:
+            a0, b0, a1, b1, c1, d1, x1 = call(
+                functools.partial(middle_kernel, rows_each),
+                [turn] * 7,
+                [VMEM] * 7,
+                (kept[0], sent[0], kept_near[0], far_turn, kept[1], staying_near, moving),
+                12 * cube,
+            )
+            x1 = from_behind(x1, "col", 1)
+            route = [(i, (i + 1) % pairs) for i in range(pairs)]
+            x2 = lax.ppermute(d1, "col", [e for e in route if (e[0] - 1) % rows_each])
         (still_near,) = call(
             functools.partial(turn_kernel, len(near)),
-            "turn",
             [panel],
             [VMEM] * (1 + len(near)),
             (staying_near, *near),
             4 * cube,
         )
-        own, near = (still, arrived), (still_near, from_behind(arrived, "col", 1))
-        if round_index == 1:
-            a0, b0, a1, b1, c1, d1, x1 = call(
-                functools.partial(middle_kernel, rows_each),
-                "middle",
-                [turn] * 7,
-                [VMEM] * 7,
-                (kept[0], sent[0], kept_near[0], far_turn, kept[1], kept_near[1], sent[1]),
-                12 * cube,
-            )
-    bits = [1 << k for k in range(row_count.bit_length() - 1)]
-    for bit in bits:
-        sums = sums + exchange(sums, "row", bit)
-    spread = jnp.sqrt(sums[0] / (rows * row_count))
-    vectors = pl.pallas_call(
-        functools.partial(vectors_kernel, rows_each),
-        name="vectors",
+        own, near = (still, arrived), (still_near, arrived_near)
+    moving, arrived, sums = call(
+        functools.partial(last_kernel, len(near)),
+        [turn, panel, f32(8, width)],
+        [VMEM] * (2 + len(near)),
+        (pack_near, still, *near),
+        turn_flops,
+    )
+    terms = [sums]
+    for mask in range(1, row_count):
+        terms.append(exchange(sums, "row", mask))
+    matrix, vectors = pl.pallas_call(
+        functools.partial(finish_kernel, rows_each),
+        name="finish",
         grid=(rows_each,),
-        out_shape=f32(rows_each * width, width),
-        in_specs=[VMEM] * 10,
-        out_specs=pl.BlockSpec((width, width), lambda i: (i, 0)),
+        out_shape=[f32(rows, width), f32(rows_each * width, width)],
+        in_specs=[VMEM] * 10 + [pl.BlockSpec((rows // rows_each, half), lambda i: (i, 0))] * 2,
+        out_specs=[
+            pl.BlockSpec((rows // rows_each, width), lambda i: (i, 0)),
+            pl.BlockSpec((width, width), lambda i: (i, 0)),
+        ],
         compiler_params=PARAMS,
         cost_estimate=cost(8 * cube),
-    )(a0, b0, a1, b1, c1, d1, x1, x2, kept[2], sent[2])
+    )(a0, b0, a1, b1, c1, d1, x1, x2, kept[2], moving, still, arrived)
+    totals = terms[0][0]
+    for term in terms[1:]:
+        totals = totals + term[0]
+    spread = jnp.sqrt(totals / (rows * row_count))
     return (matrix, vectors, spread)
 
 

time: 91.7 us -> 95.2 us (1.038)
  waiting for transfers between devices: 34.3 us -> 37.7 us
  Pallas kernels: 29.5 us -> 27.2 us
  between operations: 0.86 us -> 2.86 us
    ppermute x8, waiting for transfers between devices: 8.67 us -> 21.6 us  [from_behind(): lax.ppermute(block, axis, [((i - distance) % count, i) for i in range(cou...]
    ppermute x15 -> x16, waiting for transfers between devices: 25.6 us -> 16.2 us  [the longest x15 16.2 us: exchange(): lax.ppermute(block, axis, [(i, i ^ mask) for i in range(lax.axis_size(axi...]
    pallas_call x11, Pallas kernels: 29.5 us -> 27.2 us  [the longest x10 25.1 us: call(): pl.pallas_call(kernel, out_shape=outs, in_specs=specs, out_specs=[VMEM] *...]
    slice x0 -> x1, local copies, waits for them, and re-layouts: none -> 1.35 us  [per_device(): pack = sum_rows(top, bottom, plan[round_index, 0])]
    unnamed x3 -> x2, local copies, waits for them, and re-layouts: 1.96 us -> 1.22 us
    ppermute x15 -> x16, starting transfers between devices: 21.9 us -> 22.2 us  [the longest x15 20.9 us: exchange(): lax.ppermute(block, axis, [(i, i ^ mask) for i in range(lax.axis_size(axi...]
  transfers between devices with their start and end apart: 23 -> 24, of which waited for: 13 -> 14; matrix products, arithmetic and copies ran while one was open for 2% -> 2% of each run, Pallas kernels for 25% -> 24%
where the time goes in v2:
time: 95.2 us; the launch traced here: 95 us
  waiting for transfers between devices  37.7 us (40%)
  Pallas kernels  27.2 us (29%)
  starting transfers between devices  23.6 us (25%)
  between operations  2.86 us (3%)
  local copies, waits for them, and re-layouts  2.58 us (3%)
  other arithmetic  1.11 us (1%)
    pallas_call x10, Pallas kernels, call(): pl.pallas_call(kernel, out_shape=outs, in_specs=specs, out_specs=[VMEM] *...  25.1 us
    ppermute x8, waiting for transfers between devices, from_behind(): lax.ppermute(block, axis, [((i - distance) % count, i) for i in range(cou...  21.6 us
    ppermute x15, starting transfers between devices, exchange(): lax.ppermute(block, axis, [(i, i ^ mask) for i in range(lax.axis_size(axi...  20.9 us
    ppermute x15, waiting for transfers between devices, exchange(): lax.ppermute(block, axis, [(i, i ^ mask) for i in range(lax.axis_size(axi...  16.2 us
    pallas_call x1, Pallas kernels, per_device(): pl.pallas_call(functools.partial(finish_kernel, rows_each), name='finish'...  2.13 us
  transfers between devices with their start and end apart: 24, of which 14 were waited for; matrix products, arithmetic and copies ran while one was open for 2% of the time, Pallas kernels for 24%

profile of v2, /device:TPU:0, one launch (start us, length us, event | category | flops | bytes accessed | tf_op | source)
XLA Modules:
  0.0 95.0 jit_solution(13371511057372139540)
XLA Ops:
  0.6 0.5 collective-permute-start.5
  1.2 1.2 %copy-done = f32[512,512]{1,0:T(8,128)S(1)} copy-done((f32[512,512]{1,0:T(8,128)S(1)}, f32[512,512]{1,0:T(8,128)}, u32[]{:S(2)}) %copy-start) | copy-done | bytes 1048600
  2.4 0.5 shard_map.49
  2.9 2.5 %collective-permute-start = (f32[136,256]{1,0:T(8,128)S(1)}, f32[136,256]{1,0:T(8,128)S(1)}, u32[]{:S(2)}, u32[]{:S(2)}) collective-permute-start(f32[136,256]{1,0:T(8,128)S(1)} %get-tuple-element.33), channel_id=1, source_target_pairs={{0,8},{8,0},{16,24},{24,16},{1,9},{9,1},{17,25},{25,17},{2,10},{10... | collective-permute-start | bytes 417800 | tf_op jit(solution)/shard_map/ppermute | solution.py:25
  5.4 1.5 %collective-permute-start.2 = (f32[128,256]{1,0:T(8,128)S(1)}, f32[128,256]{1,0:T(8,128)S(1)}, u32[]{:S(2)}, u32[]{:S(2)}) collective-permute-start(f32[128,256]{1,0:T(8,128)S(1)} %get-tuple-element.34), channel_id=1, source_target_pairs={{0,16},{8,24},{16,0},{24,8},{1,17},{9,25},{17,1},{25,9},{2,18},{10... | collective-permute-start | bytes 393224 | tf_op jit(solution)/shard_map/ppermute | solution.py:25
  6.9 4.4 %collective-permute-done.2 = f32[128,256]{1,0:T(8,128)S(1)} collective-permute-done((f32[128,256]{1,0:T(8,128)S(1)}, f32[128,256]{1,0:T(8,128)S(1)}, u32[]{:S(2)}, u32[]{:S(2)}) %collective-permute-start.2) | collective-permute-done | bytes 131104 | tf_op jit(solution)/shard_map/ppermute | solution.py:25
  11.4 0.1 collective-permute-start.3
  11.4 0.0 collective-permute-done
  11.5 2.1 %collective-permute-start.1 = (f32[136,256]{1,0:T(8,128)S(1)}, f32[136,256]{1,0:T(8,128)S(1)}, u32[]{:S(2)}, u32[]{:S(2)}) collective-permute-start(f32[136,256]{1,0:T(8,128)S(1)} %add.48), channel_id=1, source_target_pairs={{0,16},{8,24},{16,0},{24,8},{1,17},{9,25},{17,1},{25,9},{2,18},{10... | collective-permute-start | bytes 417800 | tf_op jit(solution)/shard_map/ppermute | solution.py:25
  13.6 1.4 %fusion.2 = (s32[1,1]{0,1:T(1,128)}, s32[1,1]{0,1:T(1,128)}, s32[1,1]{0,1:T(1,128)}) fusion(s32[3,1]{0,1:T(1,128)} %param.3), kind=kLoop, calls=%fused_computation.12 | loop fusion | bytes 24 | tf_op jit(solution)/shard_map/slice | solution.py:258
  15.6 1.8 %collective-permute-done.3 = f32[128,256]{1,0:T(8,128)S(1)} collective-permute-done((f32[128,256]{1,0:T(8,128)S(1)}, f32[128,256]{1,0:T(8,128)S(1)}, u32[]{:S(2)}, u32[]{:S(2)}) %collective-permute-start.3) | collective-permute-done | bytes 131104 | tf_op jit(solution)/shard_map/ppermute | solution.py:25
  17.4 0.3 collective-permute-done.1
  17.7 0.1 add_select_fusion.2
  17.8 0.1 collective-permute-start.4
  17.9 3.4 %shard_map.50 = (f32[512,256]{1,0:T(8,128)S(1)}, f32[512,256]{1,0:T(8,128)S(1)}) custom-call(f32[264,256]{1,0:T(8,128)S(1)} %pad_maximum_fusion.pack_ref, f32[512,512]{1,0:T(8,128)S(1)} %copy-done), custom_call_target="tpu_custom_call" | custom-call | flops 1912602624 | bytes 1048576 | tf_op jit(solution)/shard_map/pallas_call | solution.py:126
  21.3 4.2 %collective-permute-done.4.pack_ref = f32[264,256]{1,0:T(8,128)S(1)} collective-permute-done((f32[264,256]{1,0:T(8,128)S(1)}, f32[264,256]{1,0:T(8,128)S(1)}, u32[]{:S(2)}, u32[]{:S(2)}) %collective-permute-start.4) | collective-permute-done | bytes 270368 | tf_op jit(solution)/shard_map/ppermute | solution.py:21
  25.6 0.0 collective-permute-done.5.refs_0_
  25.6 4.2 %shard_map.51 = (f32[512,256]{1,0:T(8,128)S(1)}, f32[512,256]{1,0:T(8,128)S(1)}, f32[512,256]{1,0:T(8,128)S(1)}, f32[136,256]{1,0:T(8,128)S(1)}, f32[128,256]{1,0:T(8,128)S(1)}) custom-call(f32[264,256]{1,0:T(8,128)S(1)} %collective-permute-done.4.pack_ref, f32[512,256]{1,0:T(8,128)S(1)} %get-tuple-element.36.panel_ref.refs_0_, ...), custom_call_target="tpu_custom_call" | custom-call | flops 1912602624 | bytes 1048576 | tf_op jit(solution)/shard_map/pallas_call | solution.py:126
  29.8 1.8 %collective-permute-start.7 = (f32[136,256]{1,0:T(8,128)S(1)}, f32[136,256]{1,0:T(8,128)S(1)}, u32[]{:S(2)}, u32[]{:S(2)}) collective-permute-start(f32[136,256]{1,0:T(8,128)S(1)} %get-tuple-element.39), channel_id=1, source_target_pairs={{0,8},{8,0},{16,24},{24,16},{1,9},{9,1},{17,25},{25,17},{2,10},{10... | collective-permute-start | bytes 417800 | tf_op jit(solution)/shard_map/ppermute | solution.py:25
  31.5 1.5 %collective-permute-start.9 = (f32[128,256]{1,0:T(8,128)S(1)}, f32[128,256]{1,0:T(8,128)S(1)}, u32[]{:S(2)}, u32[]{:S(2)}) collective-permute-start(f32[128,256]{1,0:T(8,128)S(1)} %get-tuple-element.40), channel_id=1, source_target_pairs={{0,16},{8,24},{16,0},{24,8},{1,17},{9,25},{17,1},{25,9},{2,18},{10... | collective-permute-start | bytes 393224 | tf_op jit(solution)/shard_map/ppermute | solution.py:25
  33.1 1.8 %collective-permute-done.7 = f32[136,256]{1,0:T(8,128)S(1)} collective-permute-done((f32[136,256]{1,0:T(8,128)S(1)}, f32[136,256]{1,0:T(8,128)S(1)}, u32[]{:S(2)}, u32[]{:S(2)}) %collective-permute-start.7) | collective-permute-done | bytes 139296 | tf_op jit(solution)/shard_map/ppermute | solution.py:25
  34.9 1.8 %collective-permute-start.8 = (f32[136,256]{1,0:T(8,128)S(1)}, f32[136,256]{1,0:T(8,128)S(1)}, u32[]{:S(2)}, u32[]{:S(2)}) collective-permute-start(f32[136,256]{1,0:T(8,128)S(1)} %add.52), channel_id=1, source_target_pairs={{0,16},{8,24},{16,0},{24,8},{1,17},{9,25},{17,1},{25,9},{2,18},{10... | collective-permute-start | bytes 417800 | tf_op jit(solution)/shard_map/ppermute | solution.py:25
  36.7 0.3 collective-permute-done.9
  37.0 2.0 %collective-permute-start.10 = (f32[128,256]{1,0:T(8,128)S(1)}, f32[128,256]{1,0:T(8,128)S(1)}, u32[]{:S(2)}, u32[]{:S(2)}) collective-permute-start(f32[128,256]{1,0:T(8,128)S(1)} %add.54), channel_id=1, source_target_pairs={{0,8},{8,0},{16,24},{24,16},{1,9},{9,1},{17,25},{25,17},{2,10},{10... | collective-permute-start | bytes 393224 | tf_op jit(solution)/shard_map/ppermute | solution.py:25
  39.6 0.1 collective-permute-start.12
  39.7 2.3 %collective-permute-done.10 = f32[128,256]{1,0:T(8,128)S(1)} collective-permute-done((f32[128,256]{1,0:T(8,128)S(1)}, f32[128,256]{1,0:T(8,128)S(1)}, u32[]{:S(2)}, u32[]{:S(2)}) %collective-permute-start.10) | collective-permute-done | bytes 131104 | tf_op jit(solution)/shard_map/ppermute | solution.py:25
  42.1 0.0 collective-permute-done.8
  42.1 0.1 add_select_fusion.1
  42.2 0.1 collective-permute-start.11
  42.3 0.2 collective-permute-start.6
  42.5 0.6 shard_map.53.refs_0_
  43.1 3.4 %shard_map.52 = (f32[512,256]{1,0:T(8,128)S(1)}, f32[512,256]{1,0:T(8,128)S(1)}) custom-call(f32[264,256]{1,0:T(8,128)S(1)} %pad_maximum_fusion.1.pack_ref, f32[512,256]{1,0:T(8,128)S(1)} %get-tuple-element.36.panel_ref.refs_0_, f32[512,256]{1,0:T(8,128)S(1)} %get-tuple-element.41.refs_1_), custom_call_target="tpu_custom_call" | custom-call | flops 1912602624 | bytes 1048576 | tf_op jit(solution)/shard_map/pallas_call | solution.py:126
  46.5 3.5 %collective-permute-done.12.refs_1_ = f32[512,256]{1,0:T(8,128)S(1)} collective-permute-done((f32[512,256]{1,0:T(8,128)S(1)}, f32[512,256]{1,0:T(8,128)S(1)}, u32[]{:S(2)}, u32[]{:S(2)}) %collective-permute-start.12) | collective-permute-done | bytes 524320 | tf_op jit(solution)/shard_map/ppermute | solution.py:21
  50.1 2.9 %collective-permute-done.11.pack_ref = f32[264,256]{1,0:T(8,128)S(1)} collective-permute-done((f32[264,256]{1,0:T(8,128)S(1)}, f32[264,256]{1,0:T(8,128)S(1)}, u32[]{:S(2)}, u32[]{:S(2)}) %collective-permute-start.11) | collective-permute-done | bytes 270368 | tf_op jit(solution)/shard_map/ppermute | solution.py:21
  53.0 4.1 %shard_map.54 = (f32[512,256]{1,0:T(8,128)S(1)}, f32[512,256]{1,0:T(8,128)S(1)}, f32[512,256]{1,0:T(8,128)S(1)}, f32[136,256]{1,0:T(8,128)S(1)}, f32[128,256]{1,0:T(8,128)S(1)}) custom-call(f32[264,256]{1,0:T(8,128)S(1)} %collective-permute-done.11.pack_ref, f32[512,256]{1,0:T(8,128)S(1)} %get-tuple-element.43.panel_ref.refs_0_, ...), custom_call_target="tpu_custom_call" | custom-call | flops 1912602624 | bytes 1048576 | tf_op jit(solution)/shard_map/pallas_call | solution.py:126
  57.1 0.2 collective-permute-start.15
  57.3 1.5 %collective-permute-start.17 = (f32[128,256]{1,0:T(8,128)S(1)}, f32[128,256]{1,0:T(8,128)S(1)}, u32[]{:S(2)}, u32[]{:S(2)}) collective-permute-start(f32[128,256]{1,0:T(8,128)S(1)} %get-tuple-element.54), channel_id=1, source_target_pairs={{0,16},{8,24},{16,0},{24,8},{1,17},{9,25},{17,1},{25,9},{2,18},{10... | collective-permute-start | bytes 393224 | tf_op jit(solution)/shard_map/ppermute | solution.py:25
  58.8 3.6 %collective-permute-done.15 = f32[136,256]{1,0:T(8,128)S(1)} collective-permute-done((f32[136,256]{1,0:T(8,128)S(1)}, f32[136,256]{1,0:T(8,128)S(1)}, u32[]{:S(2)}, u32[]{:S(2)}) %collective-permute-start.15) | collective-permute-done | bytes 139296 | tf_op jit(solution)/shard_map/ppermute | solution.py:25
  62.5 1.6 %collective-permute-start.16 = (f32[136,256]{1,0:T(8,128)S(1)}, f32[136,256]{1,0:T(8,128)S(1)}, u32[]{:S(2)}, u32[]{:S(2)}) collective-permute-start(f32[136,256]{1,0:T(8,128)S(1)} %add.56), channel_id=1, source_target_pairs={{0,16},{8,24},{16,0},{24,8},{1,17},{9,25},{17,1},{25,9},{2,18},{10... | collective-permute-start | bytes 417800 | tf_op jit(solution)/shard_map/ppermute | solution.py:25
  64.0 0.0 collective-permute-done.17
  64.1 0.7 collective-permute-start.18
  65.5 0.1 collective-permute-start.20
  65.5 0.0 collective-permute-done.6.m12
  65.5 1.4 %shard_map.55 = (f32[512,256]{1,0:T(8,128)S(1)}, f32[512,256]{1,0:T(8,128)S(1)}, f32[512,256]{1,0:T(8,128)S(1)}, f32[512,256]{1,0:T(8,128)S(1)}, f32[512,256]{1,...) custom-call(f32[512,256]{1,0:T(8,128)S(1)} %get-tuple-element.35.s10, ...), custom_call_target="tpu_custom_call" | custom-call | flops 1207959552 | bytes 1048576 | tf_op jit(solution)/shard_map/pallas_call | solution.py:126
  67.0 0.1 collective-permute-start.13
  67.0 1.3 %collective-permute-start.14 = (f32[512,256]{1,0:T(8,128)S(1)}, f32[512,256]{1,0:T(8,128)S(1)}, u32[]{:S(2)}, u32[]{:S(2)}) collective-permute-start(f32[512,256]{1,0:T(8,128)S(1)} %get-tuple-element.51.d1), channel_id=1, source_target_pairs={{0,1},{2,3},{4,5},{6,7},{8,9},{10,11},{12,13},{14,15},{16,17},{18,... | collective-permute-start | bytes 1572872 | tf_op jit(solution)/shard_map/ppermute | solution.py:292
  68.4 0.7 collective-permute-done.18
  69.1 0.0 collective-permute-done.16
  69.1 0.1 add_select_fusion
  69.3 0.3 collective-permute-start.19
  69.5 0.6 shard_map.57.refs_0_
  70.1 3.4 %shard_map.56 = (f32[512,256]{1,0:T(8,128)S(1)}, f32[512,256]{1,0:T(8,128)S(1)}) custom-call(f32[264,256]{1,0:T(8,128)S(1)} %pad_maximum_fusion.2.pack_ref, f32[512,256]{1,0:T(8,128)S(1)} %get-tuple-element.43.panel_ref.refs_0_, f32[512,256]{1,0:T(8,128)S(1)} %get-tuple-element.55.refs_1_), custom_call_target="tpu_custom_call" | custom-call | flops 1912602624 | bytes 1048576 | tf_op jit(solution)/shard_map/pallas_call | solution.py:126
  73.6 2.3 %collective-permute-done.20.refs_1_ = f32[512,256]{1,0:T(8,128)S(1)} collective-permute-done((f32[512,256]{1,0:T(8,128)S(1)}, f32[512,256]{1,0:T(8,128)S(1)}, u32[]{:S(2)}, u32[]{:S(2)}) %collective-permute-start.20) | collective-permute-done | bytes 524320 | tf_op jit(solution)/shard_map/ppermute | solution.py:21
  75.9 8.5 %collective-permute-done.19.pack_ref = f32[264,256]{1,0:T(8,128)S(1)} collective-permute-done((f32[264,256]{1,0:T(8,128)S(1)}, f32[264,256]{1,0:T(8,128)S(1)}, u32[]{:S(2)}, u32[]{:S(2)}) %collective-permute-start.19) | collective-permute-done | bytes 270368 | tf_op jit(solution)/shard_map/ppermute | solution.py:21
  84.4 3.4 %shard_map.58 = (f32[512,256]{1,0:T(8,128)S(1)}, f32[512,256]{1,0:T(8,128)S(1)}, f32[8,512]{1,0:T(8,128)S(1)}) custom-call(f32[264,256]{1,0:T(8,128)S(1)} %collective-permute-done.19.pack_ref, f32[512,256]{1,0:T(8,128)S(1)} %get-tuple-element.57.panel_ref.still, f32[512,256]{1,0:T(8,128)S(1)} %shard_map.57.refs_0_, ...), custom_call_target="tpu_custom_call" | custom-call | flops 1912602624 | bytes 1048576 | tf_op jit(solution)/shard_map/pallas_call | solution.py:126
  87.9 1.4 %collective-permute-start.21 = (f32[8,512]{1,0:T(8,128)S(1)}, f32[8,512]{1,0:T(8,128)S(1)}, u32[]{:S(2)}, u32[]{:S(2)}) collective-permute-start(f32[8,512]{1,0:T(8,128)S(1)} %get-tuple-element.62), channel_id=1, source_target_pairs={{0,8},{8,0},{16,24},{24,16},{1,9},{9,1},{17,25},{25,17},{2,10},{10... | collective-permute-start | bytes 49160 | tf_op jit(solution)/shard_map/ppermute | solution.py:25
  89.3 0.5 collective-permute-start.22
  89.8 1.6 %collective-permute-start.23 = (f32[8,512]{1,0:T(8,128)S(1)}, f32[8,512]{1,0:T(8,128)S(1)}, u32[]{:S(2)}, u32[]{:S(2)}) collective-permute-start(f32[8,512]{1,0:T(8,128)S(1)} %get-tuple-element.62), channel_id=1, source_target_pairs={{0,24},{8,16},{16,8},{24,0},{1,25},{9,17},{17,9},{25,1},{2,26},{10... | collective-permute-start | bytes 49160 | tf_op jit(solution)/shard_map/ppermute | solution.py:25
  91.4 0.0 collective-permute-done.13.x1
  91.4 0.0 collective-permute-done.14.x2
  91.4 2.1 %finish.1 = (f32[512,512]{1,0:T(8,128)}, f32[1024,512]{1,0:T(8,128)}) custom-call(f32[512,256]{1,0:T(8,128)S(1)} %get-tuple-element.46.a0, f32[512,256]{1,0:T(8,128)S(1)} %get-tuple-element.47.b0, f32[512,256]{1,0:T(8,128)S(1)} %get-tuple-element.48.a1, f32[512,256]{1,0:T(8,128)S(1)} %get-tuple-element.49.b1, f32[512,256]{1,0:T(8,128)S(1)} %get-tuple-element.50.c1, ...), custom_call_target="tpu_custom_call" | custom-call | flops 805306368 | bytes 1048576 | tf_op jit(solution)/shard_map/finish/pallas_call | solution.py:311
  93.6 0.0 collective-permute-done.21
  93.6 0.9 collective-permute-done.23
  94.4 0.6 fusion.1
  (15 shorter events, 0.2 us)
Async XLA Ops:
  0.6 24.9 %collective-permute-start.5 = (f32[512,512]{1,0:T(8,128)}, f32[512,512]{1,0:T(8,128)S(1)}, u32[]{:S(2)}, u32[]{:S(2)}) collective-permute-start(f32[512,512]{1,0:T(8,128)} %refs_0_.1), channel_id=1, source_target_pairs={{7,0},{0,1},{1,2},{2,3},{3,4},{4,5},{5,6},{6,7},{15,8},{8,9},{9,10... | collective-permute-start | bytes 3145736 | tf_op jit(solution)/shard_map/ppermute | solution.py:21
  1.2 1.2 %copy-start = (f32[512,512]{1,0:T(8,128)S(1)}, f32[512,512]{1,0:T(8,128)}, u32[]{:S(2)}) copy-start(f32[512,512]{1,0:T(8,128)} %refs_0_.1) | copy-start | bytes 3145732
  2.9 8.6 %collective-permute-start = (f32[136,256]{1,0:T(8,128)S(1)}, f32[136,256]{1,0:T(8,128)S(1)}, u32[]{:S(2)}, u32[]{:S(2)}) collective-permute-start(f32[136,256]{1,0:T(8,128)S(1)} %get-tuple-element.33), channel_id=1, source_target_pairs={{0,8},{8,0},{16,24},{24,16},{1,9},{9,1},{17,25},{25,17},{2,10},{10... | collective-permute-start | bytes 417800 | tf_op jit(solution)/shard_map/ppermute | solution.py:25
  5.4 5.9 %collective-permute-start.2 = (f32[128,256]{1,0:T(8,128)S(1)}, f32[128,256]{1,0:T(8,128)S(1)}, u32[]{:S(2)}, u32[]{:S(2)}) collective-permute-start(f32[128,256]{1,0:T(8,128)S(1)} %get-tuple-element.34), channel_id=1, source_target_pairs={{0,16},{8,24},{16,0},{24,8},{1,17},{9,25},{17,1},{25,9},{2,18},{10... | collective-permute-start | bytes 393224 | tf_op jit(solution)/shard_map/ppermute | solution.py:25
  11.4 6.0 %collective-permute-start.3 = (f32[128,256]{1,0:T(8,128)S(1)}, f32[128,256]{1,0:T(8,128)S(1)}, u32[]{:S(2)}, u32[]{:S(2)}) collective-permute-start(f32[128,256]{1,0:T(8,128)S(1)} %add.50), channel_id=1, source_target_pairs={{0,8},{8,0},{16,24},{24,16},{1,9},{9,1},{17,25},{25,17},{2,10},{10... | collective-permute-start | bytes 393224 | tf_op jit(solution)/shard_map/ppermute | solution.py:25
  11.5 6.2 %collective-permute-start.1 = (f32[136,256]{1,0:T(8,128)S(1)}, f32[136,256]{1,0:T(8,128)S(1)}, u32[]{:S(2)}, u32[]{:S(2)}) collective-permute-start(f32[136,256]{1,0:T(8,128)S(1)} %add.48), channel_id=1, source_target_pairs={{0,16},{8,24},{16,0},{24,8},{1,17},{9,25},{17,1},{25,9},{2,18},{10... | collective-permute-start | bytes 417800 | tf_op jit(solution)/shard_map/ppermute | solution.py:25
  17.8 7.7 %collective-permute-start.4 = (f32[264,256]{1,0:T(8,128)S(1)}, f32[264,256]{1,0:T(8,128)S(1)}, u32[]{:S(2)}, u32[]{:S(2)}) collective-permute-start(f32[264,256]{1,0:T(8,128)S(1)} %pad_maximum_fusion.pack_ref), channel_id=1, source_target_pairs={{7,0},{0,1},{1,2},{2,3},{3,4},{4,5},{5,6},{6,7},{15,8},{8,9},{9,10... | collective-permute-start | bytes 811016 | tf_op jit(solution)/shard_map/ppermute | solution.py:21
  29.8 5.1 %collective-permute-start.7 = (f32[136,256]{1,0:T(8,128)S(1)}, f32[136,256]{1,0:T(8,128)S(1)}, u32[]{:S(2)}, u32[]{:S(2)}) collective-permute-start(f32[136,256]{1,0:T(8,128)S(1)} %get-tuple-element.39), channel_id=1, source_target_pairs={{0,8},{8,0},{16,24},{24,16},{1,9},{9,1},{17,25},{25,17},{2,10},{10... | collective-permute-start | bytes 417800 | tf_op jit(solution)/shard_map/ppermute | solution.py:25
  31.5 5.5 %collective-permute-start.9 = (f32[128,256]{1,0:T(8,128)S(1)}, f32[128,256]{1,0:T(8,128)S(1)}, u32[]{:S(2)}, u32[]{:S(2)}) collective-permute-start(f32[128,256]{1,0:T(8,128)S(1)} %get-tuple-element.40), channel_id=1, source_target_pairs={{0,16},{8,24},{16,0},{24,8},{1,17},{9,25},{17,1},{25,9},{2,18},{10... | collective-permute-start | bytes 393224 | tf_op jit(solution)/shard_map/ppermute | solution.py:25
  34.9 7.2 %collective-permute-start.8 = (f32[136,256]{1,0:T(8,128)S(1)}, f32[136,256]{1,0:T(8,128)S(1)}, u32[]{:S(2)}, u32[]{:S(2)}) collective-permute-start(f32[136,256]{1,0:T(8,128)S(1)} %add.52), channel_id=1, source_target_pairs={{0,16},{8,24},{16,0},{24,8},{1,17},{9,25},{17,1},{25,9},{2,18},{10... | collective-permute-start | bytes 417800 | tf_op jit(solution)/shard_map/ppermute | solution.py:25
  37.0 5.0 %collective-permute-start.10 = (f32[128,256]{1,0:T(8,128)S(1)}, f32[128,256]{1,0:T(8,128)S(1)}, u32[]{:S(2)}, u32[]{:S(2)}) collective-permute-start(f32[128,256]{1,0:T(8,128)S(1)} %add.54), channel_id=1, source_target_pairs={{0,8},{8,0},{16,24},{24,16},{1,9},{9,1},{17,25},{25,17},{2,10},{10... | collective-permute-start | bytes 393224 | tf_op jit(solution)/shard_map/ppermute | solution.py:25
  39.6 10.5 %collective-permute-start.12 = (f32[512,256]{1,0:T(8,128)S(1)}, f32[512,256]{1,0:T(8,128)S(1)}, u32[]{:S(2)}, u32[]{:S(2)}) collective-permute-start(f32[512,256]{1,0:T(8,128)S(1)} %get-tuple-element.41.refs_1_), channel_id=1, source_target_pairs={{7,0},{0,1},{1,2},{2,3},{3,4},{4,5},{5,6},{6,7},{15,8},{8,9},{9,10... | collective-permute-start | bytes 1572872 | tf_op jit(solution)/shard_map/ppermute | solution.py:21
  42.2 10.8 %collective-permute-start.11 = (f32[264,256]{1,0:T(8,128)S(1)}, f32[264,256]{1,0:T(8,128)S(1)}, u32[]{:S(2)}, u32[]{:S(2)}) collective-permute-start(f32[264,256]{1,0:T(8,128)S(1)} %pad_maximum_fusion.1.pack_ref), channel_id=1, source_target_pairs={{7,0},{0,1},{1,2},{2,3},{3,4},{4,5},{5,6},{6,7},{15,8},{8,9},{9,10... | collective-permute-start | bytes 811016 | tf_op jit(solution)/shard_map/ppermute | solution.py:21
  42.3 23.3 %collective-permute-start.6 = (f32[512,256]{1,0:T(8,128)S(1)}, f32[512,256]{1,0:T(8,128)S(1)}, u32[]{:S(2)}, u32[]{:S(2)}) collective-permute-start(f32[512,256]{1,0:T(8,128)S(1)} %get-tuple-element.37.m11), channel_id=1, source_target_pairs={{7,0},{0,1},{1,2},{2,3},{3,4},{4,5},{5,6},{6,7},{15,8},{8,9},{9,10... | collective-permute-start | bytes 1572872 | tf_op jit(solution)/shard_map/ppermute | solution.py:21
  57.1 5.3 %collective-permute-start.15 = (f32[136,256]{1,0:T(8,128)S(1)}, f32[136,256]{1,0:T(8,128)S(1)}, u32[]{:S(2)}, u32[]{:S(2)}) collective-permute-start(f32[136,256]{1,0:T(8,128)S(1)} %get-tuple-element.53), channel_id=1, source_target_pairs={{0,8},{8,0},{16,24},{24,16},{1,9},{9,1},{17,25},{25,17},{2,10},{10... | collective-permute-start | bytes 417800 | tf_op jit(solution)/shard_map/ppermute | solution.py:25
  57.3 6.8 %collective-permute-start.17 = (f32[128,256]{1,0:T(8,128)S(1)}, f32[128,256]{1,0:T(8,128)S(1)}, u32[]{:S(2)}, u32[]{:S(2)}) collective-permute-start(f32[128,256]{1,0:T(8,128)S(1)} %get-tuple-element.54), channel_id=1, source_target_pairs={{0,16},{8,24},{16,0},{24,8},{1,17},{9,25},{17,1},{25,9},{2,18},{10... | collective-permute-start | bytes 393224 | tf_op jit(solution)/shard_map/ppermute | solution.py:25
  62.5 6.7 %collective-permute-start.16 = (f32[136,256]{1,0:T(8,128)S(1)}, f32[136,256]{1,0:T(8,128)S(1)}, u32[]{:S(2)}, u32[]{:S(2)}) collective-permute-start(f32[136,256]{1,0:T(8,128)S(1)} %add.56), channel_id=1, source_target_pairs={{0,16},{8,24},{16,0},{24,8},{1,17},{9,25},{17,1},{25,9},{2,18},{10... | collective-permute-start | bytes 417800 | tf_op jit(solution)/shard_map/ppermute | solution.py:25
  64.1 5.0 %collective-permute-start.18 = (f32[128,256]{1,0:T(8,128)S(1)}, f32[128,256]{1,0:T(8,128)S(1)}, u32[]{:S(2)}, u32[]{:S(2)}) collective-permute-start(f32[128,256]{1,0:T(8,128)S(1)} %add.58), channel_id=1, source_target_pairs={{0,8},{8,0},{16,24},{24,16},{1,9},{9,1},{17,25},{25,17},{2,10},{10... | collective-permute-start | bytes 393224 | tf_op jit(solution)/shard_map/ppermute | solution.py:25
  65.5 10.5 %collective-permute-start.20 = (f32[512,256]{1,0:T(8,128)S(1)}, f32[512,256]{1,0:T(8,128)S(1)}, u32[]{:S(2)}, u32[]{:S(2)}) collective-permute-start(f32[512,256]{1,0:T(8,128)S(1)} %get-tuple-element.55.refs_1_), channel_id=1, source_target_pairs={{7,0},{0,1},{1,2},{2,3},{3,4},{4,5},{5,6},{6,7},{15,8},{8,9},{9,10... | collective-permute-start | bytes 1572872 | tf_op jit(solution)/shard_map/ppermute | solution.py:21
  67.0 24.5 %collective-permute-start.13 = (f32[512,256]{1,0:T(8,128)S(1)}, f32[512,256]{1,0:T(8,128)S(1)}, u32[]{:S(2)}, u32[]{:S(2)}) collective-permute-start(f32[512,256]{1,0:T(8,128)S(1)} %get-tuple-element.52), channel_id=1, source_target_pairs={{7,0},{0,1},{1,2},{2,3},{3,4},{4,5},{5,6},{6,7},{15,8},{8,9},{9,10... | collective-permute-start | bytes 1572872 | tf_op jit(solution)/shard_map/ppermute | solution.py:21
  67.0 24.4 %collective-permute-start.14 = (f32[512,256]{1,0:T(8,128)S(1)}, f32[512,256]{1,0:T(8,128)S(1)}, u32[]{:S(2)}, u32[]{:S(2)}) collective-permute-start(f32[512,256]{1,0:T(8,128)S(1)} %get-tuple-element.51.d1), channel_id=1, source_target_pairs={{0,1},{2,3},{4,5},{6,7},{8,9},{10,11},{12,13},{14,15},{16,17},{18,... | collective-permute-start | bytes 1572872 | tf_op jit(solution)/shard_map/ppermute | solution.py:292
  69.3 15.2 %collective-permute-start.19 = (f32[264,256]{1,0:T(8,128)S(1)}, f32[264,256]{1,0:T(8,128)S(1)}, u32[]{:S(2)}, u32[]{:S(2)}) collective-permute-start(f32[264,256]{1,0:T(8,128)S(1)} %pad_maximum_fusion.2.pack_ref), channel_id=1, source_target_pairs={{7,0},{0,1},{1,2},{2,3},{3,4},{4,5},{5,6},{6,7},{15,8},{8,9},{9,10... | collective-permute-start | bytes 811016 | tf_op jit(solution)/shard_map/ppermute | solution.py:21
  87.9 5.7 %collective-permute-start.21 = (f32[8,512]{1,0:T(8,128)S(1)}, f32[8,512]{1,0:T(8,128)S(1)}, u32[]{:S(2)}, u32[]{:S(2)}) collective-permute-start(f32[8,512]{1,0:T(8,128)S(1)} %get-tuple-element.62), channel_id=1, source_target_pairs={{0,8},{8,0},{16,24},{24,16},{1,9},{9,1},{17,25},{25,17},{2,10},{10... | collective-permute-start | bytes 49160 | tf_op jit(solution)/shard_map/ppermute | solution.py:25
  89.3 4.3 %collective-permute-start.22 = (f32[8,512]{1,0:T(8,128)S(1)}, f32[8,512]{1,0:T(8,128)S(1)}, u32[]{:S(2)}, u32[]{:S(2)}) collective-permute-start(f32[8,512]{1,0:T(8,128)S(1)} %get-tuple-element.62), channel_id=1, source_target_pairs={{0,16},{8,24},{16,0},{24,8},{1,17},{9,25},{17,1},{25,9},{2,18},{10... | collective-permute-start | bytes 49160 | tf_op jit(solution)/shard_map/ppermute | solution.py:25
  89.8 4.6 %collective-permute-start.23 = (f32[8,512]{1,0:T(8,128)S(1)}, f32[8,512]{1,0:T(8,128)S(1)}, u32[]{:S(2)}, u32[]{:S(2)}) collective-permute-start(f32[8,512]{1,0:T(8,128)S(1)} %get-tuple-element.62), channel_id=1, source_target_pairs={{0,24},{8,16},{16,8},{24,0},{1,25},{9,17},{17,9},{25,1},{2,26},{10... | collective-permute-start | bytes 49160 | tf_op jit(solution)/shard_map/ppermute | solution.py:25

commit v3 on v2

--- a/solution.py
+++ b/solution.py
@@ -34,8 +34,8 @@
         bottom_in = exchange(bottom, "row", bits[(k + 1) % len(bits)])
         top, bottom = top + top_in, bottom + bottom_in
     row = lax.broadcasted_iota(jnp.int32, top.shape, 0)
-    top = jnp.where(row == top.shape[0] - TAIL + 2, flag.astype(jnp.float32), top)
-    return jnp.concatenate([top, bottom], axis=0)
+    top = jnp.where(row == top.shape[0] - TAIL + 2, flag, top)
+    return top, bottom
 
 
 def cut(value):
@@ -58,37 +58,43 @@
     return [float(c) for c in factor[1:]]
 
 
-def rotation_halves(pack_ref):
-    half = pack_ref.shape[1]
-    cut_row = half // 2
-    tail = pack_ref[cut_row : cut_row + TAIL]
-    cross = jnp.concatenate([pack_ref[:cut_row], pack_ref[cut_row + TAIL :]], axis=0)
+def rotation_halves(top_ref, bottom_ref, wanted):
+    half = top_ref.shape[1]
+    cut_row = top_ref.shape[0] - TAIL
+    tail = top_ref[cut_row:]
+    cross = jnp.concatenate([top_ref[:cut_row], bottom_ref[...]], axis=0)
     inverse = 1.0 / jnp.sqrt(tail + 1e-06)
     coupling = (cross * inverse.T[:, 0:1]) * inverse[1:2]
-    strength = jnp.sqrt(jnp.sum(coupling * coupling))
-    scaled = coupling * (1.0 / (1.0 + strength))
-    b, bt = cut(scaled), cut(scaled.T)
+    b, bt = cut(coupling), cut(coupling.T)
+    factor = 1.0 / (1.0 + jnp.sqrt(jnp.sum(coupling * coupling)))
     rows = lax.broadcasted_iota(jnp.int32, (half, half), 0)
     cols = lax.broadcasted_iota(jnp.int32, (half, half), 1)
     unit = (rows == cols).astype(jnp.float32)
     c = polar_series()
-    x = cut(dot(b, bt))
+    x = cut(dot(b, bt) * (factor * factor))
     x2 = cut(dot(x, x))
     xb = dot(x, b)
-    powers = [scaled, xb, dot(x2, b), dot(x2, cut(xb))]
+    powers = [coupling, xb, dot(x2, b), dot(x2, cut(xb))]
     x4 = cut(dot(x2, x2))
     x8 = cut(dot(x4, x4))
     group = lambda k: sum(c[4 * k + j] * powers[j] for j in range(4))
     high = group(2) + c[12] * dot(x4, b)
-    u = cut(group(0) + dot(x4, cut(group(1))) + dot(x8, cut(high)))
-    first = unit + dot(u, bt)
-    second = unit + dot(bt, u)
-    over = scaled + dot(x, u)
+    series = group(0) + dot(x4, cut(group(1))) + dot(x8, cut(high))
+    over = (coupling + dot(x, cut(series))) * factor
     under = -over.T
+    u = cut(series * (factor * factor))
     chosen = tail[2:3] > 0.5
-    staying = jnp.where(chosen, first, over), jnp.where(chosen, under, second)
-    moving = jnp.where(chosen, over, first), jnp.where(chosen, second, under)
-    return staying, moving
+    if wanted == "both":
+        first = unit + dot(u, bt)
+        second = unit + dot(bt, u)
+        staying = jnp.where(chosen, first, over), jnp.where(chosen, under, second)
+        moving = jnp.where(chosen, over, first), jnp.where(chosen, second, under)
+        return staying, moving
+    if wanted == "moving":
+        chosen = jnp.logical_not(chosen)
+    pick = lambda yes, no: tuple(jnp.where(chosen, y, n) for y, n in zip(yes, no))
+    block = unit + dot(pick(u, bt), pick(bt, u))
+    return jnp.where(chosen, block, over), jnp.where(chosen, under, block)
 
 
 def times(parts, matrix_refs):
@@ -139,19 +145,19 @@
     store_gram(matrix_ref[:, :half], matrix_ref[:, half:], top_ref, bottom_ref)
 
 
-def own_kernel(count, pack_ref, *refs):
+def own_kernel(count, gram_top, gram_bottom, *refs):
     matrix_refs, (staying_ref, panel_ref) = refs[:count], refs[count:]
-    half = pack_ref.shape[1]
-    staying, _ = rotation_halves(pack_ref)
+    half = gram_top.shape[1]
+    staying = rotation_halves(gram_top, gram_bottom, "staying")
     staying_ref[:half], staying_ref[half:] = staying
     panel_ref[...] = times(staying, matrix_refs)
 
 
-def next_kernel(count, pack_ref, panel_ref, *refs):
+def next_kernel(count, gram_top, gram_bottom, panel_ref, *refs):
     matrix_refs, outs = refs[:count], refs[count:]
     staying_ref, moving_ref, arrived_ref, top_ref, bottom_ref = outs
-    half = pack_ref.shape[1]
-    staying, moving = rotation_halves(pack_ref)
+    half = gram_top.shape[1]
+    staying, moving = rotation_halves(gram_top, gram_bottom, "both")
     arrived = times(moving, matrix_refs)
     arrived_ref[...] = arrived
     store_gram(panel_ref[...], arrived, top_ref, bottom_ref)
@@ -159,10 +165,10 @@
     moving_ref[:half], moving_ref[half:] = moving
 
 
-def last_kernel(count, pack_ref, panel_ref, *refs):
+def last_kernel(count, gram_top, gram_bottom, panel_ref, *refs):
     matrix_refs, (moving_ref, arrived_ref, sums_ref) = refs[:count], refs[count:]
-    half = pack_ref.shape[1]
-    _, moving = rotation_halves(pack_ref)
+    half = gram_top.shape[1]
+    moving = rotation_halves(gram_top, gram_bottom, "moving")
     panel = panel_ref[...]
     arrived = times(moving, matrix_refs)
     sums_ref[:, :half] = jnp.broadcast_to(jnp.sum(panel * panel, axis=0), (8, half))
@@ -253,15 +259,18 @@
     top, bottom = call(gram_kernel, gram_shapes(half), [VMEM], (activations,), 2 * cube)
     near = (from_behind(activations, "col", 1),)
     own = (activations,)
+    flags = [plan[round_index, 0].astype(jnp.float32) for round_index in range(ROUNDS)]
     kept, sent, kept_near = [], [], []
     for round_index in range(ROUNDS):
-        pack = sum_rows(top, bottom, plan[round_index, 0])
-        pack_near = from_behind(pack, "col", 1)
+        pack = sum_rows(top, bottom, flags[round_index])
+        top_near = from_behind(pack[0], "col", 1)
+        bottom_near = from_behind(pack[1], "col", 1)
+        pack_near = top_near, bottom_near
         staying, still = call(
             functools.partial(own_kernel, len(own)),
             [turn, panel],
-            [VMEM] * (1 + len(own)),
-            (pack, *own),
+            [VMEM] * (2 + len(own)),
+            (*pack, *own),
             turn_flops,
         )
         kept.append(staying)
@@ -270,8 +279,8 @@
         staying_near, moving, arrived, top, bottom = call(
             functools.partial(next_kernel, len(near)),
             [turn, turn, panel] + gram_shapes(half),
-            [VMEM] * (2 + len(near)),
-            (pack_near, still, *near),
+            [VMEM] * (3 + len(near)),
+            (*pack_near, still, *near),
             turn_flops,
         )
         kept_near.append(staying_near)
@@ -287,9 +296,9 @@
                 (kept[0], sent[0], kept_near[0], far_turn, kept[1], staying_near, moving),
                 12 * cube,
             )
-            x1 = from_behind(x1, "col", 1)
             route = [(i, (i + 1) % pairs) for i in range(pairs)]
             x2 = lax.ppermute(d1, "col", [e for e in route if (e[0] - 1) % rows_each])
+            x1 = from_behind(x1, "col", 1)
         (still_near,) = call(
             functools.partial(turn_kernel, len(near)),
             [panel],
@@ -301,8 +310,8 @@
     moving, arrived, sums = call(
         functools.partial(last_kernel, len(near)),
         [turn, panel, f32(8, width)],
-        [VMEM] * (2 + len(near)),
-        (pack_near, still, *near),
+        [VMEM] * (3 + len(near)),
+        (*pack_near, still, *near),
         turn_flops,
     )
     terms = [sums]

time: 95.2 us -> 95.6 us (level)
  starting transfers between devices: 23.6 us -> 24.6 us
    ppermute x8 -> x11, starting transfers between devices: 1.35 us -> 3.62 us  [from_behind(): lax.ppermute(block, axis, [((i - distance) % count, i) for i in range(cou...]
    ppermute x15, starting transfers between devices: 20.9 us -> 19.7 us  [exchange(): lax.ppermute(block, axis, [(i, i ^ mask) for i in range(lax.axis_size(axi...]
    ppermute x8 -> x11, waiting for transfers between devices: 21.6 us -> 20.6 us  [from_behind(): lax.ppermute(block, axis, [((i - distance) % count, i) for i in range(cou...]
  transfers between devices with their start and end apart: 24 -> 27, of which waited for: 14 -> 14; matrix products, arithmetic and copies ran while one was open for 2% -> 2% of each run, Pallas kernels for 24% -> 24%
where the time goes in v3:
time: 95.6 us; the launch traced here: 95.4 us
  waiting for transfers between devices  37.3 us (39%)
  Pallas kernels  27 us (28%)
  starting transfers between devices  24.6 us (26%)
  between operations  2.82 us (3%)
  local copies, waits for them, and re-layouts  2.58 us (3%)
  other arithmetic  1.04 us (1%)
    pallas_call x10, Pallas kernels, call(): pl.pallas_call(kernel, out_shape=outs, in_specs=specs, out_specs=[VMEM] *...  24.9 us
    ppermute x11, waiting for transfers between devices, from_behind(): lax.ppermute(block, axis, [((i - distance) % count, i) for i in range(cou...  20.6 us
    ppermute x15, starting transfers between devices, exchange(): lax.ppermute(block, axis, [(i, i ^ mask) for i in range(lax.axis_size(axi...  19.7 us
    ppermute x15, waiting for transfers between devices, exchange(): lax.ppermute(block, axis, [(i, i ^ mask) for i in range(lax.axis_size(axi...  16.7 us
    ppermute x11, starting transfers between devices, from_behind(): lax.ppermute(block, axis, [((i - distance) % count, i) for i in range(cou...  3.62 us
    pallas_call x1, Pallas kernels, per_device(): pl.pallas_call(functools.partial(finish_kernel, rows_each), name='finish'...  2.13 us
  transfers between devices with their start and end apart: 27, of which 14 were waited for; matrix products, arithmetic and copies ran while one was open for 2% of the time, Pallas kernels for 24%

profile of v3, /device:TPU:0, one launch (start us, length us, event | category | flops | bytes accessed | tf_op | source)
XLA Modules:
  0.0 95.4 jit_solution(3489471529719681724)
XLA Ops:
  0.6 0.5 collective-permute-start.6
  1.2 1.2 %copy-done = f32[512,512]{1,0:T(8,128)S(1)} copy-done((f32[512,512]{1,0:T(8,128)S(1)}, f32[512,512]{1,0:T(8,128)}, u32[]{:S(2)}) %copy-start) | copy-done | bytes 1048600
  2.4 0.5 shard_map.49
  2.9 2.5 %collective-permute-start = (f32[136,256]{1,0:T(8,128)S(1)}, f32[136,256]{1,0:T(8,128)S(1)}, u32[]{:S(2)}, u32[]{:S(2)}) collective-permute-start(f32[136,256]{1,0:T(8,128)S(1)} %get-tuple-element.33), channel_id=1, source_target_pairs={{0,8},{8,0},{16,24},{24,16},{1,9},{9,1},{17,25},{25,17},{2,10},{10... | collective-permute-start | bytes 417800 | tf_op jit(solution)/shard_map/ppermute | solution.py:25
  5.4 1.5 %collective-permute-start.2 = (f32[128,256]{1,0:T(8,128)S(1)}, f32[128,256]{1,0:T(8,128)S(1)}, u32[]{:S(2)}, u32[]{:S(2)}) collective-permute-start(f32[128,256]{1,0:T(8,128)S(1)} %get-tuple-element.34), channel_id=1, source_target_pairs={{0,16},{8,24},{16,0},{24,8},{1,17},{9,25},{17,1},{25,9},{2,18},{10... | collective-permute-start | bytes 393224 | tf_op jit(solution)/shard_map/ppermute | solution.py:25
  6.9 4.4 %collective-permute-done.2 = f32[128,256]{1,0:T(8,128)S(1)} collective-permute-done((f32[128,256]{1,0:T(8,128)S(1)}, f32[128,256]{1,0:T(8,128)S(1)}, u32[]{:S(2)}, u32[]{:S(2)}) %collective-permute-start.2) | collective-permute-done | bytes 131104 | tf_op jit(solution)/shard_map/ppermute | solution.py:25
  11.4 0.1 collective-permute-start.3
  11.4 0.0 collective-permute-done
  11.5 2.1 %collective-permute-start.1 = (f32[136,256]{1,0:T(8,128)S(1)}, f32[136,256]{1,0:T(8,128)S(1)}, u32[]{:S(2)}, u32[]{:S(2)}) collective-permute-start(f32[136,256]{1,0:T(8,128)S(1)} %add.48), channel_id=1, source_target_pairs={{0,16},{8,24},{16,0},{24,8},{1,17},{9,25},{17,1},{25,9},{2,18},{10... | collective-permute-start | bytes 417800 | tf_op jit(solution)/shard_map/ppermute | solution.py:25
  13.6 1.4 %fusion.2 = (s32[1,1]{0,1:T(1,128)}, s32[1,1]{0,1:T(1,128)}, s32[1,1]{0,1:T(1,128)}) fusion(s32[3,1]{0,1:T(1,128)} %param.3), kind=kLoop, calls=%fused_computation.9 | loop fusion | bytes 24 | tf_op jit(solution)/shard_map/slice | solution.py:262
  15.6 1.8 %collective-permute-done.3 = f32[128,256]{1,0:T(8,128)S(1)} collective-permute-done((f32[128,256]{1,0:T(8,128)S(1)}, f32[128,256]{1,0:T(8,128)S(1)}, u32[]{:S(2)}, u32[]{:S(2)}) %collective-permute-start.3) | collective-permute-done | bytes 131104 | tf_op jit(solution)/shard_map/ppermute | solution.py:25
  17.4 0.1 collective-permute-start.5
  17.5 0.2 collective-permute-done.1
  17.7 0.1 add_select_fusion.2.gram_top
  17.8 1.5 %collective-permute-start.4 = (f32[136,256]{1,0:T(8,128)S(1)}, f32[136,256]{1,0:T(8,128)S(1)}, u32[]{:S(2)}, u32[]{:S(2)}) collective-permute-start(f32[136,256]{1,0:T(8,128)S(1)} %add_select_fusion.2.gram_top), channel_id=1, source_target_pairs={{7,0},{0,1},{1,2},{2,3},{3,4},{4,5},{5,6},{6,7},{15,8},{8,9},{9,10... | collective-permute-start | bytes 417800 | tf_op jit(solution)/shard_map/ppermute | solution.py:21
  19.3 3.4 %shard_map.50 = (f32[512,256]{1,0:T(8,128)S(1)}, f32[512,256]{1,0:T(8,128)S(1)}) custom-call(f32[136,256]{1,0:T(8,128)S(1)} %add_select_fusion.2.gram_top, f32[128,256]{1,0:T(8,128)S(1)} %add.51.gram_bottom, f32[512,512]{1,0:T(8,128)S(1)} %copy-done), custom_call_target="tpu_custom_call" | custom-call | flops 1912602624 | bytes 1048576 | tf_op jit(solution)/shard_map/pallas_call | solution.py:132
  22.7 1.0 %collective-permute-done.5.gram_bottom = f32[128,256]{1,0:T(8,128)S(1)} collective-permute-done((f32[128,256]{1,0:T(8,128)S(1)}, f32[128,256]{1,0:T(8,128)S(1)}, u32[]{:S(2)}, u32[]{:S(2)}) %collective-permute-start.5) | collective-permute-done | bytes 131104 | tf_op jit(solution)/shard_map/ppermute | solution.py:21
  23.7 1.5 %collective-permute-done.4.gram_top = f32[136,256]{1,0:T(8,128)S(1)} collective-permute-done((f32[136,256]{1,0:T(8,128)S(1)}, f32[136,256]{1,0:T(8,128)S(1)}, u32[]{:S(2)}, u32[]{:S(2)}) %collective-permute-start.4) | collective-permute-done | bytes 139296 | tf_op jit(solution)/shard_map/ppermute | solution.py:21
  25.2 0.0 collective-permute-done.6.refs_0_
  25.2 4.1 %shard_map.51 = (f32[512,256]{1,0:T(8,128)S(1)}, f32[512,256]{1,0:T(8,128)S(1)}, f32[512,256]{1,0:T(8,128)S(1)}, f32[136,256]{1,0:T(8,128)S(1)}, f32[128,256]{1,0:T(8,128)S(1)}) custom-call(f32[136,256]{1,0:T(8,128)S(1)} %collective-permute-done.4.gram_top, f32[128,256]{1,0:T(8,128)S(1)} %collective-permute-done.5.gram_bottom, ...), custom_call_target="tpu_custom_call" | custom-call | flops 1912602624 | bytes 1048576 | tf_op jit(solution)/shard_map/pallas_call | solution.py:132
  29.3 0.8 collective-permute-start.8
  30.1 1.5 %collective-permute-start.10 = (f32[128,256]{1,0:T(8,128)S(1)}, f32[128,256]{1,0:T(8,128)S(1)}, u32[]{:S(2)}, u32[]{:S(2)}) collective-permute-start(f32[128,256]{1,0:T(8,128)S(1)} %get-tuple-element.40), channel_id=1, source_target_pairs={{0,16},{8,24},{16,0},{24,8},{1,17},{9,25},{17,1},{25,9},{2,18},{10... | collective-permute-start | bytes 393224 | tf_op jit(solution)/shard_map/ppermute | solution.py:25
  31.6 2.8 %collective-permute-done.8 = f32[136,256]{1,0:T(8,128)S(1)} collective-permute-done((f32[136,256]{1,0:T(8,128)S(1)}, f32[136,256]{1,0:T(8,128)S(1)}, u32[]{:S(2)}, u32[]{:S(2)}) %collective-permute-start.8) | collective-permute-done | bytes 139296 | tf_op jit(solution)/shard_map/ppermute | solution.py:25
  34.4 1.6 %collective-permute-start.9 = (f32[136,256]{1,0:T(8,128)S(1)}, f32[136,256]{1,0:T(8,128)S(1)}, u32[]{:S(2)}, u32[]{:S(2)}) collective-permute-start(f32[136,256]{1,0:T(8,128)S(1)} %add.52), channel_id=1, source_target_pairs={{0,16},{8,24},{16,0},{24,8},{1,17},{9,25},{17,1},{25,9},{2,18},{10... | collective-permute-start | bytes 417800 | tf_op jit(solution)/shard_map/ppermute | solution.py:25
  36.0 0.0 collective-permute-done.10
  36.1 1.3 %collective-permute-start.11 = (f32[128,256]{1,0:T(8,128)S(1)}, f32[128,256]{1,0:T(8,128)S(1)}, u32[]{:S(2)}, u32[]{:S(2)}) collective-permute-start(f32[128,256]{1,0:T(8,128)S(1)} %add.54), channel_id=1, source_target_pairs={{0,8},{8,0},{16,24},{24,16},{1,9},{9,1},{17,25},{25,17},{2,10},{10... | collective-permute-start | bytes 393224 | tf_op jit(solution)/shard_map/ppermute | solution.py:25
  37.3 0.0 collective-permute-start.14
  38.0 0.6 collective-permute-start.7
  38.6 0.6 shard_map.53.refs_0_
  39.2 2.0 %collective-permute-done.11 = f32[128,256]{1,0:T(8,128)S(1)} collective-permute-done((f32[128,256]{1,0:T(8,128)S(1)}, f32[128,256]{1,0:T(8,128)S(1)}, u32[]{:S(2)}, u32[]{:S(2)}) %collective-permute-start.11) | collective-permute-done | bytes 131104 | tf_op jit(solution)/shard_map/ppermute | solution.py:25
  41.1 0.1 collective-permute-start.13
  41.2 0.1 add_select_fusion.1.gram_top
  41.3 0.4 collective-permute-start.12
  41.7 3.4 %shard_map.52 = (f32[512,256]{1,0:T(8,128)S(1)}, f32[512,256]{1,0:T(8,128)S(1)}) custom-call(f32[136,256]{1,0:T(8,128)S(1)} %add_select_fusion.1.gram_top, f32[128,256]{1,0:T(8,128)S(1)} %add.55.gram_bottom, f32[512,256]{1,0:T(8,128)S(1)} %get-tuple-element.36.panel_ref.refs_0_, f32[512,256]{1,0:T(8,128)S(1)} %get-tuple-element.41.refs_1_), custom_call_target="tpu_custom_call" | custom-call | flops 1912602624 | bytes 1048576 | tf_op jit(solution)/shard_map/pallas_call | solution.py:132
  45.1 9.6 %collective-permute-done.13.gram_bottom = f32[128,256]{1,0:T(8,128)S(1)} collective-permute-done((f32[128,256]{1,0:T(8,128)S(1)}, f32[128,256]{1,0:T(8,128)S(1)}, u32[]{:S(2)}, u32[]{:S(2)}) %collective-permute-start.13) | collective-permute-done | bytes 131104 | tf_op jit(solution)/shard_map/ppermute | solution.py:21
  54.8 1.5 %collective-permute-done.12.gram_top = f32[136,256]{1,0:T(8,128)S(1)} collective-permute-done((f32[136,256]{1,0:T(8,128)S(1)}, f32[136,256]{1,0:T(8,128)S(1)}, u32[]{:S(2)}, u32[]{:S(2)}) %collective-permute-start.12) | collective-permute-done | bytes 139296 | tf_op jit(solution)/shard_map/ppermute | solution.py:21
  56.3 4.1 %shard_map.54 = (f32[512,256]{1,0:T(8,128)S(1)}, f32[512,256]{1,0:T(8,128)S(1)}, f32[512,256]{1,0:T(8,128)S(1)}, f32[136,256]{1,0:T(8,128)S(1)}, f32[128,256]{1,0:T(8,128)S(1)}) custom-call(f32[136,256]{1,0:T(8,128)S(1)} %collective-permute-done.12.gram_top, f32[128,256]{1,0:T(8,128)S(1)} %collective-permute-done.13.gram_bottom, ...), custom_call_target="tpu_custom_call" | custom-call | flops 1912602624 | bytes 1048576 | tf_op jit(solution)/shard_map/pallas_call | solution.py:132
  60.4 0.9 collective-permute-start.17
  61.3 1.5 %collective-permute-start.19 = (f32[128,256]{1,0:T(8,128)S(1)}, f32[128,256]{1,0:T(8,128)S(1)}, u32[]{:S(2)}, u32[]{:S(2)}) collective-permute-start(f32[128,256]{1,0:T(8,128)S(1)} %get-tuple-element.54), channel_id=1, source_target_pairs={{0,16},{8,24},{16,0},{24,8},{1,17},{9,25},{17,1},{25,9},{2,18},{10... | collective-permute-start | bytes 393224 | tf_op jit(solution)/shard_map/ppermute | solution.py:25
  63.5 0.1 collective-permute-start.23
  63.5 4.1 %collective-permute-done.19 = f32[128,256]{1,0:T(8,128)S(1)} collective-permute-done((f32[128,256]{1,0:T(8,128)S(1)}, f32[128,256]{1,0:T(8,128)S(1)}, u32[]{:S(2)}, u32[]{:S(2)}) %collective-permute-start.19) | collective-permute-done | bytes 131104 | tf_op jit(solution)/shard_map/ppermute | solution.py:25
  67.7 1.2 %collective-permute-start.20 = (f32[128,256]{1,0:T(8,128)S(1)}, f32[128,256]{1,0:T(8,128)S(1)}, u32[]{:S(2)}, u32[]{:S(2)}) collective-permute-start(f32[128,256]{1,0:T(8,128)S(1)} %add.58), channel_id=1, source_target_pairs={{0,8},{8,0},{16,24},{24,16},{1,9},{9,1},{17,25},{25,17},{2,10},{10... | collective-permute-start | bytes 393224 | tf_op jit(solution)/shard_map/ppermute | solution.py:25
  68.9 1.1 %collective-permute-start.18 = (f32[136,256]{1,0:T(8,128)S(1)}, f32[136,256]{1,0:T(8,128)S(1)}, u32[]{:S(2)}, u32[]{:S(2)}) collective-permute-start(f32[136,256]{1,0:T(8,128)S(1)} %add.56), channel_id=1, source_target_pairs={{0,16},{8,24},{16,0},{24,8},{1,17},{9,25},{17,1},{25,9},{2,18},{10... | collective-permute-start | bytes 417800 | tf_op jit(solution)/shard_map/ppermute | solution.py:25
  70.0 0.0 collective-permute-done.7.m12
  70.0 1.4 %shard_map.55 = (f32[512,256]{1,0:T(8,128)S(1)}, f32[512,256]{1,0:T(8,128)S(1)}, f32[512,256]{1,0:T(8,128)S(1)}, f32[512,256]{1,0:T(8,128)S(1)}, f32[512,256]{1,...) custom-call(f32[512,256]{1,0:T(8,128)S(1)} %get-tuple-element.35.s10, ...), custom_call_target="tpu_custom_call" | custom-call | flops 1207959552 | bytes 1048576 | tf_op jit(solution)/shard_map/pallas_call | solution.py:132
  71.4 0.1 collective-permute-start.15
  71.5 1.3 %collective-permute-start.16 = (f32[512,256]{1,0:T(8,128)S(1)}, f32[512,256]{1,0:T(8,128)S(1)}, u32[]{:S(2)}, u32[]{:S(2)}) collective-permute-start(f32[512,256]{1,0:T(8,128)S(1)} %get-tuple-element.51.d1), channel_id=1, source_target_pairs={{0,1},{2,3},{4,5},{6,7},{8,9},{10,11},{12,13},{14,15},{16,17},{18,... | collective-permute-start | bytes 1572872 | tf_op jit(solution)/shard_map/ppermute | solution.py:300
  72.8 0.6 shard_map.57.refs_0_
  73.4 0.0 collective-permute-done.20
  73.5 0.1 collective-permute-start.22
  73.5 0.5 collective-permute-done.18
  74.0 0.1 add_select_fusion.gram_top
  74.1 0.3 collective-permute-start.21
  74.4 3.4 %shard_map.56 = (f32[512,256]{1,0:T(8,128)S(1)}, f32[512,256]{1,0:T(8,128)S(1)}) custom-call(f32[136,256]{1,0:T(8,128)S(1)} %add_select_fusion.gram_top, f32[128,256]{1,0:T(8,128)S(1)} %add.59.gram_bottom, f32[512,256]{1,0:T(8,128)S(1)} %get-tuple-element.43.panel_ref.refs_0_, f32[512,256]{1,0:T(8,128)S(1)} %get-tuple-element.55.refs_1_), custom_call_target="tpu_custom_call" | custom-call | flops 1912602624 | bytes 1048576 | tf_op jit(solution)/shard_map/pallas_call | solution.py:132
  77.8 5.5 %collective-permute-done.22.gram_bottom = f32[128,256]{1,0:T(8,128)S(1)} collective-permute-done((f32[128,256]{1,0:T(8,128)S(1)}, f32[128,256]{1,0:T(8,128)S(1)}, u32[]{:S(2)}, u32[]{:S(2)}) %collective-permute-start.22) | collective-permute-done | bytes 131104 | tf_op jit(solution)/shard_map/ppermute | solution.py:21
  83.3 1.5 %collective-permute-done.21.gram_top = f32[136,256]{1,0:T(8,128)S(1)} collective-permute-done((f32[136,256]{1,0:T(8,128)S(1)}, f32[136,256]{1,0:T(8,128)S(1)}, u32[]{:S(2)}, u32[]{:S(2)}) %collective-permute-start.21) | collective-permute-done | bytes 139296 | tf_op jit(solution)/shard_map/ppermute | solution.py:21
  84.8 3.4 %shard_map.58 = (f32[512,256]{1,0:T(8,128)S(1)}, f32[512,256]{1,0:T(8,128)S(1)}, f32[8,512]{1,0:T(8,128)S(1)}) custom-call(f32[136,256]{1,0:T(8,128)S(1)} %collective-permute-done.21.gram_top, f32[128,256]{1,0:T(8,128)S(1)} %collective-permute-done.22.gram_bottom, f32[512,256]{1,0:T(8,128)S(1)} %get-tuple-element.57.panel_ref.still, ...), custom_call_target="tpu_custom_call" | custom-call | flops 1912602624 | bytes 1048576 | tf_op jit(solution)/shard_map/pallas_call | solution.py:132
  88.2 1.4 %collective-permute-start.24 = (f32[8,512]{1,0:T(8,128)S(1)}, f32[8,512]{1,0:T(8,128)S(1)}, u32[]{:S(2)}, u32[]{:S(2)}) collective-permute-start(f32[8,512]{1,0:T(8,128)S(1)} %get-tuple-element.62), channel_id=1, source_target_pairs={{0,8},{8,0},{16,24},{24,16},{1,9},{9,1},{17,25},{25,17},{2,10},{10... | collective-permute-start | bytes 49160 | tf_op jit(solution)/shard_map/ppermute | solution.py:25
  89.7 0.5 collective-permute-start.25
  90.1 1.6 %collective-permute-start.26 = (f32[8,512]{1,0:T(8,128)S(1)}, f32[8,512]{1,0:T(8,128)S(1)}, u32[]{:S(2)}, u32[]{:S(2)}) collective-permute-start(f32[8,512]{1,0:T(8,128)S(1)} %get-tuple-element.62), channel_id=1, source_target_pairs={{0,24},{8,16},{16,8},{24,0},{1,25},{9,17},{17,9},{25,1},{2,26},{10... | collective-permute-start | bytes 49160 | tf_op jit(solution)/shard_map/ppermute | solution.py:25
  91.8 0.0 collective-permute-done.15.x1
  91.8 2.1 %finish.1 = (f32[512,512]{1,0:T(8,128)}, f32[1024,512]{1,0:T(8,128)}) custom-call(f32[512,256]{1,0:T(8,128)S(1)} %get-tuple-element.46.a0, f32[512,256]{1,0:T(8,128)S(1)} %get-tuple-element.47.b0, f32[512,256]{1,0:T(8,128)S(1)} %get-tuple-element.48.a1, f32[512,256]{1,0:T(8,128)S(1)} %get-tuple-element.49.b1, f32[512,256]{1,0:T(8,128)S(1)} %get-tuple-element.50.c1, ...), custom_call_target="tpu_custom_call" | custom-call | flops 805306368 | bytes 1048576 | tf_op jit(solution)/shard_map/finish/pallas_call | solution.py:320
  93.9 0.8 collective-permute-done.26
  94.8 0.6 fusion.1
  (18 shorter events, 0.2 us)
Async XLA Ops:
  0.6 24.5 %collective-permute-start.6 = (f32[512,512]{1,0:T(8,128)}, f32[512,512]{1,0:T(8,128)S(1)}, u32[]{:S(2)}, u32[]{:S(2)}) collective-permute-start(f32[512,512]{1,0:T(8,128)} %refs_0_.1), channel_id=1, source_target_pairs={{7,0},{0,1},{1,2},{2,3},{3,4},{4,5},{5,6},{6,7},{15,8},{8,9},{9,10... | collective-permute-start | bytes 3145736 | tf_op jit(solution)/shard_map/ppermute | solution.py:21
  1.2 1.2 %copy-start = (f32[512,512]{1,0:T(8,128)S(1)}, f32[512,512]{1,0:T(8,128)}, u32[]{:S(2)}) copy-start(f32[512,512]{1,0:T(8,128)} %refs_0_.1) | copy-start | bytes 3145732
  2.9 8.6 %collective-permute-start = (f32[136,256]{1,0:T(8,128)S(1)}, f32[136,256]{1,0:T(8,128)S(1)}, u32[]{:S(2)}, u32[]{:S(2)}) collective-permute-start(f32[136,256]{1,0:T(8,128)S(1)} %get-tuple-element.33), channel_id=1, source_target_pairs={{0,8},{8,0},{16,24},{24,16},{1,9},{9,1},{17,25},{25,17},{2,10},{10... | collective-permute-start | bytes 417800 | tf_op jit(solution)/shard_map/ppermute | solution.py:25
  5.4 5.9 %collective-permute-start.2 = (f32[128,256]{1,0:T(8,128)S(1)}, f32[128,256]{1,0:T(8,128)S(1)}, u32[]{:S(2)}, u32[]{:S(2)}) collective-permute-start(f32[128,256]{1,0:T(8,128)S(1)} %get-tuple-element.34), channel_id=1, source_target_pairs={{0,16},{8,24},{16,0},{24,8},{1,17},{9,25},{17,1},{25,9},{2,18},{10... | collective-permute-start | bytes 393224 | tf_op jit(solution)/shard_map/ppermute | solution.py:25
  11.4 6.0 %collective-permute-start.3 = (f32[128,256]{1,0:T(8,128)S(1)}, f32[128,256]{1,0:T(8,128)S(1)}, u32[]{:S(2)}, u32[]{:S(2)}) collective-permute-start(f32[128,256]{1,0:T(8,128)S(1)} %add.50), channel_id=1, source_target_pairs={{0,8},{8,0},{16,24},{24,16},{1,9},{9,1},{17,25},{25,17},{2,10},{10... | collective-permute-start | bytes 393224 | tf_op jit(solution)/shard_map/ppermute | solution.py:25
  11.5 6.2 %collective-permute-start.1 = (f32[136,256]{1,0:T(8,128)S(1)}, f32[136,256]{1,0:T(8,128)S(1)}, u32[]{:S(2)}, u32[]{:S(2)}) collective-permute-start(f32[136,256]{1,0:T(8,128)S(1)} %add.48), channel_id=1, source_target_pairs={{0,16},{8,24},{16,0},{24,8},{1,17},{9,25},{17,1},{25,9},{2,18},{10... | collective-permute-start | bytes 417800 | tf_op jit(solution)/shard_map/ppermute | solution.py:25
  17.4 6.2 %collective-permute-start.5 = (f32[128,256]{1,0:T(8,128)S(1)}, f32[128,256]{1,0:T(8,128)S(1)}, u32[]{:S(2)}, u32[]{:S(2)}) collective-permute-start(f32[128,256]{1,0:T(8,128)S(1)} %add.51.gram_bottom), channel_id=1, source_target_pairs={{7,0},{0,1},{1,2},{2,3},{3,4},{4,5},{5,6},{6,7},{15,8},{8,9},{9,10... | collective-permute-start | bytes 393224 | tf_op jit(solution)/shard_map/ppermute | solution.py:21
  17.8 7.4 %collective-permute-start.4 = (f32[136,256]{1,0:T(8,128)S(1)}, f32[136,256]{1,0:T(8,128)S(1)}, u32[]{:S(2)}, u32[]{:S(2)}) collective-permute-start(f32[136,256]{1,0:T(8,128)S(1)} %add_select_fusion.2.gram_top), channel_id=1, source_target_pairs={{7,0},{0,1},{1,2},{2,3},{3,4},{4,5},{5,6},{6,7},{15,8},{8,9},{9,10... | collective-permute-start | bytes 417800 | tf_op jit(solution)/shard_map/ppermute | solution.py:21
  29.3 5.1 %collective-permute-start.8 = (f32[136,256]{1,0:T(8,128)S(1)}, f32[136,256]{1,0:T(8,128)S(1)}, u32[]{:S(2)}, u32[]{:S(2)}) collective-permute-start(f32[136,256]{1,0:T(8,128)S(1)} %get-tuple-element.39), channel_id=1, source_target_pairs={{0,8},{8,0},{16,24},{24,16},{1,9},{9,1},{17,25},{25,17},{2,10},{10... | collective-permute-start | bytes 417800 | tf_op jit(solution)/shard_map/ppermute | solution.py:25
  30.1 6.0 %collective-permute-start.10 = (f32[128,256]{1,0:T(8,128)S(1)}, f32[128,256]{1,0:T(8,128)S(1)}, u32[]{:S(2)}, u32[]{:S(2)}) collective-permute-start(f32[128,256]{1,0:T(8,128)S(1)} %get-tuple-element.40), channel_id=1, source_target_pairs={{0,16},{8,24},{16,0},{24,8},{1,17},{9,25},{17,1},{25,9},{2,18},{10... | collective-permute-start | bytes 393224 | tf_op jit(solution)/shard_map/ppermute | solution.py:25
  34.4 6.8 %collective-permute-start.9 = (f32[136,256]{1,0:T(8,128)S(1)}, f32[136,256]{1,0:T(8,128)S(1)}, u32[]{:S(2)}, u32[]{:S(2)}) collective-permute-start(f32[136,256]{1,0:T(8,128)S(1)} %add.52), channel_id=1, source_target_pairs={{0,16},{8,24},{16,0},{24,8},{1,17},{9,25},{17,1},{25,9},{2,18},{10... | collective-permute-start | bytes 417800 | tf_op jit(solution)/shard_map/ppermute | solution.py:25
  36.1 5.0 %collective-permute-start.11 = (f32[128,256]{1,0:T(8,128)S(1)}, f32[128,256]{1,0:T(8,128)S(1)}, u32[]{:S(2)}, u32[]{:S(2)}) collective-permute-start(f32[128,256]{1,0:T(8,128)S(1)} %add.54), channel_id=1, source_target_pairs={{0,8},{8,0},{16,24},{24,16},{1,9},{9,1},{17,25},{25,17},{2,10},{10... | collective-permute-start | bytes 393224 | tf_op jit(solution)/shard_map/ppermute | solution.py:25
  37.3 18.9 %collective-permute-start.14 = (f32[512,256]{1,0:T(8,128)S(1)}, f32[512,256]{1,0:T(8,128)S(1)}, u32[]{:S(2)}, u32[]{:S(2)}) collective-permute-start(f32[512,256]{1,0:T(8,128)S(1)} %get-tuple-element.41.refs_1_), channel_id=1, source_target_pairs={{7,0},{0,1},{1,2},{2,3},{3,4},{4,5},{5,6},{6,7},{15,8},{8,9},{9,10... | collective-permute-start | bytes 1572872 | tf_op jit(solution)/shard_map/ppermute | solution.py:21
  38.0 32.0 %collective-permute-start.7 = (f32[512,256]{1,0:T(8,128)S(1)}, f32[512,256]{1,0:T(8,128)S(1)}, u32[]{:S(2)}, u32[]{:S(2)}) collective-permute-start(f32[512,256]{1,0:T(8,128)S(1)} %get-tuple-element.37.m11), channel_id=1, source_target_pairs={{7,0},{0,1},{1,2},{2,3},{3,4},{4,5},{5,6},{6,7},{15,8},{8,9},{9,10... | collective-permute-start | bytes 1572872 | tf_op jit(solution)/shard_map/ppermute | solution.py:21
  41.1 13.6 %collective-permute-start.13 = (f32[128,256]{1,0:T(8,128)S(1)}, f32[128,256]{1,0:T(8,128)S(1)}, u32[]{:S(2)}, u32[]{:S(2)}) collective-permute-start(f32[128,256]{1,0:T(8,128)S(1)} %add.55.gram_bottom), channel_id=1, source_target_pairs={{7,0},{0,1},{1,2},{2,3},{3,4},{4,5},{5,6},{6,7},{15,8},{8,9},{9,10... | collective-permute-start | bytes 393224 | tf_op jit(solution)/shard_map/ppermute | solution.py:21
  41.3 14.9 %collective-permute-start.12 = (f32[136,256]{1,0:T(8,128)S(1)}, f32[136,256]{1,0:T(8,128)S(1)}, u32[]{:S(2)}, u32[]{:S(2)}) collective-permute-start(f32[136,256]{1,0:T(8,128)S(1)} %add_select_fusion.1.gram_top), channel_id=1, source_target_pairs={{7,0},{0,1},{1,2},{2,3},{3,4},{4,5},{5,6},{6,7},{15,8},{8,9},{9,10... | collective-permute-start | bytes 417800 | tf_op jit(solution)/shard_map/ppermute | solution.py:21
  60.4 8.5 %collective-permute-start.17 = (f32[136,256]{1,0:T(8,128)S(1)}, f32[136,256]{1,0:T(8,128)S(1)}, u32[]{:S(2)}, u32[]{:S(2)}) collective-permute-start(f32[136,256]{1,0:T(8,128)S(1)} %get-tuple-element.53), channel_id=1, source_target_pairs={{0,8},{8,0},{16,24},{24,16},{1,9},{9,1},{17,25},{25,17},{2,10},{10... | collective-permute-start | bytes 417800 | tf_op jit(solution)/shard_map/ppermute | solution.py:25
  61.3 6.3 %collective-permute-start.19 = (f32[128,256]{1,0:T(8,128)S(1)}, f32[128,256]{1,0:T(8,128)S(1)}, u32[]{:S(2)}, u32[]{:S(2)}) collective-permute-start(f32[128,256]{1,0:T(8,128)S(1)} %get-tuple-element.54), channel_id=1, source_target_pairs={{0,16},{8,24},{16,0},{24,8},{1,17},{9,25},{17,1},{25,9},{2,18},{10... | collective-permute-start | bytes 393224 | tf_op jit(solution)/shard_map/ppermute | solution.py:25
  63.5 21.3 %collective-permute-start.23 = (f32[512,256]{1,0:T(8,128)S(1)}, f32[512,256]{1,0:T(8,128)S(1)}, u32[]{:S(2)}, u32[]{:S(2)}) collective-permute-start(f32[512,256]{1,0:T(8,128)S(1)} %get-tuple-element.55.refs_1_), channel_id=1, source_target_pairs={{7,0},{0,1},{1,2},{2,3},{3,4},{4,5},{5,6},{6,7},{15,8},{8,9},{9,10... | collective-permute-start | bytes 1572872 | tf_op jit(solution)/shard_map/ppermute | solution.py:21
  67.7 5.8 %collective-permute-start.20 = (f32[128,256]{1,0:T(8,128)S(1)}, f32[128,256]{1,0:T(8,128)S(1)}, u32[]{:S(2)}, u32[]{:S(2)}) collective-permute-start(f32[128,256]{1,0:T(8,128)S(1)} %add.58), channel_id=1, source_target_pairs={{0,8},{8,0},{16,24},{24,16},{1,9},{9,1},{17,25},{25,17},{2,10},{10... | collective-permute-start | bytes 393224 | tf_op jit(solution)/shard_map/ppermute | solution.py:25
  68.9 5.1 %collective-permute-start.18 = (f32[136,256]{1,0:T(8,128)S(1)}, f32[136,256]{1,0:T(8,128)S(1)}, u32[]{:S(2)}, u32[]{:S(2)}) collective-permute-start(f32[136,256]{1,0:T(8,128)S(1)} %add.56), channel_id=1, source_target_pairs={{0,16},{8,24},{16,0},{24,8},{1,17},{9,25},{17,1},{25,9},{2,18},{10... | collective-permute-start | bytes 417800 | tf_op jit(solution)/shard_map/ppermute | solution.py:25
  71.4 20.3 %collective-permute-start.15 = (f32[512,256]{1,0:T(8,128)S(1)}, f32[512,256]{1,0:T(8,128)S(1)}, u32[]{:S(2)}, u32[]{:S(2)}) collective-permute-start(f32[512,256]{1,0:T(8,128)S(1)} %get-tuple-element.52), channel_id=1, source_target_pairs={{7,0},{0,1},{1,2},{2,3},{3,4},{4,5},{5,6},{6,7},{15,8},{8,9},{9,10... | collective-permute-start | bytes 1572872 | tf_op jit(solution)/shard_map/ppermute | solution.py:21
  71.5 20.3 %collective-permute-start.16 = (f32[512,256]{1,0:T(8,128)S(1)}, f32[512,256]{1,0:T(8,128)S(1)}, u32[]{:S(2)}, u32[]{:S(2)}) collective-permute-start(f32[512,256]{1,0:T(8,128)S(1)} %get-tuple-element.51.d1), channel_id=1, source_target_pairs={{0,1},{2,3},{4,5},{6,7},{8,9},{10,11},{12,13},{14,15},{16,17},{18,... | collective-permute-start | bytes 1572872 | tf_op jit(solution)/shard_map/ppermute | solution.py:300
  73.5 9.8 %collective-permute-start.22 = (f32[128,256]{1,0:T(8,128)S(1)}, f32[128,256]{1,0:T(8,128)S(1)}, u32[]{:S(2)}, u32[]{:S(2)}) collective-permute-start(f32[128,256]{1,0:T(8,128)S(1)} %add.59.gram_bottom), channel_id=1, source_target_pairs={{7,0},{0,1},{1,2},{2,3},{3,4},{4,5},{5,6},{6,7},{15,8},{8,9},{9,10... | collective-permute-start | bytes 393224 | tf_op jit(solution)/shard_map/ppermute | solution.py:21
  74.1 10.7 %collective-permute-start.21 = (f32[136,256]{1,0:T(8,128)S(1)}, f32[136,256]{1,0:T(8,128)S(1)}, u32[]{:S(2)}, u32[]{:S(2)}) collective-permute-start(f32[136,256]{1,0:T(8,128)S(1)} %add_select_fusion.gram_top), channel_id=1, source_target_pairs={{7,0},{0,1},{1,2},{2,3},{3,4},{4,5},{5,6},{6,7},{15,8},{8,9},{9,10... | collective-permute-start | bytes 417800 | tf_op jit(solution)/shard_map/ppermute | solution.py:21
  88.2 5.7 %collective-permute-start.24 = (f32[8,512]{1,0:T(8,128)S(1)}, f32[8,512]{1,0:T(8,128)S(1)}, u32[]{:S(2)}, u32[]{:S(2)}) collective-permute-start(f32[8,512]{1,0:T(8,128)S(1)} %get-tuple-element.62), channel_id=1, source_target_pairs={{0,8},{8,0},{16,24},{24,16},{1,9},{9,1},{17,25},{25,17},{2,10},{10... | collective-permute-start | bytes 49160 | tf_op jit(solution)/shard_map/ppermute | solution.py:25
  89.7 4.3 %collective-permute-start.25 = (f32[8,512]{1,0:T(8,128)S(1)}, f32[8,512]{1,0:T(8,128)S(1)}, u32[]{:S(2)}, u32[]{:S(2)}) collective-permute-start(f32[8,512]{1,0:T(8,128)S(1)} %get-tuple-element.62), channel_id=1, source_target_pairs={{0,16},{8,24},{16,0},{24,8},{1,17},{9,25},{17,1},{25,9},{2,18},{10... | collective-permute-start | bytes 49160 | tf_op jit(solution)/shard_map/ppermute | solution.py:25
  90.1 4.6 %collective-permute-start.26 = (f32[8,512]{1,0:T(8,128)S(1)}, f32[8,512]{1,0:T(8,128)S(1)}, u32[]{:S(2)}, u32[]{:S(2)}) collective-permute-start(f32[8,512]{1,0:T(8,128)S(1)} %get-tuple-element.62), channel_id=1, source_target_pairs={{0,24},{8,16},{16,8},{24,0},{1,25},{9,17},{17,9},{25,1},{2,26},{10... | collective-permute-start | bytes 49160 | tf_op jit(solution)/shard_map/ppermute | solution.py:25

commit v4 on v3

--- a/solution.py
+++ b/solution.py
@@ -46,6 +46,12 @@
 def dot(left, right, dims=(((1,), (0,)), ((), ()))):
     one = lambda a, b: lax.dot_general(a, b, dims, preferred_element_type=jnp.float32)
     return one(left[0], right[0]) + (one(left[0], right[1]) + one(left[1], right[0]))
+
+
+def exact_dot(left, right, dims=(((1,), (0,)), ((), ()))):
+    return lax.dot_general(
+        left, right, dims, precision=lax.Precision.HIGHEST, preferred_element_type=jnp.float32
+    )
 
 
 def polar_series():
@@ -99,11 +105,9 @@
 
 def times(parts, matrix_refs):
     if len(matrix_refs) == 1:
-        whole = cut(jnp.concatenate(parts, axis=0))
-        return dot(cut(matrix_refs[0][...]), whole)
-    return dot(cut(matrix_refs[0][...]), cut(parts[0])) + dot(
-        cut(matrix_refs[1][...]), cut(parts[1])
-    )
+        whole = jnp.concatenate(parts, axis=0)
+        return exact_dot(matrix_refs[0][...], whole)
+    return exact_dot(matrix_refs[0][...], parts[0]) + exact_dot(matrix_refs[1][...], parts[1])
 
 
 def store_gram(left, right, top_ref, bottom_ref):

time: 95.6 us -> 96.6 us (1.010)
  Pallas kernels: 27 us -> 30.8 us
  waiting for transfers between devices: 37.3 us -> 33.9 us
    pallas_call x10, Pallas kernels: 24.9 us -> 28.6 us  [call(): pl.pallas_call(kernel, out_shape=outs, in_specs=specs, out_specs=[VMEM] *...]
    ppermute x11, waiting for transfers between devices: 20.6 us -> 18.1 us  [from_behind(): lax.ppermute(block, axis, [((i - distance) % count, i) for i in range(cou...]
    ppermute x11, starting transfers between devices: 3.62 us -> 4.84 us  [from_behind(): lax.ppermute(block, axis, [((i - distance) % count, i) for i in range(cou...]
  transfers between devices with their start and end apart: 27 -> 27, of which waited for: 14 -> 13; matrix products, arithmetic and copies ran while one was open for 2% -> 2% of each run, Pallas kernels for 24% -> 27%
where the time goes in v4:
time: 96.6 us; the launch traced here: 96.4 us
  waiting for transfers between devices  33.9 us (35%)
  Pallas kernels  30.8 us (32%)
  starting transfers between devices  25.3 us (26%)
  between operations  2.83 us (3%)
  local copies, waits for them, and re-layouts  2.58 us (3%)
  other arithmetic  1.05 us (1%)
    pallas_call x10, Pallas kernels, call(): pl.pallas_call(kernel, out_shape=outs, in_specs=specs, out_specs=[VMEM] *...  28.6 us
    ppermute x15, starting transfers between devices, exchange(): lax.ppermute(block, axis, [(i, i ^ mask) for i in range(lax.axis_size(axi...  19.2 us
    ppermute x11, waiting for transfers between devices, from_behind(): lax.ppermute(block, axis, [((i - distance) % count, i) for i in range(cou...  18.1 us
    ppermute x15, waiting for transfers between devices, exchange(): lax.ppermute(block, axis, [(i, i ^ mask) for i in range(lax.axis_size(axi...  15.7 us
    ppermute x11, starting transfers between devices, from_behind(): lax.ppermute(block, axis, [((i - distance) % count, i) for i in range(cou...  4.84 us
    pallas_call x1, Pallas kernels, per_device(): pl.pallas_call(functools.partial(finish_kernel, rows_each), name='finish'...  2.13 us
  transfers between devices with their start and end apart: 27, of which 13 were waited for; matrix products, arithmetic and copies ran while one was open for 2% of the time, Pallas kernels for 27%

profile of v4, /device:TPU:0, one launch (start us, length us, event | category | flops | bytes accessed | tf_op | source)
XLA Modules:
  0.0 96.4 jit_solution(3732321682503153737)
XLA Ops:
  0.6 0.5 collective-permute-start.6
  1.2 1.2 %copy-done = f32[512,512]{1,0:T(8,128)S(1)} copy-done((f32[512,512]{1,0:T(8,128)S(1)}, f32[512,512]{1,0:T(8,128)}, u32[]{:S(2)}) %copy-start) | copy-done | bytes 1048600
  2.4 0.5 shard_map.49
  2.9 2.5 %collective-permute-start = (f32[136,256]{1,0:T(8,128)S(1)}, f32[136,256]{1,0:T(8,128)S(1)}, u32[]{:S(2)}, u32[]{:S(2)}) collective-permute-start(f32[136,256]{1,0:T(8,128)S(1)} %get-tuple-element.33), channel_id=1, source_target_pairs={{0,8},{8,0},{16,24},{24,16},{1,9},{9,1},{17,25},{25,17},{2,10},{10... | collective-permute-start | bytes 417800 | tf_op jit(solution)/shard_map/ppermute | solution.py:25
  5.4 1.5 %collective-permute-start.2 = (f32[128,256]{1,0:T(8,128)S(1)}, f32[128,256]{1,0:T(8,128)S(1)}, u32[]{:S(2)}, u32[]{:S(2)}) collective-permute-start(f32[128,256]{1,0:T(8,128)S(1)} %get-tuple-element.34), channel_id=1, source_target_pairs={{0,16},{8,24},{16,0},{24,8},{1,17},{9,25},{17,1},{25,9},{2,18},{10... | collective-permute-start | bytes 393224 | tf_op jit(solution)/shard_map/ppermute | solution.py:25
  6.9 4.4 %collective-permute-done.2 = f32[128,256]{1,0:T(8,128)S(1)} collective-permute-done((f32[128,256]{1,0:T(8,128)S(1)}, f32[128,256]{1,0:T(8,128)S(1)}, u32[]{:S(2)}, u32[]{:S(2)}) %collective-permute-start.2) | collective-permute-done | bytes 131104 | tf_op jit(solution)/shard_map/ppermute | solution.py:25
  11.4 0.1 collective-permute-start.3
  11.4 0.0 collective-permute-done
  11.5 2.1 %collective-permute-start.1 = (f32[136,256]{1,0:T(8,128)S(1)}, f32[136,256]{1,0:T(8,128)S(1)}, u32[]{:S(2)}, u32[]{:S(2)}) collective-permute-start(f32[136,256]{1,0:T(8,128)S(1)} %add.48), channel_id=1, source_target_pairs={{0,16},{8,24},{16,0},{24,8},{1,17},{9,25},{17,1},{25,9},{2,18},{10... | collective-permute-start | bytes 417800 | tf_op jit(solution)/shard_map/ppermute | solution.py:25
  13.6 1.4 %fusion.2 = (s32[1,1]{0,1:T(1,128)}, s32[1,1]{0,1:T(1,128)}, s32[1,1]{0,1:T(1,128)}) fusion(s32[3,1]{0,1:T(1,128)} %param.3), kind=kLoop, calls=%fused_computation.9 | loop fusion | bytes 24 | tf_op jit(solution)/shard_map/slice | solution.py:266
  15.6 1.8 %collective-permute-done.3 = f32[128,256]{1,0:T(8,128)S(1)} collective-permute-done((f32[128,256]{1,0:T(8,128)S(1)}, f32[128,256]{1,0:T(8,128)S(1)}, u32[]{:S(2)}, u32[]{:S(2)}) %collective-permute-start.3) | collective-permute-done | bytes 131104 | tf_op jit(solution)/shard_map/ppermute | solution.py:25
  17.4 0.1 collective-permute-start.5
  17.5 0.2 collective-permute-done.1
  17.7 0.1 add_select_fusion.2.gram_top
  17.8 1.5 %collective-permute-start.4 = (f32[136,256]{1,0:T(8,128)S(1)}, f32[136,256]{1,0:T(8,128)S(1)}, u32[]{:S(2)}, u32[]{:S(2)}) collective-permute-start(f32[136,256]{1,0:T(8,128)S(1)} %add_select_fusion.2.gram_top), channel_id=1, source_target_pairs={{7,0},{0,1},{1,2},{2,3},{3,4},{4,5},{5,6},{6,7},{15,8},{8,9},{9,10... | collective-permute-start | bytes 417800 | tf_op jit(solution)/shard_map/ppermute | solution.py:21
  19.3 3.9 %shard_map.50 = (f32[512,256]{1,0:T(8,128)S(1)}, f32[512,256]{1,0:T(8,128)S(1)}) custom-call(f32[136,256]{1,0:T(8,128)S(1)} %add_select_fusion.2.gram_top, f32[128,256]{1,0:T(8,128)S(1)} %add.51.gram_bottom, f32[512,512]{1,0:T(8,128)S(1)} %copy-done), custom_call_target="tpu_custom_call" | custom-call | flops 1912602624 | bytes 1048576 | tf_op jit(solution)/shard_map/pallas_call | solution.py:136
  23.2 0.5 collective-permute-done.5.gram_bottom
  23.7 1.5 %collective-permute-done.4.gram_top = f32[136,256]{1,0:T(8,128)S(1)} collective-permute-done((f32[136,256]{1,0:T(8,128)S(1)}, f32[136,256]{1,0:T(8,128)S(1)}, u32[]{:S(2)}, u32[]{:S(2)}) %collective-permute-start.4) | collective-permute-done | bytes 139296 | tf_op jit(solution)/shard_map/ppermute | solution.py:21
  25.2 0.0 collective-permute-done.6.refs_0_
  25.2 4.6 %shard_map.51 = (f32[512,256]{1,0:T(8,128)S(1)}, f32[512,256]{1,0:T(8,128)S(1)}, f32[512,256]{1,0:T(8,128)S(1)}, f32[136,256]{1,0:T(8,128)S(1)}, f32[128,256]{1,0:T(8,128)S(1)}) custom-call(f32[136,256]{1,0:T(8,128)S(1)} %collective-permute-done.4.gram_top, f32[128,256]{1,0:T(8,128)S(1)} %collective-permute-done.5.gram_bottom, ...), custom_call_target="tpu_custom_call" | custom-call | flops 1912602624 | bytes 1048576 | tf_op jit(solution)/shard_map/pallas_call | solution.py:136
  29.8 0.8 collective-permute-start.8
  30.5 1.5 %collective-permute-start.10 = (f32[128,256]{1,0:T(8,128)S(1)}, f32[128,256]{1,0:T(8,128)S(1)}, u32[]{:S(2)}, u32[]{:S(2)}) collective-permute-start(f32[128,256]{1,0:T(8,128)S(1)} %get-tuple-element.40), channel_id=1, source_target_pairs={{0,16},{8,24},{16,0},{24,8},{1,17},{9,25},{17,1},{25,9},{2,18},{10... | collective-permute-start | bytes 393224 | tf_op jit(solution)/shard_map/ppermute | solution.py:25
  32.1 2.8 %collective-permute-done.8 = f32[136,256]{1,0:T(8,128)S(1)} collective-permute-done((f32[136,256]{1,0:T(8,128)S(1)}, f32[136,256]{1,0:T(8,128)S(1)}, u32[]{:S(2)}, u32[]{:S(2)}) %collective-permute-start.8) | collective-permute-done | bytes 139296 | tf_op jit(solution)/shard_map/ppermute | solution.py:25
  34.9 1.6 %collective-permute-start.9 = (f32[136,256]{1,0:T(8,128)S(1)}, f32[136,256]{1,0:T(8,128)S(1)}, u32[]{:S(2)}, u32[]{:S(2)}) collective-permute-start(f32[136,256]{1,0:T(8,128)S(1)} %add.52), channel_id=1, source_target_pairs={{0,16},{8,24},{16,0},{24,8},{1,17},{9,25},{17,1},{25,9},{2,18},{10... | collective-permute-start | bytes 417800 | tf_op jit(solution)/shard_map/ppermute | solution.py:25
  36.5 0.8 collective-permute-start.11
  37.3 0.0 collective-permute-start.14
  38.0 1.3 %collective-permute-start.7 = (f32[512,256]{1,0:T(8,128)S(1)}, f32[512,256]{1,0:T(8,128)S(1)}, u32[]{:S(2)}, u32[]{:S(2)}) collective-permute-start(f32[512,256]{1,0:T(8,128)S(1)} %get-tuple-element.37.m11), channel_id=1, source_target_pairs={{7,0},{0,1},{1,2},{2,3},{3,4},{4,5},{5,6},{6,7},{15,8},{8,9},{9,10... | collective-permute-start | bytes 1572872 | tf_op jit(solution)/shard_map/ppermute | solution.py:21
  39.2 1.1 %shard_map.53.refs_0_ = f32[512,256]{1,0:T(8,128)S(1)} custom-call(f32[512,256]{1,0:T(8,128)S(1)} %get-tuple-element.38.staying_ref.s11, f32[512,512]{1,0:T(8,128)S(1)} %collective-permute-done.6.refs_0_), custom_call_target="tpu_custom_call" | custom-call | flops 402653184 | bytes 1048576 | tf_op jit(solution)/shard_map/pallas_call | solution.py:136
  40.3 1.2 %collective-permute-done.11 = f32[128,256]{1,0:T(8,128)S(1)} collective-permute-done((f32[128,256]{1,0:T(8,128)S(1)}, f32[128,256]{1,0:T(8,128)S(1)}, u32[]{:S(2)}, u32[]{:S(2)}) %collective-permute-start.11) | collective-permute-done | bytes 131104 | tf_op jit(solution)/shard_map/ppermute | solution.py:25
  41.6 0.1 collective-permute-start.13
  41.7 0.1 add_select_fusion.1.gram_top
  41.8 0.9 collective-permute-start.12
  42.7 3.9 %shard_map.52 = (f32[512,256]{1,0:T(8,128)S(1)}, f32[512,256]{1,0:T(8,128)S(1)}) custom-call(f32[136,256]{1,0:T(8,128)S(1)} %add_select_fusion.1.gram_top, f32[128,256]{1,0:T(8,128)S(1)} %add.55.gram_bottom, f32[512,256]{1,0:T(8,128)S(1)} %get-tuple-element.36.panel_ref.refs_0_, f32[512,256]{1,0:T(8,128)S(1)} %get-tuple-element.41.refs_1_), custom_call_target="tpu_custom_call" | custom-call | flops 1912602624 | bytes 1048576 | tf_op jit(solution)/shard_map/pallas_call | solution.py:136
  46.6 8.2 %collective-permute-done.13.gram_bottom = f32[128,256]{1,0:T(8,128)S(1)} collective-permute-done((f32[128,256]{1,0:T(8,128)S(1)}, f32[128,256]{1,0:T(8,128)S(1)}, u32[]{:S(2)}, u32[]{:S(2)}) %collective-permute-start.13) | collective-permute-done | bytes 131104 | tf_op jit(solution)/shard_map/ppermute | solution.py:21
  54.7 1.5 %collective-permute-done.12.gram_top = f32[136,256]{1,0:T(8,128)S(1)} collective-permute-done((f32[136,256]{1,0:T(8,128)S(1)}, f32[136,256]{1,0:T(8,128)S(1)}, u32[]{:S(2)}, u32[]{:S(2)}) %collective-permute-start.12) | collective-permute-done | bytes 139296 | tf_op jit(solution)/shard_map/ppermute | solution.py:21
  56.2 4.5 %shard_map.54 = (f32[512,256]{1,0:T(8,128)S(1)}, f32[512,256]{1,0:T(8,128)S(1)}, f32[512,256]{1,0:T(8,128)S(1)}, f32[136,256]{1,0:T(8,128)S(1)}, f32[128,256]{1,0:T(8,128)S(1)}) custom-call(f32[136,256]{1,0:T(8,128)S(1)} %collective-permute-done.12.gram_top, f32[128,256]{1,0:T(8,128)S(1)} %collective-permute-done.13.gram_bottom, ...), custom_call_target="tpu_custom_call" | custom-call | flops 1912602624 | bytes 1048576 | tf_op jit(solution)/shard_map/pallas_call | solution.py:136
  60.7 1.4 %collective-permute-start.17 = (f32[136,256]{1,0:T(8,128)S(1)}, f32[136,256]{1,0:T(8,128)S(1)}, u32[]{:S(2)}, u32[]{:S(2)}) collective-permute-start(f32[136,256]{1,0:T(8,128)S(1)} %get-tuple-element.53), channel_id=1, source_target_pairs={{0,8},{8,0},{16,24},{24,16},{1,9},{9,1},{17,25},{25,17},{2,10},{10... | collective-permute-start | bytes 417800 | tf_op jit(solution)/shard_map/ppermute | solution.py:25
  62.1 1.1 %collective-permute-start.19 = (f32[128,256]{1,0:T(8,128)S(1)}, f32[128,256]{1,0:T(8,128)S(1)}, u32[]{:S(2)}, u32[]{:S(2)}) collective-permute-start(f32[128,256]{1,0:T(8,128)S(1)} %get-tuple-element.54), channel_id=1, source_target_pairs={{0,16},{8,24},{16,0},{24,8},{1,17},{9,25},{17,1},{25,9},{2,18},{10... | collective-permute-start | bytes 393224 | tf_op jit(solution)/shard_map/ppermute | solution.py:25
  63.8 0.1 collective-permute-start.23
  63.9 4.3 %collective-permute-done.19 = f32[128,256]{1,0:T(8,128)S(1)} collective-permute-done((f32[128,256]{1,0:T(8,128)S(1)}, f32[128,256]{1,0:T(8,128)S(1)}, u32[]{:S(2)}, u32[]{:S(2)}) %collective-permute-start.19) | collective-permute-done | bytes 131104 | tf_op jit(solution)/shard_map/ppermute | solution.py:25
  68.2 0.3 collective-permute-start.20
  68.4 0.0 collective-permute-done.17
  68.5 2.0 %collective-permute-start.18 = (f32[136,256]{1,0:T(8,128)S(1)}, f32[136,256]{1,0:T(8,128)S(1)}, u32[]{:S(2)}, u32[]{:S(2)}) collective-permute-start(f32[136,256]{1,0:T(8,128)S(1)} %add.56), channel_id=1, source_target_pairs={{0,16},{8,24},{16,0},{24,8},{1,17},{9,25},{17,1},{25,9},{2,18},{10... | collective-permute-start | bytes 417800 | tf_op jit(solution)/shard_map/ppermute | solution.py:25
  70.5 0.0 collective-permute-done.7.m12
  70.5 1.4 %shard_map.55 = (f32[512,256]{1,0:T(8,128)S(1)}, f32[512,256]{1,0:T(8,128)S(1)}, f32[512,256]{1,0:T(8,128)S(1)}, f32[512,256]{1,0:T(8,128)S(1)}, f32[512,256]{1,...) custom-call(f32[512,256]{1,0:T(8,128)S(1)} %get-tuple-element.35.s10, ...), custom_call_target="tpu_custom_call" | custom-call | flops 1207959552 | bytes 1048576 | tf_op jit(solution)/shard_map/pallas_call | solution.py:136
  71.9 0.1 collective-permute-start.15
  72.0 1.3 %collective-permute-start.16 = (f32[512,256]{1,0:T(8,128)S(1)}, f32[512,256]{1,0:T(8,128)S(1)}, u32[]{:S(2)}, u32[]{:S(2)}) collective-permute-start(f32[512,256]{1,0:T(8,128)S(1)} %get-tuple-element.51.d1), channel_id=1, source_target_pairs={{0,1},{2,3},{4,5},{6,7},{8,9},{10,11},{12,13},{14,15},{16,17},{18,... | collective-permute-start | bytes 1572872 | tf_op jit(solution)/shard_map/ppermute | solution.py:304
  73.3 1.1 %shard_map.57.refs_0_ = f32[512,256]{1,0:T(8,128)S(1)} custom-call(f32[512,256]{1,0:T(8,128)S(1)} %get-tuple-element.44.s21.staying_ref, f32[512,256]{1,0:T(8,128)S(1)} %shard_map.53.refs_0_, f32[512,256]{1,0:T(8,128)S(1)} %collective-permute-done.14.refs_1_), custom_call_target="tpu_custom_call" | custom-call | flops 402653184 | bytes 1048576 | tf_op jit(solution)/shard_map/pallas_call | solution.py:136
  74.4 0.0 collective-permute-done.20
  74.5 0.1 collective-permute-start.22
  74.5 0.0 collective-permute-done.18
  74.5 0.1 add_select_fusion.gram_top
  74.6 0.3 collective-permute-start.21
  74.9 3.9 %shard_map.56 = (f32[512,256]{1,0:T(8,128)S(1)}, f32[512,256]{1,0:T(8,128)S(1)}) custom-call(f32[136,256]{1,0:T(8,128)S(1)} %add_select_fusion.gram_top, f32[128,256]{1,0:T(8,128)S(1)} %add.59.gram_bottom, f32[512,256]{1,0:T(8,128)S(1)} %get-tuple-element.43.panel_ref.refs_0_, f32[512,256]{1,0:T(8,128)S(1)} %get-tuple-element.55.refs_1_), custom_call_target="tpu_custom_call" | custom-call | flops 1912602624 | bytes 1048576 | tf_op jit(solution)/shard_map/pallas_call | solution.py:136
  78.8 5.0 %collective-permute-done.22.gram_bottom = f32[128,256]{1,0:T(8,128)S(1)} collective-permute-done((f32[128,256]{1,0:T(8,128)S(1)}, f32[128,256]{1,0:T(8,128)S(1)}, u32[]{:S(2)}, u32[]{:S(2)}) %collective-permute-start.22) | collective-permute-done | bytes 131104 | tf_op jit(solution)/shard_map/ppermute | solution.py:21
  83.8 1.5 %collective-permute-done.21.gram_top = f32[136,256]{1,0:T(8,128)S(1)} collective-permute-done((f32[136,256]{1,0:T(8,128)S(1)}, f32[136,256]{1,0:T(8,128)S(1)}, u32[]{:S(2)}, u32[]{:S(2)}) %collective-permute-start.21) | collective-permute-done | bytes 139296 | tf_op jit(solution)/shard_map/ppermute | solution.py:21
  85.3 0.0 collective-permute-done.23.refs_1_
  85.3 3.9 %shard_map.58 = (f32[512,256]{1,0:T(8,128)S(1)}, f32[512,256]{1,0:T(8,128)S(1)}, f32[8,512]{1,0:T(8,128)S(1)}) custom-call(f32[136,256]{1,0:T(8,128)S(1)} %collective-permute-done.21.gram_top, f32[128,256]{1,0:T(8,128)S(1)} %collective-permute-done.22.gram_bottom, f32[512,256]{1,0:T(8,128)S(1)} %get-tuple-element.57.panel_ref.still, ...), custom_call_target="tpu_custom_call" | custom-call | flops 1912602624 | bytes 1048576 | tf_op jit(solution)/shard_map/pallas_call | solution.py:136
  89.2 0.6 collective-permute-start.24
  89.8 1.4 %collective-permute-start.25 = (f32[8,512]{1,0:T(8,128)S(1)}, f32[8,512]{1,0:T(8,128)S(1)}, u32[]{:S(2)}, u32[]{:S(2)}) collective-permute-start(f32[8,512]{1,0:T(8,128)S(1)} %get-tuple-element.62), channel_id=1, source_target_pairs={{0,16},{8,24},{16,0},{24,8},{1,17},{9,25},{17,1},{25,9},{2,18},{10... | collective-permute-start | bytes 49160 | tf_op jit(solution)/shard_map/ppermute | solution.py:25
  91.2 1.6 %collective-permute-start.26 = (f32[8,512]{1,0:T(8,128)S(1)}, f32[8,512]{1,0:T(8,128)S(1)}, u32[]{:S(2)}, u32[]{:S(2)}) collective-permute-start(f32[8,512]{1,0:T(8,128)S(1)} %get-tuple-element.62), channel_id=1, source_target_pairs={{0,24},{8,16},{16,8},{24,0},{1,25},{9,17},{17,9},{25,1},{2,26},{10... | collective-permute-start | bytes 49160 | tf_op jit(solution)/shard_map/ppermute | solution.py:25
  92.8 2.1 %finish.1 = (f32[512,512]{1,0:T(8,128)}, f32[1024,512]{1,0:T(8,128)}) custom-call(f32[512,256]{1,0:T(8,128)S(1)} %get-tuple-element.46.a0, f32[512,256]{1,0:T(8,128)S(1)} %get-tuple-element.47.b0, f32[512,256]{1,0:T(8,128)S(1)} %get-tuple-element.48.a1, f32[512,256]{1,0:T(8,128)S(1)} %get-tuple-element.49.b1, f32[512,256]{1,0:T(8,128)S(1)} %get-tuple-element.50.c1, ...), custom_call_target="tpu_custom_call" | custom-call | flops 805306368 | bytes 1048576 | tf_op jit(solution)/shard_map/finish/pallas_call | solution.py:324
  94.9 0.9 collective-permute-done.26
  95.8 0.6 fusion.1
  (18 shorter events, 0.2 us)
Async XLA Ops:
  0.6 24.5 %collective-permute-start.6 = (f32[512,512]{1,0:T(8,128)}, f32[512,512]{1,0:T(8,128)S(1)}, u32[]{:S(2)}, u32[]{:S(2)}) collective-permute-start(f32[512,512]{1,0:T(8,128)} %refs_0_.1), channel_id=1, source_target_pairs={{7,0},{0,1},{1,2},{2,3},{3,4},{4,5},{5,6},{6,7},{15,8},{8,9},{9,10... | collective-permute-start | bytes 3145736 | tf_op jit(solution)/shard_map/ppermute | solution.py:21
  1.2 1.2 %copy-start = (f32[512,512]{1,0:T(8,128)S(1)}, f32[512,512]{1,0:T(8,128)}, u32[]{:S(2)}) copy-start(f32[512,512]{1,0:T(8,128)} %refs_0_.1) | copy-start | bytes 3145732
  2.9 8.6 %collective-permute-start = (f32[136,256]{1,0:T(8,128)S(1)}, f32[136,256]{1,0:T(8,128)S(1)}, u32[]{:S(2)}, u32[]{:S(2)}) collective-permute-start(f32[136,256]{1,0:T(8,128)S(1)} %get-tuple-element.33), channel_id=1, source_target_pairs={{0,8},{8,0},{16,24},{24,16},{1,9},{9,1},{17,25},{25,17},{2,10},{10... | collective-permute-start | bytes 417800 | tf_op jit(solution)/shard_map/ppermute | solution.py:25
  5.4 5.9 %collective-permute-start.2 = (f32[128,256]{1,0:T(8,128)S(1)}, f32[128,256]{1,0:T(8,128)S(1)}, u32[]{:S(2)}, u32[]{:S(2)}) collective-permute-start(f32[128,256]{1,0:T(8,128)S(1)} %get-tuple-element.34), channel_id=1, source_target_pairs={{0,16},{8,24},{16,0},{24,8},{1,17},{9,25},{17,1},{25,9},{2,18},{10... | collective-permute-start | bytes 393224 | tf_op jit(solution)/shard_map/ppermute | solution.py:25
  11.4 6.0 %collective-permute-start.3 = (f32[128,256]{1,0:T(8,128)S(1)}, f32[128,256]{1,0:T(8,128)S(1)}, u32[]{:S(2)}, u32[]{:S(2)}) collective-permute-start(f32[128,256]{1,0:T(8,128)S(1)} %add.50), channel_id=1, source_target_pairs={{0,8},{8,0},{16,24},{24,16},{1,9},{9,1},{17,25},{25,17},{2,10},{10... | collective-permute-start | bytes 393224 | tf_op jit(solution)/shard_map/ppermute | solution.py:25
  11.5 6.2 %collective-permute-start.1 = (f32[136,256]{1,0:T(8,128)S(1)}, f32[136,256]{1,0:T(8,128)S(1)}, u32[]{:S(2)}, u32[]{:S(2)}) collective-permute-start(f32[136,256]{1,0:T(8,128)S(1)} %add.48), channel_id=1, source_target_pairs={{0,16},{8,24},{16,0},{24,8},{1,17},{9,25},{17,1},{25,9},{2,18},{10... | collective-permute-start | bytes 417800 | tf_op jit(solution)/shard_map/ppermute | solution.py:25
  17.4 6.2 %collective-permute-start.5 = (f32[128,256]{1,0:T(8,128)S(1)}, f32[128,256]{1,0:T(8,128)S(1)}, u32[]{:S(2)}, u32[]{:S(2)}) collective-permute-start(f32[128,256]{1,0:T(8,128)S(1)} %add.51.gram_bottom), channel_id=1, source_target_pairs={{7,0},{0,1},{1,2},{2,3},{3,4},{4,5},{5,6},{6,7},{15,8},{8,9},{9,10... | collective-permute-start | bytes 393224 | tf_op jit(solution)/shard_map/ppermute | solution.py:21
  17.8 7.4 %collective-permute-start.4 = (f32[136,256]{1,0:T(8,128)S(1)}, f32[136,256]{1,0:T(8,128)S(1)}, u32[]{:S(2)}, u32[]{:S(2)}) collective-permute-start(f32[136,256]{1,0:T(8,128)S(1)} %add_select_fusion.2.gram_top), channel_id=1, source_target_pairs={{7,0},{0,1},{1,2},{2,3},{3,4},{4,5},{5,6},{6,7},{15,8},{8,9},{9,10... | collective-permute-start | bytes 417800 | tf_op jit(solution)/shard_map/ppermute | solution.py:21
  29.8 5.1 %collective-permute-start.8 = (f32[136,256]{1,0:T(8,128)S(1)}, f32[136,256]{1,0:T(8,128)S(1)}, u32[]{:S(2)}, u32[]{:S(2)}) collective-permute-start(f32[136,256]{1,0:T(8,128)S(1)} %get-tuple-element.39), channel_id=1, source_target_pairs={{0,8},{8,0},{16,24},{24,16},{1,9},{9,1},{17,25},{25,17},{2,10},{10... | collective-permute-start | bytes 417800 | tf_op jit(solution)/shard_map/ppermute | solution.py:25
  30.5 6.0 %collective-permute-start.10 = (f32[128,256]{1,0:T(8,128)S(1)}, f32[128,256]{1,0:T(8,128)S(1)}, u32[]{:S(2)}, u32[]{:S(2)}) collective-permute-start(f32[128,256]{1,0:T(8,128)S(1)} %get-tuple-element.40), channel_id=1, source_target_pairs={{0,16},{8,24},{16,0},{24,8},{1,17},{9,25},{17,1},{25,9},{2,18},{10... | collective-permute-start | bytes 393224 | tf_op jit(solution)/shard_map/ppermute | solution.py:25
  34.9 6.7 %collective-permute-start.9 = (f32[136,256]{1,0:T(8,128)S(1)}, f32[136,256]{1,0:T(8,128)S(1)}, u32[]{:S(2)}, u32[]{:S(2)}) collective-permute-start(f32[136,256]{1,0:T(8,128)S(1)} %add.52), channel_id=1, source_target_pairs={{0,16},{8,24},{16,0},{24,8},{1,17},{9,25},{17,1},{25,9},{2,18},{10... | collective-permute-start | bytes 417800 | tf_op jit(solution)/shard_map/ppermute | solution.py:25
  36.5 5.0 %collective-permute-start.11 = (f32[128,256]{1,0:T(8,128)S(1)}, f32[128,256]{1,0:T(8,128)S(1)}, u32[]{:S(2)}, u32[]{:S(2)}) collective-permute-start(f32[128,256]{1,0:T(8,128)S(1)} %add.54), channel_id=1, source_target_pairs={{0,8},{8,0},{16,24},{24,16},{1,9},{9,1},{17,25},{25,17},{2,10},{10... | collective-permute-start | bytes 393224 | tf_op jit(solution)/shard_map/ppermute | solution.py:25
  37.3 18.9 %collective-permute-start.14 = (f32[512,256]{1,0:T(8,128)S(1)}, f32[512,256]{1,0:T(8,128)S(1)}, u32[]{:S(2)}, u32[]{:S(2)}) collective-permute-start(f32[512,256]{1,0:T(8,128)S(1)} %get-tuple-element.41.refs_1_), channel_id=1, source_target_pairs={{7,0},{0,1},{1,2},{2,3},{3,4},{4,5},{5,6},{6,7},{15,8},{8,9},{9,10... | collective-permute-start | bytes 1572872 | tf_op jit(solution)/shard_map/ppermute | solution.py:21
  38.0 32.5 %collective-permute-start.7 = (f32[512,256]{1,0:T(8,128)S(1)}, f32[512,256]{1,0:T(8,128)S(1)}, u32[]{:S(2)}, u32[]{:S(2)}) collective-permute-start(f32[512,256]{1,0:T(8,128)S(1)} %get-tuple-element.37.m11), channel_id=1, source_target_pairs={{7,0},{0,1},{1,2},{2,3},{3,4},{4,5},{5,6},{6,7},{15,8},{8,9},{9,10... | collective-permute-start | bytes 1572872 | tf_op jit(solution)/shard_map/ppermute | solution.py:21
  41.6 13.2 %collective-permute-start.13 = (f32[128,256]{1,0:T(8,128)S(1)}, f32[128,256]{1,0:T(8,128)S(1)}, u32[]{:S(2)}, u32[]{:S(2)}) collective-permute-start(f32[128,256]{1,0:T(8,128)S(1)} %add.55.gram_bottom), channel_id=1, source_target_pairs={{7,0},{0,1},{1,2},{2,3},{3,4},{4,5},{5,6},{6,7},{15,8},{8,9},{9,10... | collective-permute-start | bytes 393224 | tf_op jit(solution)/shard_map/ppermute | solution.py:21
  41.8 14.5 %collective-permute-start.12 = (f32[136,256]{1,0:T(8,128)S(1)}, f32[136,256]{1,0:T(8,128)S(1)}, u32[]{:S(2)}, u32[]{:S(2)}) collective-permute-start(f32[136,256]{1,0:T(8,128)S(1)} %add_select_fusion.1.gram_top), channel_id=1, source_target_pairs={{7,0},{0,1},{1,2},{2,3},{3,4},{4,5},{5,6},{6,7},{15,8},{8,9},{9,10... | collective-permute-start | bytes 417800 | tf_op jit(solution)/shard_map/ppermute | solution.py:21
  60.7 7.7 %collective-permute-start.17 = (f32[136,256]{1,0:T(8,128)S(1)}, f32[136,256]{1,0:T(8,128)S(1)}, u32[]{:S(2)}, u32[]{:S(2)}) collective-permute-start(f32[136,256]{1,0:T(8,128)S(1)} %get-tuple-element.53), channel_id=1, source_target_pairs={{0,8},{8,0},{16,24},{24,16},{1,9},{9,1},{17,25},{25,17},{2,10},{10... | collective-permute-start | bytes 417800 | tf_op jit(solution)/shard_map/ppermute | solution.py:25
  62.1 6.1 %collective-permute-start.19 = (f32[128,256]{1,0:T(8,128)S(1)}, f32[128,256]{1,0:T(8,128)S(1)}, u32[]{:S(2)}, u32[]{:S(2)}) collective-permute-start(f32[128,256]{1,0:T(8,128)S(1)} %get-tuple-element.54), channel_id=1, source_target_pairs={{0,16},{8,24},{16,0},{24,8},{1,17},{9,25},{17,1},{25,9},{2,18},{10... | collective-permute-start | bytes 393224 | tf_op jit(solution)/shard_map/ppermute | solution.py:25
  63.8 21.5 %collective-permute-start.23 = (f32[512,256]{1,0:T(8,128)S(1)}, f32[512,256]{1,0:T(8,128)S(1)}, u32[]{:S(2)}, u32[]{:S(2)}) collective-permute-start(f32[512,256]{1,0:T(8,128)S(1)} %get-tuple-element.55.refs_1_), channel_id=1, source_target_pairs={{7,0},{0,1},{1,2},{2,3},{3,4},{4,5},{5,6},{6,7},{15,8},{8,9},{9,10... | collective-permute-start | bytes 1572872 | tf_op jit(solution)/shard_map/ppermute | solution.py:21
  68.2 6.2 %collective-permute-start.20 = (f32[128,256]{1,0:T(8,128)S(1)}, f32[128,256]{1,0:T(8,128)S(1)}, u32[]{:S(2)}, u32[]{:S(2)}) collective-permute-start(f32[128,256]{1,0:T(8,128)S(1)} %add.58), channel_id=1, source_target_pairs={{0,8},{8,0},{16,24},{24,16},{1,9},{9,1},{17,25},{25,17},{2,10},{10... | collective-permute-start | bytes 393224 | tf_op jit(solution)/shard_map/ppermute | solution.py:25
  68.5 6.0 %collective-permute-start.18 = (f32[136,256]{1,0:T(8,128)S(1)}, f32[136,256]{1,0:T(8,128)S(1)}, u32[]{:S(2)}, u32[]{:S(2)}) collective-permute-start(f32[136,256]{1,0:T(8,128)S(1)} %add.56), channel_id=1, source_target_pairs={{0,16},{8,24},{16,0},{24,8},{1,17},{9,25},{17,1},{25,9},{2,18},{10... | collective-permute-start | bytes 417800 | tf_op jit(solution)/shard_map/ppermute | solution.py:25
  71.9 20.8 %collective-permute-start.15 = (f32[512,256]{1,0:T(8,128)S(1)}, f32[512,256]{1,0:T(8,128)S(1)}, u32[]{:S(2)}, u32[]{:S(2)}) collective-permute-start(f32[512,256]{1,0:T(8,128)S(1)} %get-tuple-element.52), channel_id=1, source_target_pairs={{7,0},{0,1},{1,2},{2,3},{3,4},{4,5},{5,6},{6,7},{15,8},{8,9},{9,10... | collective-permute-start | bytes 1572872 | tf_op jit(solution)/shard_map/ppermute | solution.py:21
  72.0 20.8 %collective-permute-start.16 = (f32[512,256]{1,0:T(8,128)S(1)}, f32[512,256]{1,0:T(8,128)S(1)}, u32[]{:S(2)}, u32[]{:S(2)}) collective-permute-start(f32[512,256]{1,0:T(8,128)S(1)} %get-tuple-element.51.d1), channel_id=1, source_target_pairs={{0,1},{2,3},{4,5},{6,7},{8,9},{10,11},{12,13},{14,15},{16,17},{18,... | collective-permute-start | bytes 1572872 | tf_op jit(solution)/shard_map/ppermute | solution.py:304
  74.5 9.3 %collective-permute-start.22 = (f32[128,256]{1,0:T(8,128)S(1)}, f32[128,256]{1,0:T(8,128)S(1)}, u32[]{:S(2)}, u32[]{:S(2)}) collective-permute-start(f32[128,256]{1,0:T(8,128)S(1)} %add.59.gram_bottom), channel_id=1, source_target_pairs={{7,0},{0,1},{1,2},{2,3},{3,4},{4,5},{5,6},{6,7},{15,8},{8,9},{9,10... | collective-permute-start | bytes 393224 | tf_op jit(solution)/shard_map/ppermute | solution.py:21
  74.6 10.7 %collective-permute-start.21 = (f32[136,256]{1,0:T(8,128)S(1)}, f32[136,256]{1,0:T(8,128)S(1)}, u32[]{:S(2)}, u32[]{:S(2)}) collective-permute-start(f32[136,256]{1,0:T(8,128)S(1)} %add_select_fusion.gram_top), channel_id=1, source_target_pairs={{7,0},{0,1},{1,2},{2,3},{3,4},{4,5},{5,6},{6,7},{15,8},{8,9},{9,10... | collective-permute-start | bytes 417800 | tf_op jit(solution)/shard_map/ppermute | solution.py:21
  89.2 5.7 %collective-permute-start.24 = (f32[8,512]{1,0:T(8,128)S(1)}, f32[8,512]{1,0:T(8,128)S(1)}, u32[]{:S(2)}, u32[]{:S(2)}) collective-permute-start(f32[8,512]{1,0:T(8,128)S(1)} %get-tuple-element.62), channel_id=1, source_target_pairs={{0,8},{8,0},{16,24},{24,16},{1,9},{9,1},{17,25},{25,17},{2,10},{10... | collective-permute-start | bytes 49160 | tf_op jit(solution)/shard_map/ppermute | solution.py:25
  89.8 5.1 %collective-permute-start.25 = (f32[8,512]{1,0:T(8,128)S(1)}, f32[8,512]{1,0:T(8,128)S(1)}, u32[]{:S(2)}, u32[]{:S(2)}) collective-permute-start(f32[8,512]{1,0:T(8,128)S(1)} %get-tuple-element.62), channel_id=1, source_target_pairs={{0,16},{8,24},{16,0},{24,8},{1,17},{9,25},{17,1},{25,9},{2,18},{10... | collective-permute-start | bytes 49160 | tf_op jit(solution)/shard_map/ppermute | solution.py:25
  91.2 4.6 %collective-permute-start.26 = (f32[8,512]{1,0:T(8,128)S(1)}, f32[8,512]{1,0:T(8,128)S(1)}, u32[]{:S(2)}, u32[]{:S(2)}) collective-permute-start(f32[8,512]{1,0:T(8,128)S(1)} %get-tuple-element.62), channel_id=1, source_target_pairs={{0,24},{8,16},{16,8},{24,0},{1,25},{9,17},{17,9},{25,1},{2,26},{10... | collective-permute-start | bytes 49160 | tf_op jit(solution)/shard_map/ppermute | solution.py:25

commit v5 on v4

--- a/solution.py
+++ b/solution.py
@@ -48,10 +48,12 @@
     return one(left[0], right[0]) + (one(left[0], right[1]) + one(left[1], right[0]))
 
 
-def exact_dot(left, right, dims=(((1,), (0,)), ((), ()))):
-    return lax.dot_general(
-        left, right, dims, precision=lax.Precision.HIGHEST, preferred_element_type=jnp.float32
-    )
+def fine_dot(left, right):
+    one = lambda x, y: jnp.dot(x, y, preferred_element_type=jnp.float32)
+    high, low = cut(left)
+    first, second = cut(right)
+    third = (right - first.astype(jnp.float32) - second.astype(jnp.float32)).astype(jnp.bfloat16)
+    return one(high, first) + (one(high, second) + one(low, first) + one(high, third))
 
 
 def polar_series():
@@ -84,7 +86,8 @@
     x4 = cut(dot(x2, x2))
     x8 = cut(dot(x4, x4))
     group = lambda k: sum(c[4 * k + j] * powers[j] for j in range(4))
-    high = group(2) + c[12] * dot(x4, b)
+    last = jnp.dot(x4[0], b[0], preferred_element_type=jnp.float32)
+    high = group(2) + c[12] * last
     series = group(0) + dot(x4, cut(group(1))) + dot(x8, cut(high))
     over = (coupling + dot(x, cut(series))) * factor
     under = -over.T
@@ -106,8 +109,8 @@
 def times(parts, matrix_refs):
     if len(matrix_refs) == 1:
         whole = jnp.concatenate(parts, axis=0)
-        return exact_dot(matrix_refs[0][...], whole)
-    return exact_dot(matrix_refs[0][...], parts[0]) + exact_dot(matrix_refs[1][...], parts[1])
+        return fine_dot(matrix_refs[0][...], whole)
+    return fine_dot(matrix_refs[0][...], parts[0]) + fine_dot(matrix_refs[1][...], parts[1])
 
 
 def store_gram(left, right, top_ref, bottom_ref):

time: 96.6 us -> 95.4 us (0.988)
  Pallas kernels: 30.8 us -> 27.4 us
  waiting for transfers between devices: 33.9 us -> 36.3 us
    pallas_call x10, Pallas kernels: 28.6 us -> 25.3 us  [call(): pl.pallas_call(kernel, out_shape=outs, in_specs=specs, out_specs=[VMEM] *...]
    ppermute x11, waiting for transfers between devices: 18.1 us -> 20.4 us  [from_behind(): lax.ppermute(block, axis, [((i - distance) % count, i) for i in range(cou...]
  transfers between devices with their start and end apart: 27 -> 27, of which waited for: 13 -> 14; matrix products, arithmetic and copies ran while one was open for 2% -> 2% of each run, Pallas kernels for 27% -> 24%
where the time goes in v5:
time: 95.4 us; the launch traced here: 95.2 us
  waiting for transfers between devices  36.3 us (38%)
  Pallas kernels  27.4 us (29%)
  starting transfers between devices  25 us (26%)
  between operations  2.82 us (3%)
  local copies, waits for them, and re-layouts  2.58 us (3%)
  other arithmetic  1.04 us (1%)
    pallas_call x10, Pallas kernels, call(): pl.pallas_call(kernel, out_shape=outs, in_specs=specs, out_specs=[VMEM] *...  25.3 us
    ppermute x11, waiting for transfers between devices, from_behind(): lax.ppermute(block, axis, [((i - distance) % count, i) for i in range(cou...  20.4 us
    ppermute x15, starting transfers between devices, exchange(): lax.ppermute(block, axis, [(i, i ^ mask) for i in range(lax.axis_size(axi...  19.8 us
    ppermute x15, waiting for transfers between devices, exchange(): lax.ppermute(block, axis, [(i, i ^ mask) for i in range(lax.axis_size(axi...  15.9 us
    ppermute x11, starting transfers between devices, from_behind(): lax.ppermute(block, axis, [((i - distance) % count, i) for i in range(cou...  3.89 us
    pallas_call x1, Pallas kernels, per_device(): pl.pallas_call(functools.partial(finish_kernel, rows_each), name='finish'...  2.13 us
  transfers between devices with their start and end apart: 27, of which 14 were waited for; matrix products, arithmetic and copies ran while one was open for 2% of the time, Pallas kernels for 24%

profile of v5, /device:TPU:0, one launch (start us, length us, event | category | flops | bytes accessed | tf_op | source)
XLA Modules:
  0.0 95.2 jit_solution(10057763518668654840)
XLA Ops:
  0.6 0.5 collective-permute-start.6
  1.2 1.2 %copy-done = f32[512,512]{1,0:T(8,128)S(1)} copy-done((f32[512,512]{1,0:T(8,128)S(1)}, f32[512,512]{1,0:T(8,128)}, u32[]{:S(2)}) %copy-start) | copy-done | bytes 1048600
  2.4 0.5 shard_map.49
  2.9 2.5 %collective-permute-start = (f32[136,256]{1,0:T(8,128)S(1)}, f32[136,256]{1,0:T(8,128)S(1)}, u32[]{:S(2)}, u32[]{:S(2)}) collective-permute-start(f32[136,256]{1,0:T(8,128)S(1)} %get-tuple-element.33), channel_id=1, source_target_pairs={{0,8},{8,0},{16,24},{24,16},{1,9},{9,1},{17,25},{25,17},{2,10},{10... | collective-permute-start | bytes 417800 | tf_op jit(solution)/shard_map/ppermute | solution.py:25
  5.4 1.5 %collective-permute-start.2 = (f32[128,256]{1,0:T(8,128)S(1)}, f32[128,256]{1,0:T(8,128)S(1)}, u32[]{:S(2)}, u32[]{:S(2)}) collective-permute-start(f32[128,256]{1,0:T(8,128)S(1)} %get-tuple-element.34), channel_id=1, source_target_pairs={{0,16},{8,24},{16,0},{24,8},{1,17},{9,25},{17,1},{25,9},{2,18},{10... | collective-permute-start | bytes 393224 | tf_op jit(solution)/shard_map/ppermute | solution.py:25
  6.9 4.4 %collective-permute-done.2 = f32[128,256]{1,0:T(8,128)S(1)} collective-permute-done((f32[128,256]{1,0:T(8,128)S(1)}, f32[128,256]{1,0:T(8,128)S(1)}, u32[]{:S(2)}, u32[]{:S(2)}) %collective-permute-start.2) | collective-permute-done | bytes 131104 | tf_op jit(solution)/shard_map/ppermute | solution.py:25
  11.4 0.1 collective-permute-start.3
  11.4 0.0 collective-permute-done
  11.5 2.1 %collective-permute-start.1 = (f32[136,256]{1,0:T(8,128)S(1)}, f32[136,256]{1,0:T(8,128)S(1)}, u32[]{:S(2)}, u32[]{:S(2)}) collective-permute-start(f32[136,256]{1,0:T(8,128)S(1)} %add.48), channel_id=1, source_target_pairs={{0,16},{8,24},{16,0},{24,8},{1,17},{9,25},{17,1},{25,9},{2,18},{10... | collective-permute-start | bytes 417800 | tf_op jit(solution)/shard_map/ppermute | solution.py:25
  13.6 1.4 %fusion.2 = (s32[1,1]{0,1:T(1,128)}, s32[1,1]{0,1:T(1,128)}, s32[1,1]{0,1:T(1,128)}) fusion(s32[3,1]{0,1:T(1,128)} %param.3), kind=kLoop, calls=%fused_computation.9 | loop fusion | bytes 24 | tf_op jit(solution)/shard_map/slice | solution.py:269
  15.6 1.8 %collective-permute-done.3 = f32[128,256]{1,0:T(8,128)S(1)} collective-permute-done((f32[128,256]{1,0:T(8,128)S(1)}, f32[128,256]{1,0:T(8,128)S(1)}, u32[]{:S(2)}, u32[]{:S(2)}) %collective-permute-start.3) | collective-permute-done | bytes 131104 | tf_op jit(solution)/shard_map/ppermute | solution.py:25
  17.4 0.1 collective-permute-start.5
  17.5 0.2 collective-permute-done.1
  17.7 0.1 add_select_fusion.2.gram_top
  17.8 1.5 %collective-permute-start.4 = (f32[136,256]{1,0:T(8,128)S(1)}, f32[136,256]{1,0:T(8,128)S(1)}, u32[]{:S(2)}, u32[]{:S(2)}) collective-permute-start(f32[136,256]{1,0:T(8,128)S(1)} %add_select_fusion.2.gram_top), channel_id=1, source_target_pairs={{7,0},{0,1},{1,2},{2,3},{3,4},{4,5},{5,6},{6,7},{15,8},{8,9},{9,10... | collective-permute-start | bytes 417800 | tf_op jit(solution)/shard_map/ppermute | solution.py:21
  19.3 3.4 %shard_map.50 = (f32[512,256]{1,0:T(8,128)S(1)}, f32[512,256]{1,0:T(8,128)S(1)}) custom-call(f32[136,256]{1,0:T(8,128)S(1)} %add_select_fusion.2.gram_top, f32[128,256]{1,0:T(8,128)S(1)} %add.51.gram_bottom, f32[512,512]{1,0:T(8,128)S(1)} %copy-done), custom_call_target="tpu_custom_call" | custom-call | flops 1912602624 | bytes 1048576 | tf_op jit(solution)/shard_map/pallas_call | solution.py:139
  22.8 0.9 collective-permute-done.5.gram_bottom
  23.7 1.5 %collective-permute-done.4.gram_top = f32[136,256]{1,0:T(8,128)S(1)} collective-permute-done((f32[136,256]{1,0:T(8,128)S(1)}, f32[136,256]{1,0:T(8,128)S(1)}, u32[]{:S(2)}, u32[]{:S(2)}) %collective-permute-start.4) | collective-permute-done | bytes 139296 | tf_op jit(solution)/shard_map/ppermute | solution.py:21
  25.2 0.0 collective-permute-done.6.refs_0_
  25.2 4.1 %shard_map.51 = (f32[512,256]{1,0:T(8,128)S(1)}, f32[512,256]{1,0:T(8,128)S(1)}, f32[512,256]{1,0:T(8,128)S(1)}, f32[136,256]{1,0:T(8,128)S(1)}, f32[128,256]{1,0:T(8,128)S(1)}) custom-call(f32[136,256]{1,0:T(8,128)S(1)} %collective-permute-done.4.gram_top, f32[128,256]{1,0:T(8,128)S(1)} %collective-permute-done.5.gram_bottom, ...), custom_call_target="tpu_custom_call" | custom-call | flops 1912602624 | bytes 1048576 | tf_op jit(solution)/shard_map/pallas_call | solution.py:139
  29.2 0.8 collective-permute-start.8
  30.0 1.5 %collective-permute-start.10 = (f32[128,256]{1,0:T(8,128)S(1)}, f32[128,256]{1,0:T(8,128)S(1)}, u32[]{:S(2)}, u32[]{:S(2)}) collective-permute-start(f32[128,256]{1,0:T(8,128)S(1)} %get-tuple-element.40), channel_id=1, source_target_pairs={{0,16},{8,24},{16,0},{24,8},{1,17},{9,25},{17,1},{25,9},{2,18},{10... | collective-permute-start | bytes 393224 | tf_op jit(solution)/shard_map/ppermute | solution.py:25
  31.5 2.8 %collective-permute-done.8 = f32[136,256]{1,0:T(8,128)S(1)} collective-permute-done((f32[136,256]{1,0:T(8,128)S(1)}, f32[136,256]{1,0:T(8,128)S(1)}, u32[]{:S(2)}, u32[]{:S(2)}) %collective-permute-start.8) | collective-permute-done | bytes 139296 | tf_op jit(solution)/shard_map/ppermute | solution.py:25
  34.4 1.6 %collective-permute-start.9 = (f32[136,256]{1,0:T(8,128)S(1)}, f32[136,256]{1,0:T(8,128)S(1)}, u32[]{:S(2)}, u32[]{:S(2)}) collective-permute-start(f32[136,256]{1,0:T(8,128)S(1)} %add.52), channel_id=1, source_target_pairs={{0,16},{8,24},{16,0},{24,8},{1,17},{9,25},{17,1},{25,9},{2,18},{10... | collective-permute-start | bytes 417800 | tf_op jit(solution)/shard_map/ppermute | solution.py:25
  36.0 1.2 %collective-permute-start.11 = (f32[128,256]{1,0:T(8,128)S(1)}, f32[128,256]{1,0:T(8,128)S(1)}, u32[]{:S(2)}, u32[]{:S(2)}) collective-permute-start(f32[128,256]{1,0:T(8,128)S(1)} %add.54), channel_id=1, source_target_pairs={{0,8},{8,0},{16,24},{24,16},{1,9},{9,1},{17,25},{25,17},{2,10},{10... | collective-permute-start | bytes 393224 | tf_op jit(solution)/shard_map/ppermute | solution.py:25
  37.8 0.7 collective-permute-start.7
  38.6 0.7 shard_map.53.refs_0_
  39.3 1.7 %collective-permute-done.11 = f32[128,256]{1,0:T(8,128)S(1)} collective-permute-done((f32[128,256]{1,0:T(8,128)S(1)}, f32[128,256]{1,0:T(8,128)S(1)}, u32[]{:S(2)}, u32[]{:S(2)}) %collective-permute-start.11) | collective-permute-done | bytes 131104 | tf_op jit(solution)/shard_map/ppermute | solution.py:25
  41.0 0.1 collective-permute-start.13
  41.1 0.0 collective-permute-done.9
  41.1 0.1 add_select_fusion.1.gram_top
  41.2 0.5 collective-permute-start.12
  41.7 3.4 %shard_map.52 = (f32[512,256]{1,0:T(8,128)S(1)}, f32[512,256]{1,0:T(8,128)S(1)}) custom-call(f32[136,256]{1,0:T(8,128)S(1)} %add_select_fusion.1.gram_top, f32[128,256]{1,0:T(8,128)S(1)} %add.55.gram_bottom, f32[512,256]{1,0:T(8,128)S(1)} %get-tuple-element.36.panel_ref.refs_0_, f32[512,256]{1,0:T(8,128)S(1)} %get-tuple-element.41.refs_1_), custom_call_target="tpu_custom_call" | custom-call | flops 1912602624 | bytes 1048576 | tf_op jit(solution)/shard_map/pallas_call | solution.py:139
  45.2 9.4 %collective-permute-done.13.gram_bottom = f32[128,256]{1,0:T(8,128)S(1)} collective-permute-done((f32[128,256]{1,0:T(8,128)S(1)}, f32[128,256]{1,0:T(8,128)S(1)}, u32[]{:S(2)}, u32[]{:S(2)}) %collective-permute-start.13) | collective-permute-done | bytes 131104 | tf_op jit(solution)/shard_map/ppermute | solution.py:21
  54.6 1.5 %collective-permute-done.12.gram_top = f32[136,256]{1,0:T(8,128)S(1)} collective-permute-done((f32[136,256]{1,0:T(8,128)S(1)}, f32[136,256]{1,0:T(8,128)S(1)}, u32[]{:S(2)}, u32[]{:S(2)}) %collective-permute-start.12) | collective-permute-done | bytes 139296 | tf_op jit(solution)/shard_map/ppermute | solution.py:21
  56.1 0.0 collective-permute-done.14.refs_1_
  56.1 4.1 %shard_map.54 = (f32[512,256]{1,0:T(8,128)S(1)}, f32[512,256]{1,0:T(8,128)S(1)}, f32[512,256]{1,0:T(8,128)S(1)}, f32[136,256]{1,0:T(8,128)S(1)}, f32[128,256]{1,0:T(8,128)S(1)}) custom-call(f32[136,256]{1,0:T(8,128)S(1)} %collective-permute-done.12.gram_top, f32[128,256]{1,0:T(8,128)S(1)} %collective-permute-done.13.gram_bottom, ...), custom_call_target="tpu_custom_call" | custom-call | flops 1912602624 | bytes 1048576 | tf_op jit(solution)/shard_map/pallas_call | solution.py:139
  60.2 1.0 %collective-permute-start.17 = (f32[136,256]{1,0:T(8,128)S(1)}, f32[136,256]{1,0:T(8,128)S(1)}, u32[]{:S(2)}, u32[]{:S(2)}) collective-permute-start(f32[136,256]{1,0:T(8,128)S(1)} %get-tuple-element.53), channel_id=1, source_target_pairs={{0,8},{8,0},{16,24},{24,16},{1,9},{9,1},{17,25},{25,17},{2,10},{10... | collective-permute-start | bytes 417800 | tf_op jit(solution)/shard_map/ppermute | solution.py:25
  61.1 1.5 %collective-permute-start.19 = (f32[128,256]{1,0:T(8,128)S(1)}, f32[128,256]{1,0:T(8,128)S(1)}, u32[]{:S(2)}, u32[]{:S(2)}) collective-permute-start(f32[128,256]{1,0:T(8,128)S(1)} %get-tuple-element.54), channel_id=1, source_target_pairs={{0,16},{8,24},{16,0},{24,8},{1,17},{9,25},{17,1},{25,9},{2,18},{10... | collective-permute-start | bytes 393224 | tf_op jit(solution)/shard_map/ppermute | solution.py:25
  63.3 0.1 collective-permute-start.23
  63.3 4.0 %collective-permute-done.19 = f32[128,256]{1,0:T(8,128)S(1)} collective-permute-done((f32[128,256]{1,0:T(8,128)S(1)}, f32[128,256]{1,0:T(8,128)S(1)}, u32[]{:S(2)}, u32[]{:S(2)}) %collective-permute-start.19) | collective-permute-done | bytes 131104 | tf_op jit(solution)/shard_map/ppermute | solution.py:25
  67.4 1.3 %collective-permute-start.20 = (f32[128,256]{1,0:T(8,128)S(1)}, f32[128,256]{1,0:T(8,128)S(1)}, u32[]{:S(2)}, u32[]{:S(2)}) collective-permute-start(f32[128,256]{1,0:T(8,128)S(1)} %add.58), channel_id=1, source_target_pairs={{0,8},{8,0},{16,24},{24,16},{1,9},{9,1},{17,25},{25,17},{2,10},{10... | collective-permute-start | bytes 393224 | tf_op jit(solution)/shard_map/ppermute | solution.py:25
  68.7 0.0 collective-permute-done.17
  68.8 1.2 %collective-permute-start.18 = (f32[136,256]{1,0:T(8,128)S(1)}, f32[136,256]{1,0:T(8,128)S(1)}, u32[]{:S(2)}, u32[]{:S(2)}) collective-permute-start(f32[136,256]{1,0:T(8,128)S(1)} %add.56), channel_id=1, source_target_pairs={{0,16},{8,24},{16,0},{24,8},{1,17},{9,25},{17,1},{25,9},{2,18},{10... | collective-permute-start | bytes 417800 | tf_op jit(solution)/shard_map/ppermute | solution.py:25
  70.0 1.4 %shard_map.55 = (f32[512,256]{1,0:T(8,128)S(1)}, f32[512,256]{1,0:T(8,128)S(1)}, f32[512,256]{1,0:T(8,128)S(1)}, f32[512,256]{1,0:T(8,128)S(1)}, f32[512,256]{1,...) custom-call(f32[512,256]{1,0:T(8,128)S(1)} %get-tuple-element.35.s10, ...), custom_call_target="tpu_custom_call" | custom-call | flops 1207959552 | bytes 1048576 | tf_op jit(solution)/shard_map/pallas_call | solution.py:139
  71.4 0.1 collective-permute-start.15
  71.5 1.3 %collective-permute-start.16 = (f32[512,256]{1,0:T(8,128)S(1)}, f32[512,256]{1,0:T(8,128)S(1)}, u32[]{:S(2)}, u32[]{:S(2)}) collective-permute-start(f32[512,256]{1,0:T(8,128)S(1)} %get-tuple-element.51.d1), channel_id=1, source_target_pairs={{0,1},{2,3},{4,5},{6,7},{8,9},{10,11},{12,13},{14,15},{16,17},{18,... | collective-permute-start | bytes 1572872 | tf_op jit(solution)/shard_map/ppermute | solution.py:307
  72.8 0.7 shard_map.57.refs_0_
  73.5 0.0 collective-permute-done.20
  73.6 0.1 collective-permute-start.22
  73.6 0.2 collective-permute-done.18
  73.9 0.1 add_select_fusion.gram_top
  74.0 0.3 collective-permute-start.21
  74.3 3.4 %shard_map.56 = (f32[512,256]{1,0:T(8,128)S(1)}, f32[512,256]{1,0:T(8,128)S(1)}) custom-call(f32[136,256]{1,0:T(8,128)S(1)} %add_select_fusion.gram_top, f32[128,256]{1,0:T(8,128)S(1)} %add.59.gram_bottom, f32[512,256]{1,0:T(8,128)S(1)} %get-tuple-element.43.panel_ref.refs_0_, f32[512,256]{1,0:T(8,128)S(1)} %get-tuple-element.55.refs_1_), custom_call_target="tpu_custom_call" | custom-call | flops 1912602624 | bytes 1048576 | tf_op jit(solution)/shard_map/pallas_call | solution.py:139
  77.7 5.6 %collective-permute-done.22.gram_bottom = f32[128,256]{1,0:T(8,128)S(1)} collective-permute-done((f32[128,256]{1,0:T(8,128)S(1)}, f32[128,256]{1,0:T(8,128)S(1)}, u32[]{:S(2)}, u32[]{:S(2)}) %collective-permute-start.22) | collective-permute-done | bytes 131104 | tf_op jit(solution)/shard_map/ppermute | solution.py:21
  83.3 1.5 %collective-permute-done.21.gram_top = f32[136,256]{1,0:T(8,128)S(1)} collective-permute-done((f32[136,256]{1,0:T(8,128)S(1)}, f32[136,256]{1,0:T(8,128)S(1)}, u32[]{:S(2)}, u32[]{:S(2)}) %collective-permute-start.21) | collective-permute-done | bytes 139296 | tf_op jit(solution)/shard_map/ppermute | solution.py:21
  84.8 0.0 collective-permute-done.23.refs_1_
  84.8 3.5 %shard_map.58 = (f32[512,256]{1,0:T(8,128)S(1)}, f32[512,256]{1,0:T(8,128)S(1)}, f32[8,512]{1,0:T(8,128)S(1)}) custom-call(f32[136,256]{1,0:T(8,128)S(1)} %collective-permute-done.21.gram_top, f32[128,256]{1,0:T(8,128)S(1)} %collective-permute-done.22.gram_bottom, f32[512,256]{1,0:T(8,128)S(1)} %get-tuple-element.57.panel_ref.still, ...), custom_call_target="tpu_custom_call" | custom-call | flops 1912602624 | bytes 1048576 | tf_op jit(solution)/shard_map/pallas_call | solution.py:139
  88.3 1.0 %collective-permute-start.24 = (f32[8,512]{1,0:T(8,128)S(1)}, f32[8,512]{1,0:T(8,128)S(1)}, u32[]{:S(2)}, u32[]{:S(2)}) collective-permute-start(f32[8,512]{1,0:T(8,128)S(1)} %get-tuple-element.62), channel_id=1, source_target_pairs={{0,8},{8,0},{16,24},{24,16},{1,9},{9,1},{17,25},{25,17},{2,10},{10... | collective-permute-start | bytes 49160 | tf_op jit(solution)/shard_map/ppermute | solution.py:25
  89.3 0.6 collective-permute-start.25
  89.9 1.9 %collective-permute-start.26 = (f32[8,512]{1,0:T(8,128)S(1)}, f32[8,512]{1,0:T(8,128)S(1)}, u32[]{:S(2)}, u32[]{:S(2)}) collective-permute-start(f32[8,512]{1,0:T(8,128)S(1)} %get-tuple-element.62), channel_id=1, source_target_pairs={{0,24},{8,16},{16,8},{24,0},{1,25},{9,17},{17,9},{25,1},{2,26},{10... | collective-permute-start | bytes 49160 | tf_op jit(solution)/shard_map/ppermute | solution.py:25
  91.8 2.1 %finish.1 = (f32[512,512]{1,0:T(8,128)}, f32[1024,512]{1,0:T(8,128)}) custom-call(f32[512,256]{1,0:T(8,128)S(1)} %get-tuple-element.46.a0, f32[512,256]{1,0:T(8,128)S(1)} %get-tuple-element.47.b0, f32[512,256]{1,0:T(8,128)S(1)} %get-tuple-element.48.a1, f32[512,256]{1,0:T(8,128)S(1)} %get-tuple-element.49.b1, f32[512,256]{1,0:T(8,128)S(1)} %get-tuple-element.50.c1, ...), custom_call_target="tpu_custom_call" | custom-call | flops 805306368 | bytes 1048576 | tf_op jit(solution)/shard_map/finish/pallas_call | solution.py:327
  94.0 0.6 collective-permute-done.26
  94.6 0.6 fusion.1
  (18 shorter events, 0.2 us)
Async XLA Ops:
  0.6 24.5 %collective-permute-start.6 = (f32[512,512]{1,0:T(8,128)}, f32[512,512]{1,0:T(8,128)S(1)}, u32[]{:S(2)}, u32[]{:S(2)}) collective-permute-start(f32[512,512]{1,0:T(8,128)} %refs_0_.1), channel_id=1, source_target_pairs={{7,0},{0,1},{1,2},{2,3},{3,4},{4,5},{5,6},{6,7},{15,8},{8,9},{9,10... | collective-permute-start | bytes 3145736 | tf_op jit(solution)/shard_map/ppermute | solution.py:21
  1.2 1.2 %copy-start = (f32[512,512]{1,0:T(8,128)S(1)}, f32[512,512]{1,0:T(8,128)}, u32[]{:S(2)}) copy-start(f32[512,512]{1,0:T(8,128)} %refs_0_.1) | copy-start | bytes 3145732
  2.9 8.6 %collective-permute-start = (f32[136,256]{1,0:T(8,128)S(1)}, f32[136,256]{1,0:T(8,128)S(1)}, u32[]{:S(2)}, u32[]{:S(2)}) collective-permute-start(f32[136,256]{1,0:T(8,128)S(1)} %get-tuple-element.33), channel_id=1, source_target_pairs={{0,8},{8,0},{16,24},{24,16},{1,9},{9,1},{17,25},{25,17},{2,10},{10... | collective-permute-start | bytes 417800 | tf_op jit(solution)/shard_map/ppermute | solution.py:25
  5.4 5.9 %collective-permute-start.2 = (f32[128,256]{1,0:T(8,128)S(1)}, f32[128,256]{1,0:T(8,128)S(1)}, u32[]{:S(2)}, u32[]{:S(2)}) collective-permute-start(f32[128,256]{1,0:T(8,128)S(1)} %get-tuple-element.34), channel_id=1, source_target_pairs={{0,16},{8,24},{16,0},{24,8},{1,17},{9,25},{17,1},{25,9},{2,18},{10... | collective-permute-start | bytes 393224 | tf_op jit(solution)/shard_map/ppermute | solution.py:25
  11.4 6.0 %collective-permute-start.3 = (f32[128,256]{1,0:T(8,128)S(1)}, f32[128,256]{1,0:T(8,128)S(1)}, u32[]{:S(2)}, u32[]{:S(2)}) collective-permute-start(f32[128,256]{1,0:T(8,128)S(1)} %add.50), channel_id=1, source_target_pairs={{0,8},{8,0},{16,24},{24,16},{1,9},{9,1},{17,25},{25,17},{2,10},{10... | collective-permute-start | bytes 393224 | tf_op jit(solution)/shard_map/ppermute | solution.py:25
  11.5 6.2 %collective-permute-start.1 = (f32[136,256]{1,0:T(8,128)S(1)}, f32[136,256]{1,0:T(8,128)S(1)}, u32[]{:S(2)}, u32[]{:S(2)}) collective-permute-start(f32[136,256]{1,0:T(8,128)S(1)} %add.48), channel_id=1, source_target_pairs={{0,16},{8,24},{16,0},{24,8},{1,17},{9,25},{17,1},{25,9},{2,18},{10... | collective-permute-start | bytes 417800 | tf_op jit(solution)/shard_map/ppermute | solution.py:25
  17.4 6.2 %collective-permute-start.5 = (f32[128,256]{1,0:T(8,128)S(1)}, f32[128,256]{1,0:T(8,128)S(1)}, u32[]{:S(2)}, u32[]{:S(2)}) collective-permute-start(f32[128,256]{1,0:T(8,128)S(1)} %add.51.gram_bottom), channel_id=1, source_target_pairs={{7,0},{0,1},{1,2},{2,3},{3,4},{4,5},{5,6},{6,7},{15,8},{8,9},{9,10... | collective-permute-start | bytes 393224 | tf_op jit(solution)/shard_map/ppermute | solution.py:21
  17.8 7.4 %collective-permute-start.4 = (f32[136,256]{1,0:T(8,128)S(1)}, f32[136,256]{1,0:T(8,128)S(1)}, u32[]{:S(2)}, u32[]{:S(2)}) collective-permute-start(f32[136,256]{1,0:T(8,128)S(1)} %add_select_fusion.2.gram_top), channel_id=1, source_target_pairs={{7,0},{0,1},{1,2},{2,3},{3,4},{4,5},{5,6},{6,7},{15,8},{8,9},{9,10... | collective-permute-start | bytes 417800 | tf_op jit(solution)/shard_map/ppermute | solution.py:21
  29.2 5.1 %collective-permute-start.8 = (f32[136,256]{1,0:T(8,128)S(1)}, f32[136,256]{1,0:T(8,128)S(1)}, u32[]{:S(2)}, u32[]{:S(2)}) collective-permute-start(f32[136,256]{1,0:T(8,128)S(1)} %get-tuple-element.39), channel_id=1, source_target_pairs={{0,8},{8,0},{16,24},{24,16},{1,9},{9,1},{17,25},{25,17},{2,10},{10... | collective-permute-start | bytes 417800 | tf_op jit(solution)/shard_map/ppermute | solution.py:25
  30.0 6.0 %collective-permute-start.10 = (f32[128,256]{1,0:T(8,128)S(1)}, f32[128,256]{1,0:T(8,128)S(1)}, u32[]{:S(2)}, u32[]{:S(2)}) collective-permute-start(f32[128,256]{1,0:T(8,128)S(1)} %get-tuple-element.40), channel_id=1, source_target_pairs={{0,16},{8,24},{16,0},{24,8},{1,17},{9,25},{17,1},{25,9},{2,18},{10... | collective-permute-start | bytes 393224 | tf_op jit(solution)/shard_map/ppermute | solution.py:25
  34.4 6.7 %collective-permute-start.9 = (f32[136,256]{1,0:T(8,128)S(1)}, f32[136,256]{1,0:T(8,128)S(1)}, u32[]{:S(2)}, u32[]{:S(2)}) collective-permute-start(f32[136,256]{1,0:T(8,128)S(1)} %add.52), channel_id=1, source_target_pairs={{0,16},{8,24},{16,0},{24,8},{1,17},{9,25},{17,1},{25,9},{2,18},{10... | collective-permute-start | bytes 417800 | tf_op jit(solution)/shard_map/ppermute | solution.py:25
  36.0 5.0 %collective-permute-start.11 = (f32[128,256]{1,0:T(8,128)S(1)}, f32[128,256]{1,0:T(8,128)S(1)}, u32[]{:S(2)}, u32[]{:S(2)}) collective-permute-start(f32[128,256]{1,0:T(8,128)S(1)} %add.54), channel_id=1, source_target_pairs={{0,8},{8,0},{16,24},{24,16},{1,9},{9,1},{17,25},{25,17},{2,10},{10... | collective-permute-start | bytes 393224 | tf_op jit(solution)/shard_map/ppermute | solution.py:25
  37.2 18.9 %collective-permute-start.14 = (f32[512,256]{1,0:T(8,128)S(1)}, f32[512,256]{1,0:T(8,128)S(1)}, u32[]{:S(2)}, u32[]{:S(2)}) collective-permute-start(f32[512,256]{1,0:T(8,128)S(1)} %get-tuple-element.41.refs_1_), channel_id=1, source_target_pairs={{7,0},{0,1},{1,2},{2,3},{3,4},{4,5},{5,6},{6,7},{15,8},{8,9},{9,10... | collective-permute-start | bytes 1572872 | tf_op jit(solution)/shard_map/ppermute | solution.py:21
  37.8 32.1 %collective-permute-start.7 = (f32[512,256]{1,0:T(8,128)S(1)}, f32[512,256]{1,0:T(8,128)S(1)}, u32[]{:S(2)}, u32[]{:S(2)}) collective-permute-start(f32[512,256]{1,0:T(8,128)S(1)} %get-tuple-element.37.m11), channel_id=1, source_target_pairs={{7,0},{0,1},{1,2},{2,3},{3,4},{4,5},{5,6},{6,7},{15,8},{8,9},{9,10... | collective-permute-start | bytes 1572872 | tf_op jit(solution)/shard_map/ppermute | solution.py:21
  41.0 13.6 %collective-permute-start.13 = (f32[128,256]{1,0:T(8,128)S(1)}, f32[128,256]{1,0:T(8,128)S(1)}, u32[]{:S(2)}, u32[]{:S(2)}) collective-permute-start(f32[128,256]{1,0:T(8,128)S(1)} %add.55.gram_bottom), channel_id=1, source_target_pairs={{7,0},{0,1},{1,2},{2,3},{3,4},{4,5},{5,6},{6,7},{15,8},{8,9},{9,10... | collective-permute-start | bytes 393224 | tf_op jit(solution)/shard_map/ppermute | solution.py:21
  41.2 14.9 %collective-permute-start.12 = (f32[136,256]{1,0:T(8,128)S(1)}, f32[136,256]{1,0:T(8,128)S(1)}, u32[]{:S(2)}, u32[]{:S(2)}) collective-permute-start(f32[136,256]{1,0:T(8,128)S(1)} %add_select_fusion.1.gram_top), channel_id=1, source_target_pairs={{7,0},{0,1},{1,2},{2,3},{3,4},{4,5},{5,6},{6,7},{15,8},{8,9},{9,10... | collective-permute-start | bytes 417800 | tf_op jit(solution)/shard_map/ppermute | solution.py:21
  60.2 8.6 %collective-permute-start.17 = (f32[136,256]{1,0:T(8,128)S(1)}, f32[136,256]{1,0:T(8,128)S(1)}, u32[]{:S(2)}, u32[]{:S(2)}) collective-permute-start(f32[136,256]{1,0:T(8,128)S(1)} %get-tuple-element.53), channel_id=1, source_target_pairs={{0,8},{8,0},{16,24},{24,16},{1,9},{9,1},{17,25},{25,17},{2,10},{10... | collective-permute-start | bytes 417800 | tf_op jit(solution)/shard_map/ppermute | solution.py:25
  61.1 6.2 %collective-permute-start.19 = (f32[128,256]{1,0:T(8,128)S(1)}, f32[128,256]{1,0:T(8,128)S(1)}, u32[]{:S(2)}, u32[]{:S(2)}) collective-permute-start(f32[128,256]{1,0:T(8,128)S(1)} %get-tuple-element.54), channel_id=1, source_target_pairs={{0,16},{8,24},{16,0},{24,8},{1,17},{9,25},{17,1},{25,9},{2,18},{10... | collective-permute-start | bytes 393224 | tf_op jit(solution)/shard_map/ppermute | solution.py:25
  63.3 21.5 %collective-permute-start.23 = (f32[512,256]{1,0:T(8,128)S(1)}, f32[512,256]{1,0:T(8,128)S(1)}, u32[]{:S(2)}, u32[]{:S(2)}) collective-permute-start(f32[512,256]{1,0:T(8,128)S(1)} %get-tuple-element.55.refs_1_), channel_id=1, source_target_pairs={{7,0},{0,1},{1,2},{2,3},{3,4},{4,5},{5,6},{6,7},{15,8},{8,9},{9,10... | collective-permute-start | bytes 1572872 | tf_op jit(solution)/shard_map/ppermute | solution.py:21
  67.4 6.1 %collective-permute-start.20 = (f32[128,256]{1,0:T(8,128)S(1)}, f32[128,256]{1,0:T(8,128)S(1)}, u32[]{:S(2)}, u32[]{:S(2)}) collective-permute-start(f32[128,256]{1,0:T(8,128)S(1)} %add.58), channel_id=1, source_target_pairs={{0,8},{8,0},{16,24},{24,16},{1,9},{9,1},{17,25},{25,17},{2,10},{10... | collective-permute-start | bytes 393224 | tf_op jit(solution)/shard_map/ppermute | solution.py:25
  68.8 5.1 %collective-permute-start.18 = (f32[136,256]{1,0:T(8,128)S(1)}, f32[136,256]{1,0:T(8,128)S(1)}, u32[]{:S(2)}, u32[]{:S(2)}) collective-permute-start(f32[136,256]{1,0:T(8,128)S(1)} %add.56), channel_id=1, source_target_pairs={{0,16},{8,24},{16,0},{24,8},{1,17},{9,25},{17,1},{25,9},{2,18},{10... | collective-permute-start | bytes 417800 | tf_op jit(solution)/shard_map/ppermute | solution.py:25
  71.4 20.4 %collective-permute-start.15 = (f32[512,256]{1,0:T(8,128)S(1)}, f32[512,256]{1,0:T(8,128)S(1)}, u32[]{:S(2)}, u32[]{:S(2)}) collective-permute-start(f32[512,256]{1,0:T(8,128)S(1)} %get-tuple-element.52), channel_id=1, source_target_pairs={{7,0},{0,1},{1,2},{2,3},{3,4},{4,5},{5,6},{6,7},{15,8},{8,9},{9,10... | collective-permute-start | bytes 1572872 | tf_op jit(solution)/shard_map/ppermute | solution.py:21
  71.5 20.3 %collective-permute-start.16 = (f32[512,256]{1,0:T(8,128)S(1)}, f32[512,256]{1,0:T(8,128)S(1)}, u32[]{:S(2)}, u32[]{:S(2)}) collective-permute-start(f32[512,256]{1,0:T(8,128)S(1)} %get-tuple-element.51.d1), channel_id=1, source_target_pairs={{0,1},{2,3},{4,5},{6,7},{8,9},{10,11},{12,13},{14,15},{16,17},{18,... | collective-permute-start | bytes 1572872 | tf_op jit(solution)/shard_map/ppermute | solution.py:307
  73.6 9.7 %collective-permute-start.22 = (f32[128,256]{1,0:T(8,128)S(1)}, f32[128,256]{1,0:T(8,128)S(1)}, u32[]{:S(2)}, u32[]{:S(2)}) collective-permute-start(f32[128,256]{1,0:T(8,128)S(1)} %add.59.gram_bottom), channel_id=1, source_target_pairs={{7,0},{0,1},{1,2},{2,3},{3,4},{4,5},{5,6},{6,7},{15,8},{8,9},{9,10... | collective-permute-start | bytes 393224 | tf_op jit(solution)/shard_map/ppermute | solution.py:21
  74.0 10.8 %collective-permute-start.21 = (f32[136,256]{1,0:T(8,128)S(1)}, f32[136,256]{1,0:T(8,128)S(1)}, u32[]{:S(2)}, u32[]{:S(2)}) collective-permute-start(f32[136,256]{1,0:T(8,128)S(1)} %add_select_fusion.gram_top), channel_id=1, source_target_pairs={{7,0},{0,1},{1,2},{2,3},{3,4},{4,5},{5,6},{6,7},{15,8},{8,9},{9,10... | collective-permute-start | bytes 417800 | tf_op jit(solution)/shard_map/ppermute | solution.py:21
  88.3 5.7 %collective-permute-start.24 = (f32[8,512]{1,0:T(8,128)S(1)}, f32[8,512]{1,0:T(8,128)S(1)}, u32[]{:S(2)}, u32[]{:S(2)}) collective-permute-start(f32[8,512]{1,0:T(8,128)S(1)} %get-tuple-element.62), channel_id=1, source_target_pairs={{0,8},{8,0},{16,24},{24,16},{1,9},{9,1},{17,25},{25,17},{2,10},{10... | collective-permute-start | bytes 49160 | tf_op jit(solution)/shard_map/ppermute | solution.py:25
  89.3 4.6 %collective-permute-start.25 = (f32[8,512]{1,0:T(8,128)S(1)}, f32[8,512]{1,0:T(8,128)S(1)}, u32[]{:S(2)}, u32[]{:S(2)}) collective-permute-start(f32[8,512]{1,0:T(8,128)S(1)} %get-tuple-element.62), channel_id=1, source_target_pairs={{0,16},{8,24},{16,0},{24,8},{1,17},{9,25},{17,1},{25,9},{2,18},{10... | collective-permute-start | bytes 49160 | tf_op jit(solution)/shard_map/ppermute | solution.py:25
  89.9 4.6 %collective-permute-start.26 = (f32[8,512]{1,0:T(8,128)S(1)}, f32[8,512]{1,0:T(8,128)S(1)}, u32[]{:S(2)}, u32[]{:S(2)}) collective-permute-start(f32[8,512]{1,0:T(8,128)S(1)} %get-tuple-element.62), channel_id=1, source_target_pairs={{0,24},{8,16},{16,8},{24,0},{1,25},{9,17},{17,9},{25,1},{2,26},{10... | collective-permute-start | bytes 49160 | tf_op jit(solution)/shard_map/ppermute | solution.py:25
